TPU v7x, 8 devices: a whole 2x2x1 slice. The times are simulated.
8 devices in a mesh: dp: 1 (over z), tp: 8 (over y, x, core).
Axes of the slice: x: 2, y: 2, z: 1, core: 2. Of those that a mesh axis runs over, the one named last changes fastest.
Arguments:
- x_in: bfloat16 [1536, 3072], P(('dp', 'tp'))
- grad_y: bfloat16 [1536, 3072], P(('dp', 'tp'))
- norm_gain: float32 [3, 3072], replicated
- w_qkv: bfloat16 [3, 3072, 5120], P(None, None, 'tp')
- w_out: bfloat16 [3, 3072, 3072], P(None, 'tp')
- w_gate: bfloat16 [3, 3072, 8192], P(None, None, 'tp')
- w_up: bfloat16 [3, 3072, 8192], P(None, None, 'tp')
- w_down: bfloat16 [3, 8192, 3072], P(None, 'tp')
Outputs:
- output 1: bfloat16 [1536, 3072], P(('dp', 'tp'))
- output 2: float32 [3, 3072], P('dp')
- output 3: bfloat16 [3, 3072, 5120], P('dp', None, 'tp')
- output 4: bfloat16 [3, 3072, 3072], P('dp', 'tp')
- output 5: bfloat16 [3, 3072, 8192], P('dp', None, 'tp')
- output 6: bfloat16 [3, 3072, 8192], P('dp', None, 'tp')
- output 7: bfloat16 [3, 8192, 3072], P('dp', 'tp')
All inputs are finite; a program needn't handle non-finite values.
Results may differ from a plain program's by a relative error of at most 0.02.
Values are sent between devices in bfloat16 or wider.
A program may use at most 1 GiB of HBM per device.

v0:
```python
import jax
import jax.numpy as jnp
from jax import lax
from jax.sharding import PartitionSpec as P

HEAD_DIM = 128
NORM_EPS = 1e-5
ROPE_BASE = 10000.0


def rope_tables(seq_len):
    half_dim = HEAD_DIM // 2
    freqs = ROPE_BASE ** (-2.0 * jnp.arange(half_dim, dtype=jnp.float32) / HEAD_DIM)
    angles = jnp.arange(seq_len, dtype=jnp.float32)[:, None] * freqs[None, :]
    return jnp.cos(angles)[:, None, None, :], jnp.sin(angles)[:, None, None, :]


def rotate(values, cos_tab, sin_tab):
    half_dim = values.shape[-1] // 2
    lower_half = values[..., :half_dim]
    upper_half = values[..., half_dim:]
    return jnp.concatenate([lower_half * cos_tab - upper_half * sin_tab, upper_half * cos_tab + lower_half * sin_tab], axis=-1)


def rms_scale(x_f32, gain_row):
    inv_rms = lax.rsqrt(jnp.mean(x_f32 * x_f32, axis=-1, keepdims=True) + NORM_EPS)
    return x_f32 * inv_rms * gain_row


def gated(gate_f32, up_f32):
    return jax.nn.silu(gate_f32) * up_f32


def causal_scores(query, keys_rot):
    seq_len = query.shape[0]
    causal = jnp.arange(seq_len)[:, None] >= jnp.arange(seq_len)[None, :]
    scores = jnp.einsum('skgd,tkd->kgst', query, keys_rot, preferred_element_type=jnp.float32) * HEAD_DIM ** -0.5
    return jnp.where(causal, scores, -1e30)


def block_forward(x_loc, gain_row, w_qkv_l, w_out_l, w_gate_l, w_up_l, w_down_l, cos_tab, sin_tab, with_output):
    seq_len = cos_tab.shape[0]
    heads_local = w_out_l.shape[0] // HEAD_DIM
    kv_local = (w_qkv_l.shape[1] // HEAD_DIM - heads_local) // 2
    group_size = heads_local // kv_local
    x_f32 = x_loc.astype(jnp.float32)
    u_loc = rms_scale(x_f32, gain_row).astype(jnp.bfloat16)
    u_full = lax.all_gather(u_loc, 'tp', axis=0, tiled=True)
    qkv_all = jnp.dot(u_full, w_qkv_l, preferred_element_type=jnp.float32).astype(jnp.bfloat16).reshape(seq_len, kv_local, group_size + 2, HEAD_DIM)
    rotated = rotate(qkv_all[:, :, :group_size + 1].astype(jnp.float32), cos_tab, sin_tab).astype(jnp.bfloat16)
    query = rotated[:, :, :group_size]
    keys_rot = rotated[:, :, group_size]
    values_v = qkv_all[:, :, group_size + 1]
    scores = causal_scores(query, keys_rot)
    row_max = jnp.max(scores, axis=-1, keepdims=True)
    log_norm = row_max + jnp.log(jnp.sum(jnp.exp(scores - row_max), axis=-1, keepdims=True))
    attn_prob = jnp.exp(scores - log_norm).astype(jnp.bfloat16)
    attn_out = jnp.einsum('kgst,tkd->skgd', attn_prob, values_v, preferred_element_type=jnp.float32).astype(jnp.bfloat16).reshape(seq_len, heads_local * HEAD_DIM)
    gate_act = jnp.dot(u_full, w_gate_l, preferred_element_type=jnp.float32).astype(jnp.bfloat16)
    up_act = jnp.dot(u_full, w_up_l, preferred_element_type=jnp.float32).astype(jnp.bfloat16)
    saved = {'x_loc': x_loc, 'u_loc': u_loc, 'query': query, 'keys_rot': keys_rot, 'values_v': values_v, 'attn_out': attn_out, 'log_norm': log_norm, 'gate_act': gate_act, 'up_act': up_act}
    if not with_output:
        return None, saved
    hidden = gated(gate_act.astype(jnp.float32), up_act.astype(jnp.float32)).astype(jnp.bfloat16)
    block_part = jnp.dot(attn_out, w_out_l, preferred_element_type=jnp.float32) + jnp.dot(hidden, w_down_l, preferred_element_type=jnp.float32)
    y_loc = (x_f32 + lax.psum_scatter(block_part, 'tp', scatter_dimension=0, tiled=True)).astype(jnp.bfloat16)
    return y_loc, saved


def block_backward(dy_loc, saved, gain_row, w_qkv_l, w_out_l, w_gate_l, w_up_l, w_down_l, cos_tab, sin_tab):
    saved, dy_loc = lax.optimization_barrier((saved, dy_loc))
    query = saved['query']
    keys_rot = saved['keys_rot']
    values_v = saved['values_v']
    seq_len, kv_local, group_size = query.shape[0], query.shape[1], query.shape[2]
    u_full = lax.all_gather(saved['u_loc'], 'tp', axis=0, tiled=True)
    dy_full = lax.all_gather(dy_loc, 'tp', axis=0, tiled=True)
    grad_out_l = jnp.einsum('sh,sd->hd', saved['attn_out'], dy_full, preferred_element_type=jnp.float32).astype(jnp.bfloat16)
    d_attn = jnp.einsum('sd,hd->sh', dy_full, w_out_l, preferred_element_type=jnp.float32).astype(jnp.bfloat16).reshape(seq_len, kv_local, group_size, HEAD_DIM)
    hidden_f32, gated_pull = jax.vjp(gated, saved['gate_act'].astype(jnp.float32), saved['up_act'].astype(jnp.float32))
    hidden = hidden_f32.astype(jnp.bfloat16)
    grad_down_l = jnp.einsum('sf,sd->fd', hidden, dy_full, preferred_element_type=jnp.float32).astype(jnp.bfloat16)
    d_hidden = jnp.einsum('sd,fd->sf', dy_full, w_down_l, preferred_element_type=jnp.float32).astype(jnp.bfloat16)
    d_gate_f32, d_up_f32 = gated_pull(d_hidden.astype(jnp.float32))
    d_gate = d_gate_f32.astype(jnp.bfloat16)
    d_up = d_up_f32.astype(jnp.bfloat16)
    grad_gate_l = jnp.einsum('sd,sf->df', u_full, d_gate, preferred_element_type=jnp.float32).astype(jnp.bfloat16)
    grad_up_l = jnp.einsum('sd,sf->df', u_full, d_up, preferred_element_type=jnp.float32).astype(jnp.bfloat16)
    attn_prob_f32 = jnp.exp(causal_scores(query, keys_rot) - saved['log_norm'])
    attn_prob = attn_prob_f32.astype(jnp.bfloat16)
    d_values = jnp.einsum('kgst,skgd->tkd', attn_prob, d_attn, preferred_element_type=jnp.float32).astype(jnp.bfloat16)
    d_prob = jnp.einsum('skgd,tkd->kgst', d_attn, values_v, preferred_element_type=jnp.float32).astype(jnp.bfloat16).astype(jnp.float32)
    d_scores = (attn_prob_f32 * (d_prob - jnp.sum(attn_prob_f32 * d_prob, axis=-1, keepdims=True)) * HEAD_DIM ** -0.5).astype(jnp.bfloat16)
    d_query = jnp.einsum('kgst,tkd->skgd', d_scores, keys_rot, preferred_element_type=jnp.float32).astype(jnp.bfloat16)
    d_keys = jnp.einsum('kgst,skgd->tkd', d_scores, query, preferred_element_type=jnp.float32).astype(jnp.bfloat16)
    d_rotated = jnp.concatenate([d_query, d_keys[:, :, None]], axis=2).astype(jnp.float32)
    d_unrotated = rotate(d_rotated, cos_tab, -sin_tab).astype(jnp.bfloat16)
    d_qkv = jnp.concatenate([d_unrotated, d_values[:, :, None]], axis=2).reshape(seq_len, w_qkv_l.shape[1])
    grad_qkv_l = jnp.einsum('sd,sc->dc', u_full, d_qkv, preferred_element_type=jnp.float32).astype(jnp.bfloat16)
    normed_part = jnp.einsum('sc,dc->sd', d_qkv, w_qkv_l, preferred_element_type=jnp.float32) + jnp.einsum('sf,df->sd', d_gate, w_gate_l, preferred_element_type=jnp.float32) + jnp.einsum('sf,df->sd', d_up, w_up_l, preferred_element_type=jnp.float32)
    d_normed = lax.psum_scatter(normed_part, 'tp', scatter_dimension=0, tiled=True).astype(jnp.bfloat16)
    norm_pull = jax.vjp(rms_scale, saved['x_loc'].astype(jnp.float32), gain_row)[1]
    d_x_norm, grad_gain_l = norm_pull(d_normed.astype(jnp.float32))
    grad_x_loc = (dy_loc.astype(jnp.float32) + d_x_norm).astype(jnp.bfloat16)
    return grad_x_loc, grad_gain_l, grad_qkv_l, grad_out_l, grad_gate_l, grad_up_l, grad_down_l


def solution(mesh):
    tp_size = mesh.shape['tp']
    row_spec = P(('dp', 'tp'), None)
    col_spec = P(None, None, 'tp')
    inner_spec = P(None, 'tp', None)

    def device_program(x_loc, dy_loc, norm_gain, w_qkv, w_out, w_gate, w_up, w_down):
        n_layers = w_qkv.shape[0]
        cos_tab, sin_tab = rope_tables(x_loc.shape[0] * tp_size)
        saved_all = []
        x_cur = x_loc
        for layer_idx in range(n_layers):
            x_cur, saved = block_forward(x_cur, norm_gain[layer_idx], w_qkv[layer_idx], w_out[layer_idx], w_gate[layer_idx], w_up[layer_idx], w_down[layer_idx], cos_tab, sin_tab, layer_idx < n_layers - 1)
            saved_all.append(saved)
        grad_cur = dy_loc
        layer_grads = []
        for layer_idx in reversed(range(n_layers)):
            results = block_backward(grad_cur, saved_all[layer_idx], norm_gain[layer_idx], w_qkv[layer_idx], w_out[layer_idx], w_gate[layer_idx], w_up[layer_idx], w_down[layer_idx], cos_tab, sin_tab)
            grad_cur = results[0]
            layer_grads.insert(0, results[1:])
        grad_gain = lax.psum(jnp.stack([item[0] for item in layer_grads]), 'tp')
        stacked = [jnp.stack([item[grad_idx] for item in layer_grads]) for grad_idx in range(1, 6)]
        return (grad_cur, grad_gain, stacked[0], stacked[1], stacked[2], stacked[3], stacked[4])

    return jax.shard_map(device_program, mesh=mesh, in_specs=(row_spec, row_spec, P(None, None), col_spec, inner_spec, col_spec, col_spec, inner_spec), out_specs=(row_spec, P('dp', None), P('dp', None, 'tp'), P('dp', 'tp', None), P('dp', None, 'tp'), P('dp', None, 'tp'), P('dp', 'tp', None)), check_vma=False)
```

profile of v0, /device:TPU:0, one launch (start us, length us, event | category | flops | bytes accessed | tf_op | source)
XLA Modules:
  0.0 1923.1 jit_solution(99578637053402029)
XLA Ops:
  17.6 51.4 %all-gather.10.cloned.1.call-done = bf16[1536,3072]{1,0:T(8,128)(2,1)} async-done(((bf16[192,3072]{1,0:T(8,128)(2,1)}), bf16[1536,3072]{1,0:T(8,128)(2,1)}) %all-gather.10.cloned.1.call-update) | async-done | bytes 9437200 | tf_op jit(solution)/shard_map/all_gather | solution.py:48
  89.1 12.1 fusion.24
  101.2 12.8 exponential_reduce_fusion.2
  114.0 13.5 fusion.203
  127.6 14.4 fusion.151
  142.1 15.1 fusion.154
  157.2 17.9 fusion.105
  175.1 13.9 convolution_add_fusion.1
  189.1 117.2 %reduce-scatter.6.cloned.1.call-done = f32[192,3072]{1,0:T(8,128)} async-done(((f32[1536,3072]{1,0:T(8,128)}), f32[192,3072]{1,0:T(8,128)}) %reduce-scatter.6.cloned.1.call-update) | async-done | bytes 2359312 | tf_op jit(solution)/shard_map/reduce_scatter | solution.py:66
  309.9 53.1 %all-gather.12.cloned.1.call-done = bf16[1536,3072]{1,0:T(8,128)(2,1)} async-done(((bf16[192,3072]{1,0:T(8,128)(2,1)}), bf16[1536,3072]{1,0:T(8,128)(2,1)}) %all-gather.12.cloned.1.call-update) | async-done | bytes 9437200 | tf_op jit(solution)/shard_map/all_gather | solution.py:48
  383.0 12.1 fusion.25
  395.1 12.8 exponential_reduce_fusion.1
  407.9 13.8 fusion.206
  421.7 14.4 fusion.160
  436.2 15.1 fusion.163
  451.4 17.9 fusion.94
  469.3 13.9 convolution_add_fusion
  483.2 117.2 %reduce-scatter.8.cloned.1.call-done = f32[192,3072]{1,0:T(8,128)} async-done(((f32[1536,3072]{1,0:T(8,128)}), f32[192,3072]{1,0:T(8,128)}) %reduce-scatter.8.cloned.1.call-update) | async-done | bytes 2359312 | tf_op jit(solution)/shard_map/reduce_scatter | solution.py:66
  604.0 53.1 %all-gather.14.cloned.1.call-done = bf16[1536,3072]{1,0:T(8,128)(2,1)} async-done(((bf16[192,3072]{1,0:T(8,128)(2,1)}), bf16[1536,3072]{1,0:T(8,128)(2,1)}) %all-gather.14.cloned.1.call-update) | async-done | bytes 9437200 | tf_op jit(solution)/shard_map/all_gather | solution.py:48
  676.2 12.1 fusion.26
  688.3 12.8 exponential_reduce_fusion
  701.1 14.7 fusion.209
  715.8 15.4 fusion.169
  731.2 15.5 fusion.172
  746.8 53.1 %all-gather.16.cloned.1.call-done = bf16[1536,3072]{1,0:T(8,128)(2,1)} async-done(((bf16[192,3072]{1,0:T(8,128)(2,1)}), bf16[1536,3072]{1,0:T(8,128)(2,1)}) %all-gather.16.cloned.1.call-update) | async-done | bytes 9437200 | tf_op jit(solution)/shard_map/all_gather | solution.py:77
  815.6 19.6 %fusion.20 = (f32[3,1536]{1,0:T(4,128)}, f32[1,3,1536,1536]{2,3,1,0:T(8,128)}) fusion(bf16[1536,1536,3]{1,0,2:T(8,128)(2,1)} %convolution_convert_fusion.2, f32[3,1536]{1,0:T(4,128)} %copy-done.58, bf16[1536,1,3,128]{3,0,2,1:T(8,128)(2,1)} %copy-done.45, bf16[1536,1,128]{2,0,1:T(8,128)(2,1)S(1)} %bitcast.634, pred[1536,1536]{0,1:T(8,128)(4,1)S(1)} %copy-done.11), kind=kOutput, calls=%fused_computation.29 | convolution fusion | flops 1854402048 | bytes 46436352 | tf_op jit(solution)/shard_map/skgd,tkd->kgst/dot_general | solution.py:37
  835.2 13.3 fusion.271
  848.5 14.7 fusion.30
  889.2 13.9 fusion.136
  903.2 14.2 fusion.175
  919.2 19.3 %fusion.88 = f32[1536,3072]{1,0:T(8,128)} fusion(bf16[3,3072,1024]{2,1,0:T(8,128)(2,1)} %param.13, bf16[1536,1024]{1,0:T(8,128)(2,1)S(1)} %copy-done.69, bf16[1536,1024]{1,0:T(8,128)(2,1)S(1)} %copy-done.77, bf16[1536,1024]{1,0:T(8,128)(2,1)S(1)} %fusion.175), kind=kOutput, calls=%fused_computation.139 | convolution fusion | flops 9685696512 | bytes 34603008 | tf_op jit(solution)/shard_map/sf,df->sd/dot_general | solution.py:100
  938.4 27.4 %add_add_fusion.2 = f32[1536,3072]{1,0:T(8,128)} fusion(f32[1536,3072]{1,0:T(8,128)} %fusion.136, f32[1536,3072]{1,0:T(8,128)} %fusion.88, bf16[3,3072,1024]{2,1,0:T(8,128)(2,1)} %param.14, bf16[1536,1024]{1,0:T(8,128)(2,1)} %copy-done.71, bf16[1536,1024]{1,0:T(8,128)(2,1)} %fusion.169), kind=kOutput, calls=%fused_computation.47 | convolution fusion | flops 9685696512 | bytes 69206016 | tf_op jit(solution)/shard_map/sf,df->sd/dot_general | solution.py:100
  968.7 114.4 %reduce-scatter.10.cloned.1.call-done = f32[192,3072]{1,0:T(8,128)} async-done(((f32[1536,3072]{1,0:T(8,128)}), f32[192,3072]{1,0:T(8,128)}) %reduce-scatter.10.cloned.1.call-update) | async-done | bytes 2359312 | tf_op jit(solution)/shard_map/reduce_scatter | solution.py:101
  1091.2 52.9 %all-gather.18.cloned.1.call-done = bf16[1536,3072]{1,0:T(8,128)(2,1)} async-done(((bf16[192,3072]{1,0:T(8,128)(2,1)}), bf16[1536,3072]{1,0:T(8,128)(2,1)}) %all-gather.18.cloned.1.call-update) | async-done | bytes 9437200 | tf_op jit(solution)/shard_map/all_gather | solution.py:77
  1160.6 18.8 fusion.14
  1179.4 11.1 fusion.274
  1190.6 14.9 fusion.31
  1228.3 14.1 fusion.140
  1242.4 13.8 fusion.166
  1256.2 22.4 %fusion.99 = f32[1536,3072]{1,0:T(8,128)} fusion(bf16[3,3072,1024]{2,1,0:T(8,128)(2,1)} %param.13, bf16[1536,1024]{1,0:T(8,128)(2,1)} %copy-done.66, bf16[1536,1024]{1,0:T(8,128)(2,1)} %copy-done.75, bf16[1536,1024]{1,0:T(8,128)(2,1)} %fusion.166), kind=kOutput, calls=%fused_computation.150 | convolution fusion | flops 9685696512 | bytes 34603008 | tf_op jit(solution)/shard_map/sf,df->sd/dot_general | solution.py:100
  1278.7 28.1 %add_add_fusion.1 = f32[1536,3072]{1,0:T(8,128)} fusion(f32[1536,3072]{1,0:T(8,128)} %fusion.140, f32[1536,3072]{1,0:T(8,128)} %fusion.99, bf16[3,3072,1024]{2,1,0:T(8,128)(2,1)} %param.14, bf16[1536,1024]{1,0:T(8,128)(2,1)} %fusion.166, bf16[1536,1024]{1,0:T(8,128)(2,1)S(1)} %copy-done.67), kind=kOutput, calls=%fused_computation.46 | convolution fusion | flops 9685696512 | bytes 69206016 | tf_op jit(solution)/shard_map/sf,df->sd/dot_general | solution.py:100
  1309.6 114.4 %reduce-scatter.12.cloned.1.call-done = f32[192,3072]{1,0:T(8,128)} async-done(((f32[1536,3072]{1,0:T(8,128)}), f32[192,3072]{1,0:T(8,128)}) %reduce-scatter.12.cloned.1.call-update) | async-done | bytes 2359312 | tf_op jit(solution)/shard_map/reduce_scatter | solution.py:101
  1431.5 17.5 convert_bitcast_fusion.3
  1449.0 29.7 %all-gather.26.cloned.1.call-done = bf16[1536,3072]{1,0:T(8,128)(2,1)} async-done(((bf16[192,3072]{1,0:T(8,128)(2,1)}), bf16[1536,3072]{1,0:T(8,128)(2,1)}) %all-gather.26.cloned.1.call-update) | async-done | bytes 9437200 | tf_op jit(solution)/shard_map/all_gather | solution.py:76
  1478.7 11.6 fusion.135
  1490.2 16.2 convert_bitcast_fusion.9
  1506.5 13.0 convert_bitcast_fusion.6
  1519.5 13.9 all-gather.20.cloned.1.call-done
  1550.3 18.9 fusion.8
  1569.2 20.2 %fusion.32 = bf16[3,1536,1536]{1,2,0:T(8,128)(2,1)} fusion(f32[1,3,1536,1536]{2,3,1,0:T(8,128)} %get-tuple-element.106, bf16[1536,1536,3]{1,0,2:T(8,128)(2,1)} %convolution_convert_fusion, f32[3,1536]{1,0:T(4,128)} %get-tuple-element.105), kind=kLoop, calls=%fused_computation.53 | loop fusion | flops 35389440 | bytes 56641536 | tf_op jit(solution)/shard_map/reshape.100
  1610.6 11.1 fusion.277
  1626.9 14.1 fusion.144
  1640.9 13.7 fusion.157
  1654.7 22.3 %fusion.110 = f32[1536,3072]{1,0:T(8,128)} fusion(bf16[3,3072,1024]{2,1,0:T(8,128)(2,1)} %param.13, bf16[1536,1024]{1,0:T(8,128)(2,1)} %copy-done.63, bf16[1536,1024]{1,0:T(8,128)(2,1)} %copy-done.74, bf16[1536,1024]{1,0:T(8,128)(2,1)} %fusion.157), kind=kOutput, calls=%fused_computation.161 | convolution fusion | flops 9685696512 | bytes 34603008 | tf_op jit(solution)/shard_map/sf,df->sd/dot_general | solution.py:100
  1676.9 28.0 %add_add_fusion = f32[1536,3072]{1,0:T(8,128)} fusion(f32[1536,3072]{1,0:T(8,128)} %fusion.144, f32[1536,3072]{1,0:T(8,128)} %fusion.110, bf16[3,3072,1024]{2,1,0:T(8,128)(2,1)} %param.14, bf16[1536,1024]{1,0:T(8,128)(2,1)} %fusion.157, bf16[1536,1024]{1,0:T(8,128)(2,1)S(1)} %copy-done.64), kind=kOutput, calls=%fused_computation.45 | convolution fusion | flops 9685696512 | bytes 69206016 | tf_op jit(solution)/shard_map/sf,df->sd/dot_general | solution.py:100
  1723.5 13.9 convert_bitcast_fusion.4
  1737.4 12.4 fusion.134
  1749.8 15.7 convert_bitcast_fusion.10
  1765.5 15.4 convert_bitcast_fusion.7
  1805.8 16.7 convert_bitcast_fusion.5
  1830.4 18.2 convert_bitcast_fusion.11
  1848.6 13.3 convert_bitcast_fusion.8
  1862.0 24.9 %pad_maximum_fusion = (bf16[3,3072,1024]{2,1,0:T(8,128)(2,1)}, bf16[3,3072,1024]{2,1,0:T(8,128)(2,1)}) fusion(bf16[1,3072,1024]{2,1,0:T(8,128)(2,1)} %convert_bitcast_fusion.9, bf16[1,3072,1024]{2,1,0:T(8,128)(2,1)} %convert_bitcast_fusion.10, bf16[1,3072,1024]{2,1,0:T(8,128)(2,1)} %convert_bitcast_fusion.11, ...), kind=kLoop, calls=%fused_computation.42 | loop fusion | flops 37748736 | bytes 75497472 | tf_op jit(solution)/shard_map/stack | solution.py:129
  1889.8 23.1 %psum.7 = f32[3,3072]{1,0:T(4,128)} all-reduce(f32[3,3072]{1,0:T(4,128)S(1)} %pad_maximum_fusion.14), channel_id=1, replica_groups=mesh['dp'=1,'tp'=8] {'tp'}, use_global_device_ids=true, to_apply=%region_26.27 | all-reduce | flops 9216 | bytes 73728 | tf_op jit(solution)/shard_map/psum | solution.py:128
  (319 shorter events, 281.2 us)
Async XLA Ops:
  7.2 61.8 %all-gather.10.cloned.1.call-start = ((), (), s32[]{:S(2)}) async-start(), calls=%async_computation.5 | async-start | bytes 10616832 | tf_op jit(solution)/shard_map/all_gather | solution.py:48
  8.8 299.7 %copy-start.49 = (f32[1,3072]{1,0:T(1,128)}, f32[1,3072]{1,0:T(1,128)S(1)}, u32[]{:S(2)}) copy-start(f32[1,3072]{1,0:T(1,128)S(1)} %get-tuple-element.91) | copy-start | bytes 36868
  13.1 293.2 %reduce-scatter.6.cloned.1.call-start = ((), (), s32[]{:S(2)}) async-start(), calls=%async_computation.6 | async-start | bytes 21233664 | tf_op jit(solution)/shard_map/reduce_scatter | solution.py:66
  16.9 865.0 %copy-start.6 = (f32[1536,64]{1,0:T(8,128)}, f32[1536,64]{1,0:T(8,128)S(1)}, u32[]{:S(2)}) copy-start(f32[1536,64]{1,0:T(8,128)S(1)} %get-tuple-element.94) | copy-start | bytes 1179652
  17.6 96.5 %copy-start.9 = (pred[1536,1536]{0,1:T(8,128)(4,1)}, pred[1536,1536]{0,1:T(8,128)(4,1)S(1)}, u32[]{:S(2)}) copy-start(pred[1536,1536]{0,1:T(8,128)(4,1)S(1)} %iota_compare_fusion) | copy-start | bytes 7077892
  127.6 47.6 %copy-start.26 = (bf16[128,3,1536]{2,0,1:T(8,128)(2,1)}, bf16[128,3,1536]{2,0,1:T(8,128)(2,1)S(1)}, u32[]{:S(2)}) copy-start(bf16[128,3,1536]{2,0,1:T(8,128)(2,1)S(1)} %fusion.203) | copy-start | bytes 3538948
  142.0 15.2 copy-start.63
  157.2 17.9 copy-start.74
  189.0 117.2 %copy-start.4 = (bf16[192,3072]{1,0:T(8,128)(2,1)S(1)}, bf16[192,3072]{1,0:T(8,128)(2,1)}, u32[]{:S(2)}) copy-start(bf16[192,3072]{1,0:T(8,128)(2,1)} %param.8) | copy-start | bytes 3538948
  189.0 173.9 %all-gather.12.cloned.1.call-start = ((), (), s32[]{:S(2)}) async-start(), calls=%async_computation.7 | async-start | bytes 10616832 | tf_op jit(solution)/shard_map/all_gather | solution.py:48
  308.4 292.0 %copy-start.2 = (bf16[192,3072]{1,0:T(8,128)(2,1)}, bf16[192,3072]{1,0:T(8,128)(2,1)S(1)}, u32[]{:S(2)}) copy-start(bf16[192,3072]{1,0:T(8,128)(2,1)S(1)} %get-tuple-element.52) | copy-start | bytes 3538948
  309.9 290.5 %reduce-scatter.8.cloned.1.call-start = ((), (), s32[]{:S(2)}) async-start(), calls=%async_computation.8 | async-start | bytes 21233664 | tf_op jit(solution)/shard_map/reduce_scatter | solution.py:66
  421.7 47.6 %copy-start.28 = (bf16[128,3,1536]{2,0,1:T(8,128)(2,1)}, bf16[128,3,1536]{2,0,1:T(8,128)(2,1)S(1)}, u32[]{:S(2)}) copy-start(bf16[128,3,1536]{2,0,1:T(8,128)(2,1)S(1)} %fusion.206) | copy-start | bytes 3538948
  436.2 15.2 copy-start.66
  451.3 17.9 copy-start.75
  483.1 119.4 %copy-start.51 = (f32[1,3072]{1,0:T(1,128)S(1)}, f32[1,3072]{1,0:T(1,128)}, u32[]{:S(2)}) copy-start(f32[1,3072]{1,0:T(1,128)} %get-tuple-element.89) | copy-start | bytes 36868
  483.2 173.9 %all-gather.14.cloned.1.call-start = ((), (), s32[]{:S(2)}) async-start(), calls=%async_computation.9 | async-start | bytes 10616832 | tf_op jit(solution)/shard_map/all_gather | solution.py:48
  602.5 64.9 %copy-start.13 = (bf16[192,3072]{1,0:T(8,128)(2,1)}, bf16[192,3072]{1,0:T(8,128)(2,1)S(1)}, u32[]{:S(2)}) copy-start(bf16[192,3072]{1,0:T(8,128)(2,1)S(1)} %get-tuple-element.44) | copy-start | bytes 3538948
  604.0 195.8 %all-gather.16.cloned.1.call-start = ((), (), s32[]{:S(2)}) async-start(), calls=%async_computation.10 | async-start | bytes 10616832 | tf_op jit(solution)/shard_map/all_gather | solution.py:77
  673.9 14.4 copy-start.45
  674.1 141.5 %copy-start.38 = (bf16[1536,1,1,128]{3,0,2,1:T(8,128)(2,1)}, bf16[1536,1,1,128]{3,0,2,1:T(8,128)(2,1)S(1)}, u32[]{:S(2)}) copy-start(bf16[1536,1,1,128]{3,0,2,1:T(8,128)(2,1)S(1)} %pad_maximum_fusion.11) | copy-start | bytes 1179652
  701.1 14.7 copy-start.58
  746.7 336.4 %reduce-scatter.10.cloned.1.call-start = ((), (), s32[]{:S(2)}) async-start(), calls=%async_computation.11 | async-start | bytes 21233664 | tf_op jit(solution)/shard_map/reduce_scatter | solution.py:101
  848.5 20.0 %copy-start.46 = (bf16[1536,1,3,128]{3,0,2,1:T(8,128)(2,1)S(1)}, bf16[1536,1,3,128]{3,0,2,1:T(8,128)(2,1)}, u32[]{:S(2)}) copy-start(bf16[1536,1,3,128]{3,0,2,1:T(8,128)(2,1)} %copy-done.45) | copy-start | bytes 3538948
  903.2 16.0 copy-start.69
  903.2 16.0 copy-start.77
  965.9 117.3 %copy-start.52 = (f32[1,3072]{1,0:T(1,128)S(1)}, f32[1,3072]{1,0:T(1,128)}, u32[]{:S(2)}) copy-start(f32[1,3072]{1,0:T(1,128)} %get-tuple-element.89) | copy-start | bytes 36868
  965.9 178.2 %all-gather.18.cloned.1.call-start = ((), (), s32[]{:S(2)}) async-start(), calls=%async_computation.12 | async-start | bytes 10616832 | tf_op jit(solution)/shard_map/all_gather | solution.py:77
  1091.0 333.0 %reduce-scatter.12.cloned.1.call-start = ((), (), s32[]{:S(2)}) async-start(), calls=%async_computation.13 | async-start | bytes 21233664 | tf_op jit(solution)/shard_map/reduce_scatter | solution.py:101
  1190.6 20.2 %copy-start.44 = (bf16[1536,1,3,128]{3,0,2,1:T(8,128)(2,1)S(1)}, bf16[1536,1,3,128]{3,0,2,1:T(8,128)(2,1)}, u32[]{:S(2)}) copy-start(bf16[1536,1,3,128]{3,0,2,1:T(8,128)(2,1)} %copy-done.43) | copy-start | bytes 3538948
  1226.0 16.4 slice-start.4
  1228.3 14.1 slice-start.6
  1256.2 22.4 %copy-start.67 = (bf16[1536,1024]{1,0:T(8,128)(2,1)S(1)}, bf16[1536,1024]{1,0:T(8,128)(2,1)}, u32[]{:S(2)}) copy-start(bf16[1536,1024]{1,0:T(8,128)(2,1)} %copy-done.66) | copy-start | bytes 9437188
  1306.8 117.2 %copy-start.50 = (f32[1,3072]{1,0:T(1,128)S(1)}, f32[1,3072]{1,0:T(1,128)}, u32[]{:S(2)}) copy-start(f32[1,3072]{1,0:T(1,128)} %copy-done.49) | copy-start | bytes 36868
  1306.8 120.6 %copy-start.21 = (bf16[192,3072]{1,0:T(8,128)(2,1)S(1)}, bf16[192,3072]{1,0:T(8,128)(2,1)}, u32[]{:S(2)}) copy-start(bf16[192,3072]{1,0:T(8,128)(2,1)} %fusion.251) | copy-start | bytes 3538948
  1306.8 171.8 %all-gather.26.cloned.1.call-start = ((), (), s32[]{:S(2)}) async-start(), calls=%async_computation.18 | async-start | bytes 10616832 | tf_op jit(solution)/shard_map/all_gather | solution.py:76
  1307.4 226.0 %all-gather.20.cloned.1.call-start = ((), (), s32[]{:S(2)}) async-start(), calls=%async_computation.14 | async-start | bytes 10616832 | tf_op jit(solution)/shard_map/all_gather | solution.py:77
  1430.9 306.5 %all-gather.24.cloned.1.call-start = ((), (), s32[]{:S(2)}) async-start(), calls=%async_computation.17 | async-start | bytes 10616832 | tf_op jit(solution)/shard_map/all_gather | solution.py:76
  1431.4 47.2 %copy-start.33 = (bf16[1536,1,5,128]{0,3,2,1:T(8,128)(2,1)S(1)}, bf16[1536,1,5,128]{0,3,2,1:T(8,128)(2,1)}, u32[]{:S(2)}) copy-start(bf16[1536,1,5,128]{0,3,2,1:T(8,128)(2,1)} %copy.65) | copy-start | bytes 5898244
  1431.5 357.3 %all-gather.22.cloned.1.call-start = ((), (), s32[]{:S(2)}) async-start(), calls=%async_computation.16 | async-start | bytes 10616832 | tf_op jit(solution)/shard_map/all_gather | solution.py:76
  1519.5 367.4 %reduce-scatter.14.cloned.1.call-start = ((), (), s32[]{:S(2)}) async-start(), calls=%async_computation.15 | async-start | bytes 21233664 | tf_op jit(solution)/shard_map/reduce_scatter | solution.py:101
  1569.2 20.2 %copy-start.35 = (bf16[1536,1,1,128]{3,0,2,1:T(8,128)(2,1)S(1)}, bf16[1536,1,1,128]{3,0,2,1:T(8,128)(2,1)}, u32[]{:S(2)}) copy-start(bf16[1536,1,1,128]{3,0,2,1:T(8,128)(2,1)} %copy-done.34) | copy-start | bytes 1179652
  1624.5 16.4 slice-start.10
  1654.7 22.3 %copy-start.64 = (bf16[1536,1024]{1,0:T(8,128)(2,1)S(1)}, bf16[1536,1024]{1,0:T(8,128)(2,1)}, u32[]{:S(2)}) copy-start(bf16[1536,1024]{1,0:T(8,128)(2,1)} %copy-done.63) | copy-start | bytes 9437188
  1706.3 17.2 slice-start.7
  1706.3 17.2 slice-start.8
  1749.8 31.5 %slice-start.13 = ((s8[9437184]{0:T(1024)(128)(4,1)}), s8[1048576]{0:T(1024)(128)(4,1)S(1)}, s32[]{:S(2)}) async-start(s8[9437184]{0:T(1024)(128)(4,1)} %bitcast.654), calls=%async_computation.32 | async-start | bytes 2097152
  1749.8 31.5 %slice-start.14 = ((s8[9437184]{0:T(1024)(128)(4,1)}), s8[4194304]{0:T(1024)(128)(4,1)S(1)}, s32[]{:S(2)}) async-start(s8[9437184]{0:T(1024)(128)(4,1)} %bitcast.654), calls=%async_computation.33 | async-start | bytes 8388608
  1765.5 15.5 copy-start.5
  1765.5 15.8 copy-start.27
  1765.5 15.8 slice-start.15
  1799.7 22.8 %slice-start = ((s8[6291456]{0:T(1024)(128)(4,1)}), s8[4194304]{0:T(1024)(128)(4,1)S(1)}, s32[]{:S(2)}) async-start(s8[6291456]{0:T(1024)(128)(4,1)} %bitcast.607), calls=%async_computation.19 | async-start | bytes 8388608
  1799.7 22.8 %slice-start.2 = ((s8[6291456]{0:T(1024)(128)(4,1)}), s8[4194304]{0:T(1024)(128)(4,1)S(1)}, s32[]{:S(2)}) async-start(s8[6291456]{0:T(1024)(128)(4,1)} %bitcast.609), calls=%async_computation.21 | async-start | bytes 8388608
  1805.8 16.8 slice-start.1
  1805.8 16.8 slice-start.3
  1822.6 26.0 %slice-start.16 = ((s8[9437184]{0:T(1024)(128)(4,1)}), s8[1048576]{0:T(1024)(128)(4,1)S(1)}, s32[]{:S(2)}) async-start(s8[9437184]{0:T(1024)(128)(4,1)} %bitcast.656), calls=%async_computation.35 | async-start | bytes 2097152
  1830.4 18.2 slice-start.17
  1830.4 18.2 slice-start.18
  1830.4 18.2 copy-start.65
  1830.4 18.2 copy-start.73
  1862.0 25.0 %copy-start.48 = (f32[1,3072]{1,0:T(1,128)S(1)}, f32[1,3072]{1,0:T(1,128)}, u32[]{:S(2)}) copy-start(f32[1,3072]{1,0:T(1,128)} %copy-done.47) | copy-start | bytes 36868
  1862.0 27.8 %copy-start.53 = (f32[3072]{0:T(1024)S(1)}, f32[3072]{0:T(1024)}, u32[]{:S(2)}) copy-start(f32[3072]{0:T(1024)} %get-tuple-element.71) | copy-start | bytes 36868
  1862.0 27.8 %copy-start.54 = (f32[3072]{0:T(1024)S(1)}, f32[3072]{0:T(1024)}, u32[]{:S(2)}) copy-start(f32[3072]{0:T(1024)} %get-tuple-element.69) | copy-start | bytes 36868
  1862.0 51.0 %copy-start.20 = (bf16[192,3072]{1,0:T(8,128)(2,1)S(1)}, bf16[192,3072]{1,0:T(8,128)(2,1)}, u32[]{:S(2)}) copy-start(bf16[192,3072]{1,0:T(8,128)(2,1)} %fusion.253) | copy-start | bytes 3538948
  (47 other events, 367.2 us)
Sparse Core Ops, SparseCore 0:
  13.2 55.7 all-gather.9
  189.2 117.0 reduce-scatter.5
  310.0 52.9 all-gather.11
  483.3 117.0 reduce-scatter.7
  604.1 52.9 all-gather.13
  746.8 52.9 all-gather.15
  966.0 117.0 reduce-scatter.9
  1091.1 52.9 all-gather.17
  1307.0 117.0 reduce-scatter.11
  1425.7 52.9 all-gather.25
  1480.5 52.9 all-gather.19
  1535.1 52.9 all-gather.23
  1590.5 52.9 all-gather.21
  1705.1 117.0 reduce-scatter.13
where the time goes:
time: 1930 us; the launch traced here: 1920 us
  matrix products  876 us (45%)
  waiting for transfers between devices  771 us (40%)
  other arithmetic  191 us (10%)
  local copies, waits for them, and re-layouts  44.4 us (2%)
  blocking collectives  23.1 us (1%)
    reduce_scatter x2, waiting for transfers between devices, block_forward(): lax.psum_scatter(block_part, 'tp', scatter_dimension=0, tiled=True)  234 us
    reduce_scatter x3, waiting for transfers between devices, block_backward(): lax.psum_scatter(normed_part, 'tp', scatter_dimension=0, tiled=True)  229 us
    all_gather x3, waiting for transfers between devices, block_forward(): u_full = lax.all_gather(u_loc, 'tp', axis=0, tiled=True)  158 us
    all_gather x3, waiting for transfers between devices, block_backward(): dy_full = lax.all_gather(dy_loc, 'tp', axis=0, tiled=True)  120 us
    dot_general x6, matrix products, causal_scores(): jnp.einsum('skgd,tkd->kgst', query, keys_rot, preferred_element_type=jnp....  93.6 us
    dot_general x3, matrix products, block_backward(): jnp.einsum('sf,df->sd', d_up, w_up_l, preferred_element_type=jnp.float32)  83.6 us
    dot_general x3, matrix products, block_backward(): jnp.einsum('sf,df->sd', d_gate, w_gate_l, preferred_element_type=jnp.floa...  64 us
    another operation x9, other arithmetic  59.4 us
  transfers between devices with their start and end apart: 14, of which 11 were waited for; matrix products, arithmetic and copies ran while one was open for 22% of the time, Pallas kernels for 0%

commit v1 on v0

v1 whole, which is shorter than its diff:
```python
import functools

import jax
import jax.numpy as jnp
from jax import lax
from jax.experimental import pallas as pl
from jax.experimental.pallas import tpu as pltpu
from jax.sharding import PartitionSpec as P

HEAD_DIM = 128
NORM_EPS = 1e-5
ROPE_BASE = 10000.0
BF16 = jnp.bfloat16
F32 = jnp.float32
VMEM_MAX = 67043328


def rope_tables(seq_len):
    half_dim = HEAD_DIM // 2
    freqs = ROPE_BASE ** (-2.0 * jnp.arange(half_dim, dtype=F32) / HEAD_DIM)
    angles = jnp.arange(seq_len, dtype=F32)[:, None] * freqs[None, :]
    cos, sin = jnp.cos(angles), jnp.sin(angles)
    return jnp.concatenate([cos, cos], axis=1), jnp.concatenate([-sin, sin], axis=1)


def rms_scale(x_f32, gain_row):
    inv_rms = lax.rsqrt(jnp.mean(x_f32 * x_f32, axis=-1, keepdims=True) + NORM_EPS)
    return x_f32 * inv_rms * gain_row


def gated(gate_f32, up_f32):
    return jax.nn.silu(gate_f32) * up_f32


def dot_nt(lhs, rhs):
    return lax.dot_general(lhs, rhs, (((1,), (1,)), ((), ())), preferred_element_type=F32)


def dot_tn(lhs, rhs):
    return lax.dot_general(lhs, rhs, (((0,), (0,)), ((), ())), preferred_element_type=F32)


def dot_nn(lhs, rhs):
    return lax.dot_general(lhs, rhs, (((1,), (0,)), ((), ())), preferred_element_type=F32)


def turn(values, cos_tab, sin_tab):
    return values * cos_tab + pltpu.roll(values, HEAD_DIM // 2, 1) * sin_tab


def attn_fwd_body(heads, blk, qkv_ref, cos_ref, sin_ref, kv_ref, q_out, k_out, o_out, lse_out, score_buf, k_rot):
    step = pl.program_id(0)
    scale = HEAD_DIM ** -0.5
    kcol = heads * HEAD_DIM
    vcol = kcol + HEAD_DIM
    cos_tab, sin_tab = cos_ref[...], sin_ref[...]
    here = pl.ds(pl.multiple_of(step * blk, blk), blk)
    key = turn(qkv_ref[:, kcol:vcol].astype(F32), cos_tab, sin_tab).astype(BF16)
    k_rot[here, :] = key
    k_out[...] = key
    parts = []
    for head in range(heads):
        cols = slice(head * HEAD_DIM, (head + 1) * HEAD_DIM)
        part = turn(qkv_ref[:, cols].astype(F32), cos_tab, sin_tab).astype(BF16)
        q_out[:, cols] = part
        parts.append(part)
    query = jnp.concatenate(parts, axis=0)
    rows = heads * blk

    diag = dot_nt(query, key) * scale
    row_id = lax.broadcasted_iota(jnp.int32, (heads, blk, blk), 1).reshape(rows, blk)
    col_id = lax.broadcasted_iota(jnp.int32, (rows, blk), 1)
    diag = jnp.where(row_id >= col_id, diag, -1e30)
    top = jnp.max(diag, axis=-1, keepdims=True)

    def first(j, top):
        there = pl.ds(pl.multiple_of(j * blk, blk), blk)
        score = dot_nt(query, k_rot[there, :]) * scale
        score_buf[j] = score
        return jnp.maximum(top, jnp.max(score, axis=-1, keepdims=True))

    top = lax.fori_loop(0, step, first, top)

    diag = jnp.exp(diag - top)
    total = jnp.sum(diag, axis=-1, keepdims=True)

    def second(j, total):
        prob = jnp.exp(score_buf[j] - top)
        score_buf[j] = prob
        return total + jnp.sum(prob, axis=-1, keepdims=True)

    total = lax.fori_loop(0, step, second, total)
    inv = 1.0 / total
    acc = dot_nn((diag * inv).astype(BF16), kv_ref[here, vcol - kcol:])

    def third(j, acc):
        there = pl.ds(pl.multiple_of(j * blk, blk), blk)
        return acc + dot_nn((score_buf[j] * inv).astype(BF16), kv_ref[there, vcol - kcol:])

    acc = lax.fori_loop(0, step, third, acc)
    lse = top + jnp.log(total)
    lane = lax.broadcasted_iota(jnp.int32, (blk, HEAD_DIM), 1)
    packed = jnp.zeros((blk, HEAD_DIM), F32)
    for head in range(heads):
        rws = slice(head * blk, (head + 1) * blk)
        o_out[:, head * HEAD_DIM:(head + 1) * HEAD_DIM] = acc[rws].astype(BF16)
        packed = jnp.where(lane == head, lse[rws], packed)
    lse_out[...] = packed


def attn_forward(qkv, cos_tab, sin_tab, heads, blk=256):
    seq, width = qkv.shape
    hcols = heads * HEAD_DIM
    steps = seq // blk
    row = lambda i: (i, 0)
    flops = 4 * heads * seq * seq * HEAD_DIM // 2
    return pl.pallas_call(
        functools.partial(attn_fwd_body, heads, blk),
        grid=(steps,),
        in_specs=[pl.BlockSpec((blk, width), row), pl.BlockSpec((blk, HEAD_DIM), row), pl.BlockSpec((blk, HEAD_DIM), row), pl.BlockSpec((seq, 2 * HEAD_DIM), lambda i: (0, 0))],
        out_specs=[pl.BlockSpec((blk, hcols), row), pl.BlockSpec((blk, HEAD_DIM), row), pl.BlockSpec((blk, hcols), row), pl.BlockSpec((blk, HEAD_DIM), row)],
        out_shape=[jax.ShapeDtypeStruct((seq, hcols), BF16), jax.ShapeDtypeStruct((seq, HEAD_DIM), BF16), jax.ShapeDtypeStruct((seq, hcols), BF16), jax.ShapeDtypeStruct((seq, HEAD_DIM), F32)],
        scratch_shapes=[pltpu.VMEM((steps, heads * blk, blk), F32), pltpu.VMEM((seq, HEAD_DIM), BF16)],
        compiler_params=pltpu.CompilerParams(dimension_semantics=("arbitrary",), vmem_limit_bytes=40 * 2 ** 20),
        cost_estimate=pl.CostEstimate(flops=flops * 4, bytes_accessed=8 * 2 ** 20, transcendentals=heads * seq * seq // 2),
        name="attn_fwd",
    )(qkv, cos_tab, sin_tab, qkv[:, hcols:])


def attn_bwd_body(heads, blk, q_ref, do_ref, lse_ref, k_ref, v_ref, cos_ref, sin_ref, out_ref, prob_buf, dprob_buf, dk_acc, dv_acc):
    step = pl.program_id(0)
    scale = HEAD_DIM ** -0.5
    rows = heads * blk
    hcols = heads * HEAD_DIM
    here = pl.ds(pl.multiple_of(step * blk, blk), blk)

    @pl.when(step == 0)
    def _():
        dk_acc[...] = jnp.zeros_like(dk_acc)
        dv_acc[...] = jnp.zeros_like(dv_acc)

    def heads_of(ref):
        return jnp.concatenate([ref[:, h * HEAD_DIM:(h + 1) * HEAD_DIM] for h in range(heads)], axis=0)

    query = heads_of(q_ref)
    d_out = heads_of(do_ref)
    lse = jnp.concatenate([lse_ref[:, h:h + 1] for h in range(heads)], axis=0)
    row_id = lax.broadcasted_iota(jnp.int32, (heads, blk, blk), 1).reshape(rows, blk)
    col_id = lax.broadcasted_iota(jnp.int32, (rows, blk), 1)

    def score_part(j, masked):
        there = pl.ds(pl.multiple_of(j * blk, blk), blk)
        score = dot_nt(query, k_ref[there, :]) * scale
        if masked:
            score = jnp.where(row_id >= col_id, score, -1e30)
        prob = jnp.exp(score - lse)
        d_prob = dot_nt(d_out, v_ref[there, :]).astype(BF16)
        prob_buf[j] = prob
        dprob_buf[j] = d_prob
        dv_acc[there, :] += dot_tn(prob.astype(BF16), d_out)
        return jnp.sum(prob * d_prob.astype(F32), axis=-1, keepdims=True)

    row_dot = score_part(step, True)
    row_dot = lax.fori_loop(0, step, lambda j, tot: tot + score_part(j, False), row_dot)

    def grad_part(j, acc):
        there = pl.ds(pl.multiple_of(j * blk, blk), blk)
        d_score = (prob_buf[j] * (dprob_buf[j].astype(F32) - row_dot) * scale).astype(BF16)
        dk_acc[there, :] += dot_tn(d_score, query)
        return acc + dot_nn(d_score, k_ref[there, :])

    d_query = lax.fori_loop(0, step + 1, grad_part, jnp.zeros((rows, HEAD_DIM), F32))
    cos_tab, sin_tab = cos_ref[here, :], sin_ref[here, :]
    for head in range(heads):
        part = d_query[head * blk:(head + 1) * blk].astype(BF16).astype(F32)
        out_ref[here, head * HEAD_DIM:(head + 1) * HEAD_DIM] = turn(part, cos_tab, -sin_tab).astype(BF16)

    @pl.when(step == pl.num_programs(0) - 1)
    def _():
        d_key = dk_acc[...].astype(BF16).astype(F32)
        out_ref[:, hcols:hcols + HEAD_DIM] = turn(d_key, cos_ref[...], -sin_ref[...]).astype(BF16)
        out_ref[:, hcols + HEAD_DIM:] = dv_acc[...].astype(BF16)


def attn_backward(query, d_attn, lse, key, value, cos_tab, sin_tab, heads, blk=256):
    seq = query.shape[0]
    hcols = heads * HEAD_DIM
    width = hcols + 2 * HEAD_DIM
    steps = seq // blk
    row = lambda i: (i, 0)
    whole = lambda i: (0, 0)
    flops = 10 * heads * seq * seq * HEAD_DIM // 2
    return pl.pallas_call(
        functools.partial(attn_bwd_body, heads, blk),
        grid=(steps,),
        in_specs=[pl.BlockSpec((blk, hcols), row), pl.BlockSpec((blk, hcols), row), pl.BlockSpec((blk, HEAD_DIM), row)] + [pl.BlockSpec((seq, HEAD_DIM), whole)] * 4,
        out_specs=pl.BlockSpec((seq, width), whole),
        out_shape=jax.ShapeDtypeStruct((seq, width), BF16),
        scratch_shapes=[pltpu.VMEM((steps, heads * blk, blk), F32), pltpu.VMEM((steps, heads * blk, blk), BF16), pltpu.VMEM((seq, HEAD_DIM), F32), pltpu.VMEM((seq, HEAD_DIM), F32)],
        compiler_params=pltpu.CompilerParams(dimension_semantics=("arbitrary",), vmem_limit_bytes=48 * 2 ** 20),
        cost_estimate=pl.CostEstimate(flops=flops * 4, bytes_accessed=10 * 2 ** 20, transcendentals=heads * seq * seq // 2),
        name="attn_bwd",
    )(query, d_attn, lse, key, value, cos_tab, sin_tab)


def wgrad_body(left_ref, right_ref, *rest):
    out_ref = rest[-1]
    out_ref[0] = dot_tn(left_ref[...], right_ref[...]).astype(BF16)


def weight_grad(left, right, into, layer, n_layers, bm, bn):
    seq, rows = left.shape
    cols = right.shape[1]
    shape = jax.ShapeDtypeStruct((n_layers, rows, cols), BF16)
    in_specs = [pl.BlockSpec((seq, bm), lambda i, j: (0, i)), pl.BlockSpec((seq, bn), lambda i, j: (0, j))]
    operands = [left, right]
    aliases = {}
    if into is not None:
        in_specs.append(pl.BlockSpec(memory_space=pl.ANY))
        operands.append(into)
        aliases = {2: 0}
    return pl.pallas_call(
        wgrad_body,
        grid=(rows // bm, cols // bn),
        in_specs=in_specs,
        out_specs=pl.BlockSpec((1, bm, bn), lambda i, j: (layer, i, j)),
        out_shape=shape,
        input_output_aliases=aliases,
        compiler_params=pltpu.CompilerParams(dimension_semantics=("arbitrary", "arbitrary"), vmem_limit_bytes=48 * 2 ** 20),
        cost_estimate=pl.CostEstimate(flops=2 * seq * rows * cols, bytes_accessed=2 * (seq * (rows + cols) + rows * cols), transcendentals=0),
        name="wgrad",
    )(*operands)


TILE = 256


def rs_body(n_ops, layer, trans, tp_axis, *refs):
    lhs_hbm = refs[:n_ops]
    rhs_hbm = refs[n_ops:2 * n_ops]
    out_ref = refs[2 * n_ops]
    lhs = refs[2 * n_ops + 1:3 * n_ops + 1]
    rhs = refs[3 * n_ops + 1:4 * n_ops + 1]
    (own, stage, pair_in, diag_in, near_in, far_in, last_out, last_in,
     lhs_sem, rhs_sem, pair_ssem, pair_rsem, diag_ssem, diag_rsem, near_ssem, near_rsem, far_ssem, far_rsem, last_ssem, last_rsem) = refs[4 * n_ops + 1:]
    tiles = own.shape[1]
    rblk = own.shape[2]
    half = tiles * TILE
    rows_out = out_ref.shape[0]

    me = lax.axis_index(tp_axis)
    core = lax.rem(me, 2)
    chip = me // 2
    x = lax.rem(chip, 2)
    y = chip // 2
    partner = chip * 2 + (1 - core)
    chip_x = y * 2 + (1 - x)
    chip_y = (1 - y) * 2 + x
    chip_d = (1 - y) * 2 + (1 - x)
    dev_x = chip_x * 2 + core
    dev_y = chip_y * 2 + core
    near = dev_x * (1 - core) + dev_y * core
    far = dev_y * (1 - core) + dev_x * core
    near_slot = 1 + core
    far_slot = 2 - core
    chips = (chip_d, chip_x, chip_y, chip)

    def row_ds(slot):
        return pl.ds(pl.multiple_of(chips[slot] * rblk, rblk), rblk)

    def own_ds(t):
        return pl.ds(pl.multiple_of(core * half + t * TILE, TILE), TILE)

    def pair_ds(t):
        return pl.ds(pl.multiple_of((1 - core) * half + t * TILE, TILE), TILE)

    def lhs_copy(i, slot):
        return pltpu.make_async_copy(lhs_hbm[i].at[row_ds(slot), :], lhs[i].at[row_ds(slot), :], lhs_sem.at[i, slot])

    def rhs_copy(i, cols, which, t):
        if trans:
            return pltpu.make_async_copy(rhs_hbm[i].at[layer, cols, :], rhs[i].at[cols, :], rhs_sem.at[i, which, t])
        return pltpu.make_async_copy(rhs_hbm[i].at[layer, :, cols], rhs[i].at[:, cols], rhs_sem.at[i, which, t])

    for i in range(n_ops):
        lhs_copy(i, 0).start()
    for t in range(tiles):
        for i in range(n_ops):
            rhs_copy(i, pair_ds(t), 0, t).start()
        for i in range(n_ops):
            rhs_copy(i, own_ds(t), 1, t).start()
    for slot in (1, 2, 3):
        for i in range(n_ops):
            lhs_copy(i, slot).start()

    barrier = pltpu.get_barrier_semaphore()
    for other in (partner, dev_x, dev_y):
        pl.semaphore_signal(barrier, inc=1, device_id={tp_axis: other}, device_id_type=pl.DeviceIdType.MESH)
    pl.semaphore_wait(barrier, 3)

    def product(slot, cols):
        acc = None
        for i in range(n_ops):
            left = lhs[i][row_ds(slot), :]
            part = dot_nt(left, rhs[i][cols, :]) if trans else dot_nn(left, rhs[i][:, cols])
            acc = part if acc is None else acc + part
        return acc

    def remote(src, dst, ssem, rsem, target):
        return pltpu.make_async_remote_copy(src_ref=src, dst_ref=dst, send_sem=ssem, recv_sem=rsem, device_id={tp_axis: target}, device_id_type=pl.DeviceIdType.MESH)

    def pair_copy(slot, t):
        spot = t if slot in (0, 2) else tiles + t
        return remote(stage.at[spot], pair_in.at[slot, t], pair_ssem.at[slot, t], pair_rsem.at[slot, t], partner)

    def pair_wait(slot, t):
        remote(stage.at[t], pair_in.at[slot, t], pair_ssem.at[slot, t], pair_rsem.at[slot, t], partner).wait_recv()

    def diag_copy(t):
        return remote(own.at[0, t], diag_in.at[t], diag_ssem.at[t], diag_rsem.at[t], near)

    def near_copy(t):
        return remote(own.at[near_slot, t], near_in.at[t], near_ssem.at[t], near_rsem.at[t], near)

    def far_copy(t):
        return remote(own.at[far_slot, t], far_in.at[t], far_ssem.at[t], far_rsem.at[t], far)

    def last_copy(t):
        return remote(last_out.at[t], last_in.at[t], last_ssem.at[t], last_rsem.at[t], partner)

    def emit_pair(slot, t):
        spot = t if slot in (0, 2) else tiles + t
        stage[spot] = product(slot, pair_ds(t))
        pair_copy(slot, t).start()

    for i in range(n_ops):
        lhs_copy(i, 0).wait()

    def finish_diag(t):
        pair_wait(0, t)
        own[0, t] += pair_in[0, t]
        diag_copy(t).start()

    def diag_step(t, carry):
        for i in range(n_ops):
            rhs_copy(i, pair_ds(t), 0, t).wait()
        emit_pair(0, t)
        for i in range(n_ops):
            rhs_copy(i, own_ds(t), 1, t).wait()
        own[0, t] = product(0, own_ds(t))

        @pl.when(t > 0)
        def _():
            finish_diag(t - 1)
        return carry

    lax.fori_loop(0, tiles, diag_step, 0)
    finish_diag(tiles - 1)

    for slot in (1, 2):
        for i in range(n_ops):
            lhs_copy(i, slot).wait()

    def finish_sides(t):
        pair_wait(near_slot, t)
        own[near_slot, t] += pair_in[near_slot, t]
        near_copy(t).start()
        pair_wait(far_slot, t)
        diag_copy(t).wait_recv()
        own[far_slot, t] += pair_in[far_slot, t] + diag_in[t]
        far_copy(t).start()

    def side_step(t, carry):
        emit_pair(1, t)
        pair_copy(0, t).wait_send()
        emit_pair(2, t)
        own[1, t] = product(1, own_ds(t))
        own[2, t] = product(2, own_ds(t))

        @pl.when(t > 0)
        def _():
            finish_sides(t - 1)
        return carry

    lax.fori_loop(0, tiles, side_step, 0)
    finish_sides(tiles - 1)

    for i in range(n_ops):
        lhs_copy(i, 3).wait()

    def self_step(t, carry):
        pair_copy(1, t).wait_send()
        emit_pair(3, t)
        own[3, t] = product(3, own_ds(t))
        return carry

    lax.fori_loop(0, tiles, self_step, 0)

    def final_step(t, carry):
        pair_wait(3, t)
        near_copy(t).wait_recv()
        own[3, t] += pair_in[3, t] + near_in[t]
        far_copy(t).wait_recv()
        own[3, t] += far_in[t]
        last_out[t] = own[3, t, pl.ds(pl.multiple_of((1 - core) * rows_out, rows_out), rows_out), :]
        last_copy(t).start()
        out_ref[:, own_ds(t)] = own[3, t, pl.ds(pl.multiple_of(core * rows_out, rows_out), rows_out), :]
        return carry

    lax.fori_loop(0, tiles, final_step, 0)

    def close_step(t, carry):
        last_copy(t).wait_recv()
        out_ref[:, pair_ds(t)] = last_in[t]
        pair_copy(2, t).wait_send()
        pair_copy(3, t).wait_send()
        diag_copy(t).wait_send()
        near_copy(t).wait_send()
        far_copy(t).wait_send()
        last_copy(t).wait_send()
        return carry

    lax.fori_loop(0, tiles, close_step, 0)


def matmul_reduce_scatter(lhs_list, rhs_list, layer, trans, tp_axis, tp_size, cid):
    n_ops = len(lhs_list)
    seq = lhs_list[0].shape[0]
    d_model = rhs_list[0].shape[1] if trans else rhs_list[0].shape[2]
    rblk = seq * 2 // tp_size
    tiles = d_model // 2 // TILE
    rows_out = seq // tp_size
    ks = [item.shape[1] for item in lhs_list]
    dma = pltpu.SemaphoreType.DMA
    scratch = [pltpu.VMEM((seq, k), BF16) for k in ks]
    scratch += [pltpu.VMEM((d_model, k) if trans else (k, d_model), BF16) for k in ks]
    scratch += [
        pltpu.VMEM((4, tiles, rblk, TILE), F32),
        pltpu.VMEM((2 * tiles, rblk, TILE), F32),
        pltpu.VMEM((4, tiles, rblk, TILE), F32),
        pltpu.VMEM((tiles, rblk, TILE), F32),
        pltpu.VMEM((tiles, rblk, TILE), F32),
        pltpu.VMEM((tiles, rblk, TILE), F32),
        pltpu.VMEM((tiles, rows_out, TILE), F32),
        pltpu.VMEM((tiles, rows_out, TILE), F32),
        dma((n_ops, 4)), dma((n_ops, 2, tiles)),
        dma((4, tiles)), dma((4, tiles)),
        dma((tiles,)), dma((tiles,)), dma((tiles,)), dma((tiles,)), dma((tiles,)), dma((tiles,)), dma((tiles,)), dma((tiles,)),
    ]
    flops = 2 * seq * d_model * sum(ks)
    return pl.pallas_call(
        functools.partial(rs_body, n_ops, layer, trans, tp_axis),
        in_specs=[pl.BlockSpec(memory_space=pl.ANY)] * (2 * n_ops),
        out_specs=pl.BlockSpec(memory_space=pltpu.VMEM),
        out_shape=jax.ShapeDtypeStruct((rows_out, d_model), F32),
        scratch_shapes=scratch,
        compiler_params=pltpu.CompilerParams(collective_id=cid, has_side_effects=True, vmem_limit_bytes=VMEM_MAX),
        cost_estimate=pl.CostEstimate(flops=flops * 3, bytes_accessed=40 * 2 ** 20, transcendentals=0),
        name="matmul_rs",
    )(*lhs_list, *rhs_list)


def solution(mesh):
    tp_size = mesh.shape['tp']
    row_spec = P(('dp', 'tp'), None)
    col_spec = P(None, None, 'tp')
    inner_spec = P(None, 'tp', None)

    def device_program(x_loc, dy_loc, norm_gain, w_qkv, w_out, w_gate, w_up, w_down):
        n_layers = w_qkv.shape[0]
        heads = w_out.shape[1] // HEAD_DIM
        hcols = heads * HEAD_DIM
        seq = x_loc.shape[0] * tp_size
        cos_tab, sin_tab = rope_tables(seq)
        gather = lambda value: lax.all_gather(value, 'tp', axis=0, tiled=True)
        saved = []
        x_cur = x_loc
        u_full = None
        dy_full = None
        for layer in range(n_layers):
            x_f32 = x_cur.astype(F32)
            u_loc = rms_scale(x_f32, norm_gain[layer]).astype(BF16)
            u_full = gather(u_loc)
            qkv = dot_nn(u_full, w_qkv[layer]).astype(BF16)
            if layer == n_layers - 1:
                qkv, dy_src = lax.optimization_barrier((qkv, dy_loc))
                dy_full = gather(dy_src)
            query, key, attn, lse = attn_forward(qkv, cos_tab, sin_tab, heads)
            gate = dot_nn(u_full, w_gate[layer]).astype(BF16)
            up = dot_nn(u_full, w_up[layer]).astype(BF16)
            saved.append((x_cur, u_loc, query, key, qkv[:, hcols + HEAD_DIM:], attn, lse, gate, up))
            if layer < n_layers - 1:
                hidden = gated(gate.astype(F32), up.astype(F32)).astype(BF16)
                total = matmul_reduce_scatter([attn, hidden], [w_out, w_down], layer, False, 'tp', tp_size, layer)
                x_cur = (x_f32 + total).astype(BF16)

        grads = [None] * 5
        gains = [None] * n_layers
        dy_cur = dy_loc
        for layer in reversed(range(n_layers)):
            x_sav, u_loc, query, key, value, attn, lse, gate, up = saved[layer]
            d_attn = dot_nt(dy_full, w_out[layer]).astype(BF16)
            d_hidden = dot_nt(dy_full, w_down[layer]).astype(BF16)
            hidden_f32, gated_pull = jax.vjp(gated, gate.astype(F32), up.astype(F32))
            hidden = hidden_f32.astype(BF16)
            d_gate_f32, d_up_f32 = gated_pull(d_hidden.astype(F32))
            d_gate = d_gate_f32.astype(BF16)
            d_up = d_up_f32.astype(BF16)
            d_qkv = attn_backward(query, d_attn, lse, key, value, cos_tab, sin_tab, heads)
            total = matmul_reduce_scatter([d_qkv, d_gate, d_up], [w_qkv, w_gate, w_up], layer, True, 'tp', tp_size, n_layers + layer)
            d_normed = total.astype(BF16)
            norm_pull = jax.vjp(rms_scale, x_sav.astype(F32), norm_gain[layer])[1]
            d_x_norm, gains[layer] = norm_pull(d_normed.astype(F32))
            dy_cur = (dy_cur.astype(F32) + d_x_norm).astype(BF16)
            dy_cur, u_full, dy_full, d_qkv, d_gate, d_up, attn, hidden = lax.optimization_barrier((dy_cur, u_full, dy_full, d_qkv, d_gate, d_up, attn, hidden))
            if layer > 0:
                dy_next = gather(dy_cur)
            pairs = [(u_full, d_qkv, 512, d_qkv.shape[1]), (attn, dy_full, hcols, 1024), (u_full, d_gate, 512, d_gate.shape[1]), (u_full, d_up, 512, d_up.shape[1]), (hidden, dy_full, hidden.shape[1], 512)]
            for idx, (left, right, bm, bn) in enumerate(pairs):
                grads[idx] = weight_grad(left, right, grads[idx], layer, n_layers, bm, bn)
            if layer > 0:
                barred = lax.optimization_barrier((dy_next, saved[layer - 1][1], *grads))
                dy_full = barred[0]
                grads = list(barred[2:])
                u_full = gather(barred[1])
        grad_gain = lax.psum(jnp.stack(gains), 'tp')
        return (dy_cur, grad_gain, *grads)

    return jax.shard_map(device_program, mesh=mesh, in_specs=(row_spec, row_spec, P(None, None), col_spec, inner_spec, col_spec, col_spec, inner_spec), out_specs=(row_spec, P('dp', None), P('dp', None, 'tp'), P('dp', 'tp', None), P('dp', None, 'tp'), P('dp', None, 'tp'), P('dp', 'tp', None)), check_vma=False)
```

time: 1930 us -> 1250 us (0.65)
  Pallas kernels: 0 us -> 772 us
  matrix products: 876 us -> 203 us
  waiting for transfers between devices: 771 us -> 173 us
  other arithmetic: 191 us -> 39.5 us
  local copies, waits for them, and re-layouts: 44.4 us -> 13.9 us
    pallas_call x0 -> x26, Pallas kernels: none -> 772 us  [the longest x5 456 us: matmul_reduce_scatter(): pl.pallas_call(functools.partial(rs_body, n_ops, layer, trans, tp_axis),...]
    dot_general x64 -> x15, matrix products: 876 us -> 203 us  [the longest x9 126 us: dot_nn(): lax.dot_general(lhs, rhs, (((1,), (0,)), ((), ())), preferred_element_typ...]
    reduce_scatter x5 -> x0, waiting for transfers between devices: 463 us -> none  [the longest x2 234 us: block_forward(): lax.psum_scatter(block_part, 'tp', scatter_dimension=0, tiled=True)]
    all_gather x9 -> x8, waiting for transfers between devices: 307 us -> 173 us  [device_program(): gather = lambda value: lax.all_gather(value, 'tp', axis=0, tiled=True)]
    another operation x14 -> x1, other arithmetic: 102 us -> 0.76 us  [device_program(): grad_gain = lax.psum(jnp.stack(gains), 'tp')]
    reduce_sum x3 -> x0, other arithmetic: 38.3 us -> none  [block_forward(): jnp.sum(jnp.exp(scores - row_max), axis=-1, keepdims=True)]
  transfers between devices with their start and end apart: 14 -> 8, of which waited for: 11 -> 4; matrix products, arithmetic and copies ran while one was open for 22% -> 7% of each run, Pallas kernels for 0% -> 30%
where the time goes in v1:
time: 1250 us; the launch traced here: 1240 us
  Pallas kernels  772 us (62%)
  matrix products  203 us (16%)
  waiting for transfers between devices  173 us (14%)
  other arithmetic  39.5 us (3%)
  blocking collectives  23.1 us (2%)
  between operations  15.7 us (1%)
  local copies, waits for them, and re-layouts  13.9 us (1%)
    pallas_call x5, Pallas kernels, matmul_reduce_scatter(): pl.pallas_call(functools.partial(rs_body, n_ops, layer, trans, tp_axis),...  456 us
    pallas_call x15, Pallas kernels, weight_grad(): pl.pallas_call(wgrad_body, grid=(rows // bm, cols // bn), in_specs=in_spe...  179 us
    all_gather x8, waiting for transfers between devices, device_program(): gather = lambda value: lax.all_gather(value, 'tp', axis=0, tiled=True)  173 us
    dot_general x9, matrix products, dot_nn(): lax.dot_general(lhs, rhs, (((1,), (0,)), ((), ())), preferred_element_typ...  126 us
    pallas_call x3, Pallas kernels, attn_backward(): pl.pallas_call(functools.partial(attn_bwd_body, heads, blk), grid=(steps,...  77.1 us
    dot_general x6, matrix products, dot_nt(): lax.dot_general(lhs, rhs, (((1,), (1,)), ((), ())), preferred_element_typ...  77 us
    pallas_call x3, Pallas kernels, attn_forward(): pl.pallas_call(functools.partial(attn_fwd_body, heads, blk), grid=(steps,...  59.6 us
  transfers between devices with their start and end apart: 8, of which 4 were waited for; matrix products, arithmetic and copies ran while one was open for 7% of the time, Pallas kernels for 30%

profile of v1, /device:TPU:0, one launch (start us, length us, event | category | flops | bytes accessed | tf_op | source)
XLA Modules:
  0.0 1240.0 jit_solution(14918145245992013453)
XLA Ops:
  7.2 1.6 fusion.116
  9.4 1.6 fusion.136
  11.5 2.7 fusion.103
  14.3 2.9 fusion.130
  17.7 52.4 %all-gather.9.cloned.1.call-done = bf16[1536,3072]{1,0:T(8,128)(2,1)} async-done(((bf16[192,3072]{1,0:T(8,128)(2,1)}), bf16[1536,3072]{1,0:T(8,128)(2,1)}) %all-gather.9.cloned.1.call-update) | async-done | bytes 9437200 | tf_op jit(solution)/shard_map/all_gather | solution.py:475
  70.2 11.2 fusion.87.qkv_ref
  81.5 19.8 %attn_fwd.3 = (bf16[1536,384]{1,0:T(8,128)(2,1)S(1)}, bf16[1536,128]{1,0:T(8,128)(2,1)S(1)}, bf16[1536,384]{1,0:T(8,128)(2,1)S(1)}, f32[1536,128]{1,0:T(8,128)S(1)}) custom-call(bf16[1536,640]{1,0:T(8,128)(2,1)S(1)} %fusion.87.qkv_ref, f32[1536,128]{1,0:T(8,128)S(1)} %get-tuple-element.138.cos_ref, f32[1536,128]{1,0:T(8,128)S(1)} %get-tuple-element.139.sin_ref, ...), custom_call_target="tpu_custom_call" | custom-call | flops 7247757312 | bytes 8388608 | tf_op jit(solution)/shard_map/attn_fwd/pallas_call | solution.py:117
  101.4 13.6 %fusion.60 = bf16[1536,1024]{1,0:T(8,128)(2,1)S(1)} fusion(bf16[1536,3072]{1,0:T(8,128)(2,1)S(1)} %bitcast.121, bf16[3,3072,1024]{2,1,0:T(8,128)(2,1)} %refs_4_.5), kind=kOutput, calls=%fused_computation.95 | convolution fusion | flops 9665249280 | bytes 18874368 | tf_op jit(solution)/shard_map/dot_general | solution.py:44
  115.0 16.6 %fusion = (bf16[1536,1024]{1,0:T(8,128)(2,1)}, bf16[1536,1024]{1,0:T(8,128)(2,1)}) fusion(bf16[1536,1024]{1,0:T(8,128)(2,1)S(1)} %fusion.60, bf16[1536,3072]{1,0:T(8,128)(2,1)S(1)} %bitcast.121, bf16[3,3072,1024]{2,1,0:T(8,128)(2,1)} %refs_5_.5), kind=kOutput, calls=%fused_computation.21 | convolution fusion | flops 9677832192 | bytes 25165824 | tf_op jit(solution)/shard_map/dot_general | solution.py:44
  131.6 88.8 %matmul_rs.5 = f32[192,3072]{1,0:T(8,128)} custom-call(bf16[1536,384]{1,0:T(8,128)(2,1)} %copy-done.9, bf16[1536,1024]{1,0:T(8,128)(2,1)} %get-tuple-element.109.refs_1_.left_ref, bf16[3,384,3072]{2,1,0:T(8,128)(2,1)} %refs_2_.3, bf16[3,1024,3072]{2,1,0:T(8,128)(2,1)} %refs_3_.6), custom_call_target="tpu_custom_call" | custom-call | flops 39862665216 | bytes 41943040 | tf_op jit(solution)/shard_map/matmul_rs/pallas_call | solution.py:451
  220.4 2.5 fusion.119
  224.0 1.4 fusion.102
  225.5 52.7 %all-gather.11.cloned.1.call-done = bf16[1536,3072]{1,0:T(8,128)(2,1)} async-done(((bf16[192,3072]{1,0:T(8,128)(2,1)}), bf16[1536,3072]{1,0:T(8,128)(2,1)}) %all-gather.11.cloned.1.call-update) | async-done | bytes 9437200 | tf_op jit(solution)/shard_map/all_gather | solution.py:475
  278.1 11.6 fusion.90.qkv_ref
  289.9 19.8 %attn_fwd.4 = (bf16[1536,384]{1,0:T(8,128)(2,1)S(1)}, bf16[1536,128]{1,0:T(8,128)(2,1)S(1)}, bf16[1536,384]{1,0:T(8,128)(2,1)S(1)}, f32[1536,128]{1,0:T(8,128)S(1)}) custom-call(bf16[1536,640]{1,0:T(8,128)(2,1)S(1)} %fusion.90.qkv_ref, f32[1536,128]{1,0:T(8,128)S(1)} %copy-done.16, f32[1536,128]{1,0:T(8,128)S(1)} %copy-done.21, ...), custom_call_target="tpu_custom_call" | custom-call | flops 7247757312 | bytes 8388608 | tf_op jit(solution)/shard_map/attn_fwd/pallas_call | solution.py:117
  309.7 13.6 %fusion.66 = bf16[1536,1024]{1,0:T(8,128)(2,1)S(1)} fusion(bf16[1536,3072]{1,0:T(8,128)(2,1)S(1)} %bitcast.123, bf16[3,3072,1024]{2,1,0:T(8,128)(2,1)} %refs_4_.5), kind=kOutput, calls=%fused_computation.97 | convolution fusion | flops 9665249280 | bytes 18874368 | tf_op jit(solution)/shard_map/dot_general | solution.py:44
  323.4 16.6 %fusion.1 = (bf16[1536,1024]{1,0:T(8,128)(2,1)}, bf16[1536,1024]{1,0:T(8,128)(2,1)}) fusion(bf16[1536,1024]{1,0:T(8,128)(2,1)S(1)} %fusion.66, bf16[1536,3072]{1,0:T(8,128)(2,1)S(1)} %bitcast.123, bf16[3,3072,1024]{2,1,0:T(8,128)(2,1)} %refs_5_.5), kind=kOutput, calls=%fused_computation.22 | convolution fusion | flops 9677832192 | bytes 25165824 | tf_op jit(solution)/shard_map/dot_general | solution.py:44
  340.0 88.8 %matmul_rs.6 = f32[192,3072]{1,0:T(8,128)} custom-call(bf16[1536,384]{1,0:T(8,128)(2,1)} %copy-done.11, bf16[1536,1024]{1,0:T(8,128)(2,1)} %get-tuple-element.92.refs_1_.left_ref, bf16[3,384,3072]{2,1,0:T(8,128)(2,1)} %refs_2_.3, bf16[3,1024,3072]{2,1,0:T(8,128)(2,1)} %refs_3_.6), custom_call_target="tpu_custom_call" | custom-call | flops 39862665216 | bytes 41943040 | tf_op jit(solution)/shard_map/matmul_rs/pallas_call | solution.py:451
  428.8 2.5 fusion.114
  432.5 1.4 fusion.104
  434.0 52.7 %all-gather.13.cloned.1.call-done.left_ref = bf16[1536,3072]{1,0:T(8,128)(2,1)} async-done(((bf16[192,3072]{1,0:T(8,128)(2,1)}), bf16[1536,3072]{1,0:T(8,128)(2,1)}) %all-gather.13.cloned.1.call-update) | async-done | bytes 9437200 | tf_op jit(solution)/shard_map/all_gather | solution.py:475
  486.6 11.2 fusion.93.qkv_ref
  498.8 20.0 %attn_fwd.5 = (bf16[1536,384]{1,0:T(8,128)(2,1)S(1)}, bf16[1536,128]{1,0:T(8,128)(2,1)S(1)}, bf16[1536,384]{1,0:T(8,128)(2,1)S(1)}, f32[1536,128]{1,0:T(8,128)S(1)}) custom-call(bf16[1536,640]{1,0:T(8,128)(2,1)S(1)} %fusion.93.qkv_ref, f32[1536,128]{1,0:T(8,128)S(1)} %copy-done.17, f32[1536,128]{1,0:T(8,128)S(1)} %copy-done.22, ...), custom_call_target="tpu_custom_call" | custom-call | flops 7247757312 | bytes 8388608 | tf_op jit(solution)/shard_map/attn_fwd/pallas_call | solution.py:117
  519.8 1.0 copy-done.35
  522.4 13.2 %fusion.78 = bf16[1536,1024]{1,0:T(8,128)(2,1)} fusion(bf16[1536,3072]{1,0:T(8,128)(2,1)S(1)} %bitcast.105, bf16[3,3072,1024]{2,1,0:T(8,128)(2,1)} %refs_4_.5), kind=kOutput, calls=%fused_computation.101 | convolution fusion | flops 9665249280 | bytes 18874368 | tf_op jit(solution)/shard_map/dot_general | solution.py:44
  535.7 15.3 %all-gather.15.cloned.1.call-done.right_ref = bf16[1536,3072]{1,0:T(8,128)(2,1)} async-done(((bf16[192,3072]{1,0:T(8,128)(2,1)}), bf16[1536,3072]{1,0:T(8,128)(2,1)}) %all-gather.15.cloned.1.call-update) | async-done | bytes 9437200 | tf_op jit(solution)/shard_map/all_gather | solution.py:475
  550.9 8.4 convolution_convert_fusion.2.do_ref
  559.4 25.6 %attn_bwd.3.refs_0_.right_ref = bf16[1536,640]{1,0:T(8,128)(2,1)} custom-call(bf16[1536,384]{1,0:T(8,128)(2,1)S(1)} %copy-done.36, bf16[1536,384]{1,0:T(8,128)(2,1)S(1)} %convolution_convert_fusion.2.do_ref, f32[1536,128]{1,0:T(8,128)S(1)} %copy-done.42, bf16[1536,128]{1,0:T(8,128)(2,1)S(1)} %copy-done.48, bf16[1536,128]{1,0:T(8,128)(2,1)S(1)} %copy-done.27, ...), custom_call_target="tpu_custom_call" | custom-call | flops 18119393280 | bytes 10485760 | tf_op jit(solution)/shard_map/attn_bwd/pallas_call | solution.py:193
  585.1 14.7 %fusion.72 = bf16[1536,1024]{1,0:T(8,128)(2,1)S(1)} fusion(bf16[1536,3072]{1,0:T(8,128)(2,1)} %all-gather.15.cloned.1.call-done.right_ref, bf16[3,1024,3072]{2,1,0:T(8,128)(2,1)} %refs_3_.6), kind=kOutput, calls=%fused_computation.99 | convolution fusion | flops 9665249280 | bytes 18874368 | tf_op jit(solution)/shard_map/dot_general | solution.py:36
  599.8 18.0 %fusion.3 = (bf16[1536,1024]{1,0:T(8,128)(2,1)}, bf16[1536,1024]{1,0:T(8,128)(2,1)}, bf16[1536,1024]{1,0:T(8,128)(2,1)}) fusion(bf16[1536,1024]{1,0:T(8,128)(2,1)S(1)} %copy-done.68, bf16[1536,1024]{1,0:T(8,128)(2,1)S(1)} %fusion.72, bf16[1536,3072]{1,0:T(8,128)(2,1)S(1)} %bitcast.107, bf16[3,3072,1024]{2,1,0:T(8,128)(2,1)} %refs_5_.5), kind=kOutput, calls=%fused_computation.24 | convolution fusion | flops 9695133696 | bytes 31457280 | tf_op jit(solution)/shard_map/dot_general | solution.py:44
  617.8 93.0 %matmul_rs.7 = f32[192,3072]{1,0:T(8,128)} custom-call(bf16[1536,640]{1,0:T(8,128)(2,1)} %attn_bwd.3.refs_0_.right_ref, bf16[1536,1024]{1,0:T(8,128)(2,1)} %get-tuple-element.73.refs_1_.right_ref, bf16[1536,1024]{1,0:T(8,128)(2,1)} %get-tuple-element.74.refs_2_.right_ref, bf16[3,3072,640]{2,1,0:T(8,128)(2,1)} %refs_3_.9, bf16[3,3072,1024]{2,1,0:T(8,128)(2,1)} %refs_4_.5, ...), custom_call_target="tpu_custom_call" | custom-call | flops 76101451776 | bytes 41943040 | tf_op jit(solution)/shard_map/matmul_rs/pallas_call | solution.py:451
  710.8 3.9 fusion.105
  715.5 3.1 fusion.109
  718.7 7.9 wgrad.16.rest_0_
  726.6 11.5 wgrad.15.rest_0_
  738.1 13.6 %wgrad.19.rest_0_ = bf16[3,1024,3072]{2,1,0:T(8,128)(2,1)} custom-call(bf16[1536,1024]{1,0:T(8,128)(2,1)S(1)} %copy-done.30, bf16[1536,3072]{1,0:T(8,128)(2,1)} %all-gather.15.cloned.1.call-done.right_ref), custom_call_target="tpu_custom_call" | custom-call | flops 9663676416 | bytes 18874368 | tf_op jit(solution)/shard_map/wgrad/pallas_call | solution.py:222
  751.7 13.5 %wgrad.17.rest_0_ = bf16[3,3072,1024]{2,1,0:T(8,128)(2,1)} custom-call(bf16[1536,3072]{1,0:T(8,128)(2,1)} %all-gather.13.cloned.1.call-done.left_ref, bf16[1536,1024]{1,0:T(8,128)(2,1)S(1)} %copy-done.29), custom_call_target="tpu_custom_call" | custom-call | flops 9663676416 | bytes 18874368 | tf_op jit(solution)/shard_map/wgrad/pallas_call | solution.py:222
  765.2 13.3 %wgrad.18.rest_0_ = bf16[3,3072,1024]{2,1,0:T(8,128)(2,1)} custom-call(bf16[1536,3072]{1,0:T(8,128)(2,1)} %all-gather.13.cloned.1.call-done.left_ref, bf16[1536,1024]{1,0:T(8,128)(2,1)S(1)} %copy-done.28), custom_call_target="tpu_custom_call" | custom-call | flops 9663676416 | bytes 18874368 | tf_op jit(solution)/shard_map/wgrad/pallas_call | solution.py:222
  778.6 1.0 slice.101.v_ref
  779.7 9.0 convolution_convert_fusion.1.do_ref
  788.7 25.8 %attn_bwd.4.refs_0_.right_ref = bf16[1536,640]{1,0:T(8,128)(2,1)} custom-call(bf16[1536,384]{1,0:T(8,128)(2,1)S(1)} %copy-done.34, bf16[1536,384]{1,0:T(8,128)(2,1)S(1)} %convolution_convert_fusion.1.do_ref, f32[1536,128]{1,0:T(8,128)S(1)} %copy-done.40, bf16[1536,128]{1,0:T(8,128)(2,1)S(1)} %copy-done.46, bf16[1536,128]{1,0:T(8,128)(2,1)S(1)} %slice.101.v_ref, ...), custom_call_target="tpu_custom_call" | custom-call | flops 18119393280 | bytes 10485760 | tf_op jit(solution)/shard_map/attn_bwd/pallas_call | solution.py:193
  814.5 18.1 %fusion.4 = (bf16[1536,1024]{1,0:T(8,128)(2,1)}, bf16[1536,1024]{1,0:T(8,128)(2,1)}) fusion(bf16[1536,1024]{1,0:T(8,128)(2,1)} %copy-done.67, bf16[1536,1024]{1,0:T(8,128)(2,1)} %get-tuple-element.137, bf16[1536,3072]{1,0:T(8,128)(2,1)S(1)} %bitcast.103, bf16[3,1024,3072]{2,1,0:T(8,128)(2,1)} %refs_3_.6), kind=kOutput, calls=%fused_computation.25 | convolution fusion | flops 9691987968 | bytes 28311552 | tf_op jit(solution)/shard_map/dot_general | solution.py:36
  832.6 92.1 %matmul_rs.8 = f32[192,3072]{1,0:T(8,128)} custom-call(bf16[1536,640]{1,0:T(8,128)(2,1)} %attn_bwd.4.refs_0_.right_ref, bf16[1536,1024]{1,0:T(8,128)(2,1)} %get-tuple-element.88.refs_1_.right_ref, bf16[1536,1024]{1,0:T(8,128)(2,1)} %get-tuple-element.90.refs_2_.right_ref, bf16[3,3072,640]{2,1,0:T(8,128)(2,1)} %refs_3_.9, bf16[3,3072,1024]{2,1,0:T(8,128)(2,1)} %refs_4_.5, ...), custom_call_target="tpu_custom_call" | custom-call | flops 76101451776 | bytes 41943040 | tf_op jit(solution)/shard_map/matmul_rs/pallas_call | solution.py:451
  924.7 3.9 fusion.106
  929.3 3.5 fusion.111
  932.9 7.9 wgrad.21.rest_0_
  940.8 11.5 wgrad.20.rest_0_
  952.3 13.6 %wgrad.24.rest_0_ = bf16[3,1024,3072]{2,1,0:T(8,128)(2,1)} custom-call(bf16[1536,1024]{1,0:T(8,128)(2,1)S(1)} %copy-done.1, bf16[1536,3072]{1,0:T(8,128)(2,1)} %all-gather.17.cloned.1.call-done.right_ref, bf16[3,1024,3072]{2,1,0:T(8,128)(2,1)} %wgrad.19.rest_0_), custom_call_target="tpu_custom_call", output_to_operand_aliasing={{}: (2, {})} | custom-call | flops 9663676416 | bytes 18874368 | tf_op jit(solution)/shard_map/wgrad/pallas_call | solution.py:222
  965.9 13.5 %wgrad.23.rest_0_ = bf16[3,3072,1024]{2,1,0:T(8,128)(2,1)} custom-call(bf16[1536,3072]{1,0:T(8,128)(2,1)} %all-gather.19.cloned.1.call-done.left_ref, bf16[1536,1024]{1,0:T(8,128)(2,1)S(1)} %copy-done.3, bf16[3,3072,1024]{2,1,0:T(8,128)(2,1)} %wgrad.18.rest_0_), custom_call_target="tpu_custom_call", output_to_operand_aliasing={{}: (2, {})} | custom-call | flops 9663676416 | bytes 18874368 | tf_op jit(solution)/shard_map/wgrad/pallas_call | solution.py:222
  979.4 13.4 %wgrad.22.rest_0_ = bf16[3,3072,1024]{2,1,0:T(8,128)(2,1)} custom-call(bf16[1536,3072]{1,0:T(8,128)(2,1)} %all-gather.19.cloned.1.call-done.left_ref, bf16[1536,1024]{1,0:T(8,128)(2,1)S(1)} %copy-done.2, bf16[3,3072,1024]{2,1,0:T(8,128)(2,1)} %wgrad.17.rest_0_), custom_call_target="tpu_custom_call", output_to_operand_aliasing={{}: (2, {})} | custom-call | flops 9663676416 | bytes 18874368 | tf_op jit(solution)/shard_map/wgrad/pallas_call | solution.py:222
  992.8 1.0 slice.102.v_ref
  993.9 8.5 convolution_convert_fusion.do_ref
  1002.5 25.7 %attn_bwd.5.refs_0_.right_ref = bf16[1536,640]{1,0:T(8,128)(2,1)} custom-call(bf16[1536,384]{1,0:T(8,128)(2,1)S(1)} %copy-done.32, bf16[1536,384]{1,0:T(8,128)(2,1)S(1)} %convolution_convert_fusion.do_ref, f32[1536,128]{1,0:T(8,128)S(1)} %copy-done.38, bf16[1536,128]{1,0:T(8,128)(2,1)S(1)} %copy-done.44, bf16[1536,128]{1,0:T(8,128)(2,1)S(1)} %slice.102.v_ref, ...), custom_call_target="tpu_custom_call" | custom-call | flops 18119393280 | bytes 10485760 | tf_op jit(solution)/shard_map/attn_bwd/pallas_call | solution.py:193
  1028.2 18.4 %fusion.5 = (bf16[1536,1024]{1,0:T(8,128)(2,1)}, bf16[1536,1024]{1,0:T(8,128)(2,1)}) fusion(bf16[1536,1024]{1,0:T(8,128)(2,1)} %copy-done.66, bf16[1536,1024]{1,0:T(8,128)(2,1)} %get-tuple-element.135, bf16[1536,3072]{1,0:T(8,128)(2,1)S(1)} %bitcast.101, bf16[3,1024,3072]{2,1,0:T(8,128)(2,1)} %refs_3_.6), kind=kOutput, calls=%fused_computation.26 | convolution fusion | flops 9691987968 | bytes 28311552 | tf_op jit(solution)/shard_map/dot_general | solution.py:36
  1046.5 93.1 %matmul_rs.9 = f32[192,3072]{1,0:T(8,128)} custom-call(bf16[1536,640]{1,0:T(8,128)(2,1)} %attn_bwd.5.refs_0_.right_ref, bf16[1536,1024]{1,0:T(8,128)(2,1)} %get-tuple-element.105.refs_1_.right_ref, bf16[1536,1024]{1,0:T(8,128)(2,1)} %get-tuple-element.107.refs_2_.right_ref, bf16[3,3072,640]{2,1,0:T(8,128)(2,1)} %refs_3_.9, bf16[3,3072,1024]{2,1,0:T(8,128)(2,1)} %refs_4_.5, ...), custom_call_target="tpu_custom_call" | custom-call | flops 76101451776 | bytes 41943040 | tf_op jit(solution)/shard_map/matmul_rs/pallas_call | solution.py:451
  1139.7 3.3 fusion.107
  1143.8 23.1 %psum.7 = f32[3,3072]{1,0:T(4,128)} all-reduce(f32[3,3072]{1,0:T(4,128)S(1)} %pad_maximum_fusion.2), channel_id=1, replica_groups=mesh['dp'=1,'tp'=8] {'tp'}, use_global_device_ids=true, to_apply=%region_9.10 | all-reduce | flops 9216 | bytes 73728 | tf_op jit(solution)/shard_map/psum | solution.py:526
  1167.6 3.5 fusion.113
  1171.0 2.0 copy-done.5
  1173.1 13.4 %wgrad.28 = bf16[3,3072,1024]{2,1,0:T(8,128)(2,1)} custom-call(bf16[1536,3072]{1,0:T(8,128)(2,1)} %all-gather.23.cloned.1.call-done.left_ref, bf16[1536,1024]{1,0:T(8,128)(2,1)S(1)} %copy-done.5, bf16[3,3072,1024]{2,1,0:T(8,128)(2,1)} %wgrad.23.rest_0_), custom_call_target="tpu_custom_call", output_to_operand_aliasing={{}: (2, {})} | custom-call | flops 9663676416 | bytes 18874368 | tf_op jit(solution)/shard_map/wgrad/pallas_call | solution.py:222
  1186.4 13.5 %wgrad.27 = bf16[3,3072,1024]{2,1,0:T(8,128)(2,1)} custom-call(bf16[1536,3072]{1,0:T(8,128)(2,1)} %all-gather.23.cloned.1.call-done.left_ref, bf16[1536,1024]{1,0:T(8,128)(2,1)S(1)} %copy-done.4, bf16[3,3072,1024]{2,1,0:T(8,128)(2,1)} %wgrad.22.rest_0_), custom_call_target="tpu_custom_call", output_to_operand_aliasing={{}: (2, {})} | custom-call | flops 9663676416 | bytes 18874368 | tf_op jit(solution)/shard_map/wgrad/pallas_call | solution.py:222
  1200.0 13.5 %wgrad.29 = bf16[3,1024,3072]{2,1,0:T(8,128)(2,1)} custom-call(bf16[1536,1024]{1,0:T(8,128)(2,1)S(1)} %copy-done, bf16[1536,3072]{1,0:T(8,128)(2,1)} %all-gather.21.cloned.1.call-done.right_ref, bf16[3,1024,3072]{2,1,0:T(8,128)(2,1)} %wgrad.24.rest_0_), custom_call_target="tpu_custom_call", output_to_operand_aliasing={{}: (2, {})} | custom-call | flops 9663676416 | bytes 18874368 | tf_op jit(solution)/shard_map/wgrad/pallas_call | solution.py:222
  1213.5 7.9 wgrad.26
  1221.4 11.3 wgrad.25
  (211 shorter events, 11.2 us)
Async XLA Ops:
  7.2 63.0 %all-gather.9.cloned.1.call-start = ((), (), s32[]{:S(2)}) async-start(), calls=%async_computation | async-start | bytes 10616832 | tf_op jit(solution)/shard_map/all_gather | solution.py:475
  14.2 263.9 %all-gather.11.cloned.1.call-start = ((), (), s32[]{:S(2)}) async-start(), calls=%async_computation.1 | async-start | bytes 10616832 | tf_op jit(solution)/shard_map/all_gather | solution.py:475
  17.7 63.7 %copy-start.15 = (f32[1536,128]{1,0:T(8,128)}, f32[1536,128]{1,0:T(8,128)S(1)}, u32[]{:S(2)}) copy-start(f32[1536,128]{1,0:T(8,128)S(1)} %get-tuple-element.138.cos_ref) | copy-start | bytes 2359300
  17.7 63.7 %copy-start.20 = (f32[1536,128]{1,0:T(8,128)}, f32[1536,128]{1,0:T(8,128)S(1)}, u32[]{:S(2)}) copy-start(f32[1536,128]{1,0:T(8,128)S(1)} %get-tuple-element.139.sin_ref) | copy-start | bytes 2359300
  81.4 19.9 %copy-start.25 = (bf16[1536,640]{1,0:T(8,128)(2,1)}, bf16[1536,640]{1,0:T(8,128)(2,1)S(1)}, u32[]{:S(2)}) copy-start(bf16[1536,640]{1,0:T(8,128)(2,1)S(1)} %fusion.87.qkv_ref) | copy-start | bytes 5898244
  81.4 19.9 %slice-start.12 = ((s8[9437184]{0:T(1024)(128)(4,1)}), s8[4194304]{0:T(1024)(128)(4,1)S(1)}, s32[]{:S(2)}) async-start(s8[9437184]{0:T(1024)(128)(4,1)} %bitcast.120), calls=%async_computation.20 | async-start | bytes 8388608
  81.5 19.8 %slice-start.13 = ((s8[9437184]{0:T(1024)(128)(4,1)}), s8[4194304]{0:T(1024)(128)(4,1)S(1)}, s32[]{:S(2)}) async-start(s8[9437184]{0:T(1024)(128)(4,1)} %bitcast.120), calls=%async_computation.21 | async-start | bytes 8388608
  81.5 19.8 %slice-start.14 = ((s8[9437184]{0:T(1024)(128)(4,1)}), s8[1048576]{0:T(1024)(128)(4,1)S(1)}, s32[]{:S(2)}) async-start(s8[9437184]{0:T(1024)(128)(4,1)} %bitcast.120), calls=%async_computation.22 | async-start | bytes 2097152
  101.3 13.6 %copy-start.9 = (bf16[1536,384]{1,0:T(8,128)(2,1)}, bf16[1536,384]{1,0:T(8,128)(2,1)S(1)}, u32[]{:S(2)}) copy-start(bf16[1536,384]{1,0:T(8,128)(2,1)S(1)} %get-tuple-element.102.refs_0_.left_ref) | copy-start | bytes 3538948
  101.3 13.6 %copy-start.31 = (bf16[1536,384]{1,0:T(8,128)(2,1)}, bf16[1536,384]{1,0:T(8,128)(2,1)S(1)}, u32[]{:S(2)}) copy-start(bf16[1536,384]{1,0:T(8,128)(2,1)S(1)} %get-tuple-element.81.q_ref) | copy-start | bytes 3538948
  101.3 13.6 %copy-start.37 = (f32[1536,128]{1,0:T(8,128)}, f32[1536,128]{1,0:T(8,128)S(1)}, u32[]{:S(2)}) copy-start(f32[1536,128]{1,0:T(8,128)S(1)} %get-tuple-element.95.lse_ref) | copy-start | bytes 2359300
  101.4 13.6 %copy-start.43 = (bf16[1536,128]{1,0:T(8,128)(2,1)}, bf16[1536,128]{1,0:T(8,128)(2,1)S(1)}, u32[]{:S(2)}) copy-start(bf16[1536,128]{1,0:T(8,128)(2,1)S(1)} %get-tuple-element.96.k_ref) | copy-start | bytes 1179652
  115.0 16.6 %copy-start.66 = (bf16[1536,1024]{1,0:T(8,128)(2,1)}, bf16[1536,1024]{1,0:T(8,128)(2,1)S(1)}, u32[]{:S(2)}) copy-start(bf16[1536,1024]{1,0:T(8,128)(2,1)S(1)} %fusion.60) | copy-start | bytes 9437188
  225.4 64.4 %copy-start.16 = (f32[1536,128]{1,0:T(8,128)S(1)}, f32[1536,128]{1,0:T(8,128)}, u32[]{:S(2)}) copy-start(f32[1536,128]{1,0:T(8,128)} %copy-done.15) | copy-start | bytes 2359300
  225.4 64.4 %copy-start.21 = (f32[1536,128]{1,0:T(8,128)S(1)}, f32[1536,128]{1,0:T(8,128)}, u32[]{:S(2)}) copy-start(f32[1536,128]{1,0:T(8,128)} %copy-done.20) | copy-start | bytes 2359300
  225.4 261.2 %all-gather.13.cloned.1.call-start = ((), (), s32[]{:S(2)}) async-start(), calls=%async_computation.2 | async-start | bytes 10616832 | tf_op jit(solution)/shard_map/all_gather | solution.py:475
  289.7 19.9 %copy-start.26 = (bf16[1536,640]{1,0:T(8,128)(2,1)}, bf16[1536,640]{1,0:T(8,128)(2,1)S(1)}, u32[]{:S(2)}) copy-start(bf16[1536,640]{1,0:T(8,128)(2,1)S(1)} %fusion.90.qkv_ref) | copy-start | bytes 5898244
  289.8 19.9 %slice-start.15 = ((s8[9437184]{0:T(1024)(128)(4,1)}), s8[4194304]{0:T(1024)(128)(4,1)S(1)}, s32[]{:S(2)}) async-start(s8[9437184]{0:T(1024)(128)(4,1)} %bitcast.122), calls=%async_computation.23 | async-start | bytes 8388608
  289.8 19.8 %slice-start.16 = ((s8[9437184]{0:T(1024)(128)(4,1)}), s8[4194304]{0:T(1024)(128)(4,1)S(1)}, s32[]{:S(2)}) async-start(s8[9437184]{0:T(1024)(128)(4,1)} %bitcast.122), calls=%async_computation.24 | async-start | bytes 8388608
  289.9 19.8 %slice-start.17 = ((s8[9437184]{0:T(1024)(128)(4,1)}), s8[1048576]{0:T(1024)(128)(4,1)S(1)}, s32[]{:S(2)}) async-start(s8[9437184]{0:T(1024)(128)(4,1)} %bitcast.122), calls=%async_computation.25 | async-start | bytes 2097152
  309.7 13.6 %copy-start.11 = (bf16[1536,384]{1,0:T(8,128)(2,1)}, bf16[1536,384]{1,0:T(8,128)(2,1)S(1)}, u32[]{:S(2)}) copy-start(bf16[1536,384]{1,0:T(8,128)(2,1)S(1)} %get-tuple-element.85.refs_0_.left_ref) | copy-start | bytes 3538948
  309.7 13.6 %copy-start.33 = (bf16[1536,384]{1,0:T(8,128)(2,1)}, bf16[1536,384]{1,0:T(8,128)(2,1)S(1)}, u32[]{:S(2)}) copy-start(bf16[1536,384]{1,0:T(8,128)(2,1)S(1)} %get-tuple-element.68.q_ref) | copy-start | bytes 3538948
  309.7 13.6 %copy-start.39 = (f32[1536,128]{1,0:T(8,128)}, f32[1536,128]{1,0:T(8,128)S(1)}, u32[]{:S(2)}) copy-start(f32[1536,128]{1,0:T(8,128)S(1)} %get-tuple-element.77.lse_ref) | copy-start | bytes 2359300
  309.7 13.6 %copy-start.45 = (bf16[1536,128]{1,0:T(8,128)(2,1)}, bf16[1536,128]{1,0:T(8,128)(2,1)S(1)}, u32[]{:S(2)}) copy-start(bf16[1536,128]{1,0:T(8,128)(2,1)S(1)} %get-tuple-element.78.k_ref) | copy-start | bytes 1179652
  323.3 16.7 %copy-start.67 = (bf16[1536,1024]{1,0:T(8,128)(2,1)}, bf16[1536,1024]{1,0:T(8,128)(2,1)S(1)}, u32[]{:S(2)}) copy-start(bf16[1536,1024]{1,0:T(8,128)(2,1)S(1)} %fusion.66) | copy-start | bytes 9437188
  433.9 64.9 %copy-start.17 = (f32[1536,128]{1,0:T(8,128)S(1)}, f32[1536,128]{1,0:T(8,128)}, u32[]{:S(2)}) copy-start(f32[1536,128]{1,0:T(8,128)} %copy-done.15) | copy-start | bytes 2359300
  433.9 64.9 %copy-start.22 = (f32[1536,128]{1,0:T(8,128)S(1)}, f32[1536,128]{1,0:T(8,128)}, u32[]{:S(2)}) copy-start(f32[1536,128]{1,0:T(8,128)} %copy-done.20) | copy-start | bytes 2359300
  433.9 117.0 %all-gather.15.cloned.1.call-start = ((), (), s32[]{:S(2)}) async-start(), calls=%async_computation.3 | async-start | bytes 10616832 | tf_op jit(solution)/shard_map/all_gather | solution.py:475
  497.8 280.7 %all-gather.17.cloned.1.call-start = ((), (), s32[]{:S(2)}) async-start(), calls=%async_computation.4 | async-start | bytes 10616832 | tf_op jit(solution)/shard_map/all_gather | solution.py:475
  498.7 23.8 %slice-start.6 = ((s8[9437184]{0:T(1024)(128)(4,1)}), s8[4194304]{0:T(1024)(128)(4,1)S(1)}, s32[]{:S(2)}) async-start(s8[9437184]{0:T(1024)(128)(4,1)} %bitcast.104), calls=%async_computation.14 | async-start | bytes 8388608
  498.8 23.7 %slice-start.7 = ((s8[9437184]{0:T(1024)(128)(4,1)}), s8[4194304]{0:T(1024)(128)(4,1)S(1)}, s32[]{:S(2)}) async-start(s8[9437184]{0:T(1024)(128)(4,1)} %bitcast.104), calls=%async_computation.15 | async-start | bytes 8388608
  498.8 23.7 %slice-start.8 = ((s8[9437184]{0:T(1024)(128)(4,1)}), s8[1048576]{0:T(1024)(128)(4,1)S(1)}, s32[]{:S(2)}) async-start(s8[9437184]{0:T(1024)(128)(4,1)} %bitcast.104), calls=%async_computation.16 | async-start | bytes 2097152
  535.6 23.7 %copy-start.27 = (bf16[1536,128]{1,0:T(8,128)(2,1)S(1)}, bf16[1536,128]{1,0:T(8,128)(2,1)}, u32[]{:S(2)}) copy-start(bf16[1536,128]{1,0:T(8,128)(2,1)} %slice.89.v_ref) | copy-start | bytes 1179652
  535.7 23.7 %copy-start.36 = (bf16[1536,384]{1,0:T(8,128)(2,1)S(1)}, bf16[1536,384]{1,0:T(8,128)(2,1)}, u32[]{:S(2)}) copy-start(bf16[1536,384]{1,0:T(8,128)(2,1)} %copy-done.35) | copy-start | bytes 3538948
  535.7 23.8 %copy-start.48 = (bf16[1536,128]{1,0:T(8,128)(2,1)S(1)}, bf16[1536,128]{1,0:T(8,128)(2,1)}, u32[]{:S(2)}) copy-start(bf16[1536,128]{1,0:T(8,128)(2,1)} %copy-done.47) | copy-start | bytes 1179652
  559.4 40.3 %slice-start.9 = ((s8[9437184]{0:T(1024)(128)(4,1)}), s8[1048576]{0:T(1024)(128)(4,1)S(1)}, s32[]{:S(2)}) async-start(s8[9437184]{0:T(1024)(128)(4,1)} %bitcast.106), calls=%async_computation.17 | async-start | bytes 2097152
  559.4 40.3 %slice-start.10 = ((s8[9437184]{0:T(1024)(128)(4,1)}), s8[4194304]{0:T(1024)(128)(4,1)S(1)}, s32[]{:S(2)}) async-start(s8[9437184]{0:T(1024)(128)(4,1)} %bitcast.106), calls=%async_computation.18 | async-start | bytes 8388608
  585.1 14.7 %slice-start.11 = ((s8[9437184]{0:T(1024)(128)(4,1)}), s8[4194304]{0:T(1024)(128)(4,1)S(1)}, s32[]{:S(2)}) async-start(s8[9437184]{0:T(1024)(128)(4,1)} %bitcast.106), calls=%async_computation.19 | async-start | bytes 8388608
  585.1 14.7 %copy-start.68 = (bf16[1536,1024]{1,0:T(8,128)(2,1)S(1)}, bf16[1536,1024]{1,0:T(8,128)(2,1)}, u32[]{:S(2)}) copy-start(bf16[1536,1024]{1,0:T(8,128)(2,1)} %fusion.78) | copy-start | bytes 9437188
  718.6 214.2 %all-gather.19.cloned.1.call-start = ((), (), s32[]{:S(2)}) async-start(), calls=%async_computation.5 | async-start | bytes 10616832 | tf_op jit(solution)/shard_map/all_gather | solution.py:475
  726.6 11.5 copy-start.30
  738.1 13.6 %copy-start.29 = (bf16[1536,1024]{1,0:T(8,128)(2,1)S(1)}, bf16[1536,1024]{1,0:T(8,128)(2,1)}, u32[]{:S(2)}) copy-start(bf16[1536,1024]{1,0:T(8,128)(2,1)} %get-tuple-element.73.refs_1_.right_ref) | copy-start | bytes 9437188
  751.7 13.5 %copy-start.28 = (bf16[1536,1024]{1,0:T(8,128)(2,1)S(1)}, bf16[1536,1024]{1,0:T(8,128)(2,1)}, u32[]{:S(2)}) copy-start(bf16[1536,1024]{1,0:T(8,128)(2,1)} %get-tuple-element.74.refs_2_.right_ref) | copy-start | bytes 9437188
  778.5 214.2 %all-gather.21.cloned.1.call-start = ((), (), s32[]{:S(2)}) async-start(), calls=%async_computation.6 | async-start | bytes 10616832 | tf_op jit(solution)/shard_map/all_gather | solution.py:475
  779.6 9.1 copy-start.18
  779.6 9.1 copy-start.23
  779.6 9.1 copy-start.34
  779.6 9.1 copy-start.40
  779.7 9.1 copy-start.46
  779.7 34.9 %slice-start.3 = ((s8[9437184]{0:T(1024)(128)(4,1)}), s8[4194304]{0:T(1024)(128)(4,1)S(1)}, s32[]{:S(2)}) async-start(s8[9437184]{0:T(1024)(128)(4,1)} %bitcast.102), calls=%async_computation.11 | async-start | bytes 8388608
  788.7 25.8 %slice-start.4 = ((s8[9437184]{0:T(1024)(128)(4,1)}), s8[4194304]{0:T(1024)(128)(4,1)S(1)}, s32[]{:S(2)}) async-start(s8[9437184]{0:T(1024)(128)(4,1)} %bitcast.102), calls=%async_computation.12 | async-start | bytes 8388608
  788.7 25.8 %slice-start.5 = ((s8[9437184]{0:T(1024)(128)(4,1)}), s8[1048576]{0:T(1024)(128)(4,1)S(1)}, s32[]{:S(2)}) async-start(s8[9437184]{0:T(1024)(128)(4,1)} %bitcast.102), calls=%async_computation.13 | async-start | bytes 2097152
  932.9 238.2 %all-gather.23.cloned.1.call-start = ((), (), s32[]{:S(2)}) async-start(), calls=%async_computation.7 | async-start | bytes 10616832 | tf_op jit(solution)/shard_map/all_gather | solution.py:475
  940.8 11.5 copy-start.1
  952.3 13.6 %copy-start.3 = (bf16[1536,1024]{1,0:T(8,128)(2,1)S(1)}, bf16[1536,1024]{1,0:T(8,128)(2,1)}, u32[]{:S(2)}) copy-start(bf16[1536,1024]{1,0:T(8,128)(2,1)} %get-tuple-element.90.refs_2_.right_ref) | copy-start | bytes 9437188
  965.9 13.5 %copy-start.2 = (bf16[1536,1024]{1,0:T(8,128)(2,1)S(1)}, bf16[1536,1024]{1,0:T(8,128)(2,1)}, u32[]{:S(2)}) copy-start(bf16[1536,1024]{1,0:T(8,128)(2,1)} %get-tuple-element.88.refs_1_.right_ref) | copy-start | bytes 9437188
  993.9 34.3 %slice-start = ((s8[9437184]{0:T(1024)(128)(4,1)}), s8[4194304]{0:T(1024)(128)(4,1)S(1)}, s32[]{:S(2)}) async-start(s8[9437184]{0:T(1024)(128)(4,1)} %bitcast.100), calls=%async_computation.8 | async-start | bytes 8388608
  1002.4 25.7 %slice-start.1 = ((s8[9437184]{0:T(1024)(128)(4,1)}), s8[4194304]{0:T(1024)(128)(4,1)S(1)}, s32[]{:S(2)}) async-start(s8[9437184]{0:T(1024)(128)(4,1)} %bitcast.100), calls=%async_computation.9 | async-start | bytes 8388608
  1002.4 25.7 %slice-start.2 = ((s8[9437184]{0:T(1024)(128)(4,1)}), s8[1048576]{0:T(1024)(128)(4,1)S(1)}, s32[]{:S(2)}) async-start(s8[9437184]{0:T(1024)(128)(4,1)} %bitcast.100), calls=%async_computation.10 | async-start | bytes 2097152
  1139.7 27.9 %copy-start.51 = (bf16[192,3072]{1,0:T(8,128)(2,1)S(1)}, bf16[192,3072]{1,0:T(8,128)(2,1)}, u32[]{:S(2)}) copy-start(bf16[192,3072]{1,0:T(8,128)(2,1)} %param.8) | copy-start | bytes 3538948
  1139.7 27.8 %copy-start.54 = (bf16[192,3072]{1,0:T(8,128)(2,1)S(1)}, bf16[192,3072]{1,0:T(8,128)(2,1)}, u32[]{:S(2)}) copy-start(bf16[192,3072]{1,0:T(8,128)(2,1)} %fusion.111) | copy-start | bytes 3538948
  1171.0 15.4 %copy-start.4 = (bf16[1536,1024]{1,0:T(8,128)(2,1)S(1)}, bf16[1536,1024]{1,0:T(8,128)(2,1)}, u32[]{:S(2)}) copy-start(bf16[1536,1024]{1,0:T(8,128)(2,1)} %get-tuple-element.105.refs_1_.right_ref) | copy-start | bytes 9437188
  1186.4 13.5 %copy-start = (bf16[1536,1024]{1,0:T(8,128)(2,1)S(1)}, bf16[1536,1024]{1,0:T(8,128)(2,1)}, u32[]{:S(2)}) copy-start(bf16[1536,1024]{1,0:T(8,128)(2,1)} %get-tuple-element.109.refs_1_.left_ref) | copy-start | bytes 9437188
  1199.9 13.5 %copy-start.10 = (bf16[1536,384]{1,0:T(8,128)(2,1)S(1)}, bf16[1536,384]{1,0:T(8,128)(2,1)}, u32[]{:S(2)}) copy-start(bf16[1536,384]{1,0:T(8,128)(2,1)} %copy-done.9) | copy-start | bytes 3538948
  (31 other events, 122.1 us)
Sparse Core Ops, SparseCore 0:
  14.3 55.7 all-gather.8
  225.5 52.5 all-gather.10
  434.0 52.5 all-gather.12
  498.0 52.9 all-gather.14
  718.7 52.6 all-gather.16
  778.7 52.6 all-gather.18
  933.0 52.9 all-gather.20
  992.9 52.9 all-gather.22

commit v2 on v1

v2 whole, which is shorter than its diff:
```python
import functools

import jax
import jax.numpy as jnp
from jax import lax
from jax.experimental import pallas as pl
from jax.experimental.pallas import tpu as pltpu
from jax.sharding import PartitionSpec as P

HEAD_DIM = 128
NORM_EPS = 1e-5
ROPE_BASE = 10000.0
BF16 = jnp.bfloat16
F32 = jnp.float32
VMEM_MAX = 67043328


DIAG, XSIDE, YSIDE, SELF = range(4)
HALVES = range(2)
WHOLE = slice(None)


def loop(count, body):
    def step(i, carry):
        body(i)
        return carry

    lax.fori_loop(0, count, step, 0)


def take(refs, count):
    return [next(refs) for _ in range(count)]


def tile_ds(index, size):
    return pl.ds(pl.multiple_of(index * size, size), size)


def rope_tables(seq_len):
    half_dim = HEAD_DIM // 2
    freqs = ROPE_BASE ** (-2.0 * jnp.arange(half_dim, dtype=F32) / HEAD_DIM)
    angles = jnp.arange(seq_len, dtype=F32)[:, None] * freqs[None, :]
    cos, sin = jnp.cos(angles), jnp.sin(angles)
    return jnp.concatenate([cos, cos], axis=1), jnp.concatenate([-sin, sin], axis=1)


def rms_scale(x_f32, gain_row):
    inv_rms = lax.rsqrt(jnp.mean(x_f32 * x_f32, axis=-1, keepdims=True) + NORM_EPS)
    return x_f32 * inv_rms * gain_row


def gated(gate_f32, up_f32):
    return jax.nn.silu(gate_f32) * up_f32


def dot_nt(lhs, rhs):
    return lax.dot_general(lhs, rhs, (((1,), (1,)), ((), ())), preferred_element_type=F32)


def dot_tn(lhs, rhs):
    return lax.dot_general(lhs, rhs, (((0,), (0,)), ((), ())), preferred_element_type=F32)


def dot_nn(lhs, rhs):
    return lax.dot_general(lhs, rhs, (((1,), (0,)), ((), ())), preferred_element_type=F32)


def turn(values, cos_tab, sin_tab):
    return values * cos_tab + pltpu.roll(values, HEAD_DIM // 2, 1) * sin_tab


def ring_ids(tp_axis):
    me = lax.axis_index(tp_axis)
    core = lax.rem(me, 2)
    chip = me // 2
    x = lax.rem(chip, 2)
    y = chip // 2
    chips = ((1 - y) * 2 + (1 - x), y * 2 + (1 - x), (1 - y) * 2 + x, chip)
    partner = chip * 2 + (1 - core)
    dev_x = chips[1] * 2 + core
    dev_y = chips[2] * 2 + core
    near = dev_x * (1 - core) + dev_y * core
    far = dev_y * (1 - core) + dev_x * core
    return core, chips, partner, dev_x, dev_y, near, far


def greet(tp_axis, others):
    barrier = pltpu.get_barrier_semaphore()
    for other in others:
        pl.semaphore_signal(barrier, device_id={tp_axis: other}, device_id_type=pl.DeviceIdType.MESH)
    pl.semaphore_wait(barrier, len(others))


def remote_copy(tp_axis, src, dst, ssem, rsem, target):
    return pltpu.make_async_remote_copy(src_ref=src, dst_ref=dst, send_sem=ssem, recv_sem=rsem, device_id={tp_axis: target}, device_id_type=pl.DeviceIdType.MESH)


class PushGather:
    def __init__(self, tp_axis, src, dst, sems):
        self.tp_axis, self.src, self.dst = tp_axis, src, dst
        self.near_sem, self.far_sem, self.fwd_sem, self.ici_sem, self.pair_ssem, self.pair_rsem, self.own_sem = sems
        self.core, self.chips, self.partner, self.dev_x, self.dev_y, self.near, self.far = ring_ids(tp_axis)
        self.rows = src.shape[0]
        near_chip = self.chips[1] * (1 - self.core) + self.chips[2] * self.core
        far_chip = self.chips[2] * (1 - self.core) + self.chips[1] * self.core
        self.order = (self.chips[3], near_chip, far_chip, self.chips[0])

    def spot(self, chip, core):
        return self.dst.at[pl.ds(pl.multiple_of((chip * 2 + core) * self.rows, self.rows), self.rows), :]

    def remote(self, src, dst, ssem, rsem, target):
        return remote_copy(self.tp_axis, src, dst, ssem, rsem, target)

    def mine(self):
        return self.spot(self.chips[3], self.core)

    def near_copy(self):
        return self.remote(self.src, self.mine(), self.near_sem, self.ici_sem.at[1], self.near)

    def far_copy(self):
        return self.remote(self.src, self.mine(), self.far_sem, self.ici_sem.at[2], self.far)

    def fwd_copy(self):
        block = self.spot(self.order[1], self.core)
        return self.remote(block, block, self.fwd_sem, self.ici_sem.at[3], self.far)

    def pair_copy(self, k):
        block = self.spot(self.order[k], self.core)
        return self.remote(self.src if k == 0 else block, block, self.pair_ssem.at[k], self.pair_rsem.at[self.slot(k)], self.partner)

    def slot(self, k):
        return (0, 2, 1, 3)[k]

    def own_copy(self):
        return pltpu.make_async_copy(self.src, self.mine(), self.own_sem)

    def start(self):
        greet(self.tp_axis, (self.partner, self.dev_x, self.dev_y))
        self.near_copy().start()
        self.far_copy().start()
        self.pair_copy(0).start()
        self.own_copy().start()

    def ici_arrived(self, k):
        block = self.spot(self.order[k], self.core)
        self.remote(self.src, block, self.near_sem, self.ici_sem.at[k], self.near).wait_recv()

    def pass_sides(self):
        self.ici_arrived(1)
        self.fwd_copy().start()
        self.pair_copy(1).start()
        self.ici_arrived(2)
        self.pair_copy(2).start()

    def finish(self):
        self.ici_arrived(3)
        self.pair_copy(3).start()
        self.own_copy().wait()
        self.near_copy().wait_send()
        self.far_copy().wait_send()
        self.fwd_copy().wait_send()
        for k in range(4):
            self.pair_copy(k).wait_send()
            block = self.spot(self.order[k], 1 - self.core)
            self.remote(self.src, block, self.pair_ssem.at[k], self.pair_rsem.at[k], self.partner).wait_recv()


def push_sems():
    dma = pltpu.SemaphoreType.DMA
    return [dma(()), dma(()), dma(()), dma((4,)), dma((4,)), dma((4,)), dma(())]


def fold(values, op):
    acc = values[:, :HEAD_DIM]
    for at in range(HEAD_DIM, values.shape[1], HEAD_DIM):
        acc = op(acc, values[:, at:at + HEAD_DIM])
    return acc


def attn_fwd_body(heads, blk, tp_axis, part, qkv_ref, cos_ref, sin_ref, v_ref, dy_hbm, q_out, k_out, v_out, o_out, lse_out, dy_full, score_buf, k_rot, *sems):
    step = pl.program_id(0)
    width = dy_full.shape[1]
    push = PushGather(tp_axis, dy_hbm.at[:, pl.ds(part * width, width)], dy_full, sems)

    @pl.when(step == 0)
    def _():
        push.start()

    @pl.when(step == pl.num_programs(0) - 1)
    def _():
        push.pass_sides()
    scale = HEAD_DIM ** -0.5
    kcol = heads * HEAD_DIM
    vcol = kcol + HEAD_DIM
    cos_tab, sin_tab = cos_ref[...], sin_ref[...]
    here = tile_ds(step, blk)
    key = turn(qkv_ref[:, kcol:vcol].astype(F32), cos_tab, sin_tab).astype(BF16)
    k_rot[here, :] = key
    k_out[...] = key
    v_out[...] = qkv_ref[:, vcol:]
    parts = []
    for head in range(heads):
        cols = slice(head * HEAD_DIM, (head + 1) * HEAD_DIM)
        part = turn(qkv_ref[:, cols].astype(F32), cos_tab, sin_tab).astype(BF16)
        q_out[:, cols] = part
        parts.append(part)
    query = jnp.concatenate(parts, axis=0)
    rows = heads * blk

    diag = dot_nt(query, key) * scale
    row_id = lax.broadcasted_iota(jnp.int32, (heads, blk, blk), 1).reshape(rows, blk)
    col_id = lax.broadcasted_iota(jnp.int32, (rows, blk), 1)
    diag = jnp.where(row_id >= col_id, diag, -1e30)
    top = fold(diag, jnp.maximum)

    def first(j, top):
        there = tile_ds(j, blk)
        score = dot_nt(query, k_rot[there, :]) * scale
        score_buf[j] = score
        return jnp.maximum(top, fold(score, jnp.maximum))

    top = jnp.max(lax.fori_loop(0, step, first, top), axis=-1, keepdims=True)

    diag = jnp.exp(diag - top)
    total = fold(diag, jnp.add)

    def second(j, total):
        prob = jnp.exp(score_buf[j] - top)
        score_buf[j] = prob
        return total + fold(prob, jnp.add)

    total = jnp.sum(lax.fori_loop(0, step, second, total), axis=-1, keepdims=True)
    inv = 1.0 / total
    acc = dot_nn((diag * inv).astype(BF16), v_ref[here, :])

    def third(j, acc):
        there = tile_ds(j, blk)
        return acc + dot_nn((score_buf[j] * inv).astype(BF16), v_ref[there, :])

    acc = lax.fori_loop(0, step, third, acc)
    lse = top + jnp.log(total)
    lane = lax.broadcasted_iota(jnp.int32, (blk, HEAD_DIM), 1)
    packed = jnp.zeros((blk, HEAD_DIM), F32)
    for head in range(heads):
        rws = slice(head * blk, (head + 1) * blk)
        o_out[:, head * HEAD_DIM:(head + 1) * HEAD_DIM] = acc[rws].astype(BF16)
        packed = jnp.where(lane == head, lse[rws], packed)
    lse_out[...] = packed

    @pl.when(step == pl.num_programs(0) - 1)
    def _():
        push.finish()


def attn_forward(qkv, cos_tab, sin_tab, dy_loc, heads, tp_axis, cid, part, n_parts, blk=384):
    seq, width = qkv.shape
    hcols = heads * HEAD_DIM
    steps = seq // blk
    row = lambda i: (i, 0)
    flops = 4 * heads * seq * seq * HEAD_DIM // 2
    return pl.pallas_call(
        functools.partial(attn_fwd_body, heads, blk, tp_axis, part),
        grid=(steps,),
        in_specs=[pl.BlockSpec((blk, width), row), pl.BlockSpec((blk, HEAD_DIM), row), pl.BlockSpec((blk, HEAD_DIM), row), pl.BlockSpec((seq, HEAD_DIM), lambda i: (0, heads + 1)), pl.BlockSpec(memory_space=pl.ANY)],
        out_specs=[pl.BlockSpec((blk, hcols), row), pl.BlockSpec((blk, HEAD_DIM), row), pl.BlockSpec((blk, HEAD_DIM), row), pl.BlockSpec((blk, hcols), row), pl.BlockSpec((blk, HEAD_DIM), row), pl.BlockSpec(memory_space=pl.ANY)],
        out_shape=[jax.ShapeDtypeStruct((seq, hcols), BF16), jax.ShapeDtypeStruct((seq, HEAD_DIM), BF16), jax.ShapeDtypeStruct((seq, HEAD_DIM), BF16), jax.ShapeDtypeStruct((seq, hcols), BF16), jax.ShapeDtypeStruct((seq, HEAD_DIM), F32), jax.ShapeDtypeStruct((seq, dy_loc.shape[1] // n_parts), BF16)],
        scratch_shapes=[pltpu.VMEM((steps, heads * blk, blk), F32), pltpu.VMEM((seq, HEAD_DIM), BF16)] + push_sems(),
        compiler_params=pltpu.CompilerParams(collective_id=cid, has_side_effects=True, dimension_semantics=("arbitrary",), vmem_limit_bytes=VMEM_MAX),
        cost_estimate=pl.CostEstimate(flops=flops * 4, bytes_accessed=8 * 2 ** 20, transcendentals=heads * seq * seq // 2),
        name="attn_fwd",
    )(qkv, cos_tab, sin_tab, qkv, dy_loc)


def attn_bwd_body(heads, blk, q_ref, do_ref, lse_ref, k_ref, v_ref, cos_ref, sin_ref, out_ref, prob_buf, dprob_buf, dk_acc, dv_acc):
    step = pl.program_id(0)
    scale = HEAD_DIM ** -0.5
    rows = heads * blk
    hcols = heads * HEAD_DIM
    here = tile_ds(step, blk)

    @pl.when(step == 0)
    def _():
        dk_acc[...] = jnp.zeros_like(dk_acc)
        dv_acc[...] = jnp.zeros_like(dv_acc)

    def heads_of(ref):
        return jnp.concatenate([ref[:, h * HEAD_DIM:(h + 1) * HEAD_DIM] for h in range(heads)], axis=0)

    query = heads_of(q_ref)
    d_out = heads_of(do_ref)
    lse = jnp.concatenate([lse_ref[:, h:h + 1] for h in range(heads)], axis=0)
    row_id = lax.broadcasted_iota(jnp.int32, (heads, blk, blk), 1).reshape(rows, blk)
    col_id = lax.broadcasted_iota(jnp.int32, (rows, blk), 1)

    def score_part(j, masked):
        there = tile_ds(j, blk)
        score = dot_nt(query, k_ref[there, :]) * scale
        if masked:
            score = jnp.where(row_id >= col_id, score, -1e30)
        prob = jnp.exp(score - lse)
        d_prob = dot_nt(d_out, v_ref[there, :]).astype(BF16)
        prob_buf[j] = prob
        dprob_buf[j] = d_prob
        dv_acc[there, :] += dot_tn(prob.astype(BF16), d_out)
        return fold(prob * d_prob.astype(F32), jnp.add)

    row_dot = score_part(step, True)
    row_dot = lax.fori_loop(0, step, lambda j, tot: tot + score_part(j, False), row_dot)
    row_dot = jnp.sum(row_dot, axis=-1, keepdims=True)

    def grad_part(j, acc):
        there = tile_ds(j, blk)
        d_score = (prob_buf[j] * (dprob_buf[j].astype(F32) - row_dot) * scale).astype(BF16)
        dk_acc[there, :] += dot_tn(d_score, query)
        return acc + dot_nn(d_score, k_ref[there, :])

    d_query = lax.fori_loop(0, step + 1, grad_part, jnp.zeros((rows, HEAD_DIM), F32))
    cos_tab, sin_tab = cos_ref[here, :], sin_ref[here, :]
    for head in range(heads):
        part = d_query[head * blk:(head + 1) * blk].astype(BF16).astype(F32)
        out_ref[here, head * HEAD_DIM:(head + 1) * HEAD_DIM] = turn(part, cos_tab, -sin_tab).astype(BF16)

    @pl.when(step == pl.num_programs(0) - 1)
    def _():
        d_key = dk_acc[...].astype(BF16).astype(F32)
        out_ref[:, hcols:hcols + HEAD_DIM] = turn(d_key, cos_ref[...], -sin_ref[...]).astype(BF16)
        out_ref[:, hcols + HEAD_DIM:] = dv_acc[...].astype(BF16)


def attn_backward(query, d_attn, lse, key, value, cos_tab, sin_tab, heads, blk=384):
    seq = query.shape[0]
    hcols = heads * HEAD_DIM
    width = hcols + 2 * HEAD_DIM
    steps = seq // blk
    row = lambda i: (i, 0)
    whole = lambda i: (0, 0)
    flops = 10 * heads * seq * seq * HEAD_DIM // 2
    return pl.pallas_call(
        functools.partial(attn_bwd_body, heads, blk),
        grid=(steps,),
        in_specs=[pl.BlockSpec((blk, hcols), row), pl.BlockSpec((blk, hcols), row), pl.BlockSpec((blk, HEAD_DIM), row)] + [pl.BlockSpec((seq, HEAD_DIM), whole)] * 4,
        out_specs=pl.BlockSpec((seq, width), whole),
        out_shape=jax.ShapeDtypeStruct((seq, width), BF16),
        scratch_shapes=[pltpu.VMEM((steps, heads * blk, blk), F32), pltpu.VMEM((steps, heads * blk, blk), BF16), pltpu.VMEM((seq, HEAD_DIM), F32), pltpu.VMEM((seq, HEAD_DIM), F32)],
        compiler_params=pltpu.CompilerParams(dimension_semantics=("arbitrary",), vmem_limit_bytes=VMEM_MAX),
        cost_estimate=pl.CostEstimate(flops=flops * 4, bytes_accessed=10 * 2 ** 20, transcendentals=heads * seq * seq // 2),
        name="attn_bwd",
    )(query, d_attn, lse, key, value, cos_tab, sin_tab)


def dgrad_body(n_parts, *refs):
    parts = refs[:n_parts]
    wo_ref, wd_ref, gate_ref, up_ref, dattn_ref, dgate_ref, dup_ref, hid_ref = refs[n_parts:]

    def product(w_ref, rows):
        acc, at = None, 0
        for part in parts:
            width = part.shape[1]
            term = dot_nt(part[...], w_ref[0, rows, at:at + width])
            acc = term if acc is None else acc + term
            at += width
        return acc.astype(BF16)

    dattn_ref[...] = product(wo_ref, slice(None))
    for t in range(gate_ref.shape[1] // WIDE):
        cols = slice(t * WIDE, (t + 1) * WIDE)
        d_hidden = product(wd_ref, cols)
        hidden, pull = jax.vjp(gated, gate_ref[:, cols].astype(F32), up_ref[:, cols].astype(F32))
        d_gate, d_up = pull(d_hidden.astype(F32))
        hid_ref[:, cols] = hidden.astype(BF16)
        dgate_ref[:, cols] = d_gate.astype(BF16)
        dup_ref[:, cols] = d_up.astype(BF16)


def cotangents(dy_parts, w_out, w_down, gate, up, layer, blk=512):
    seq, fcols = gate.shape
    hcols, d_model = w_out.shape[1:]
    row = lambda i: (i, 0)
    flops = 2 * seq * d_model * (hcols + fcols)
    wide = pl.BlockSpec((blk, fcols), row)
    return pl.pallas_call(
        functools.partial(dgrad_body, len(dy_parts)),
        grid=(seq // blk,),
        in_specs=[pl.BlockSpec((blk, part.shape[1]), row) for part in dy_parts] + [pl.BlockSpec((1, hcols, d_model), lambda i: (layer, 0, 0)), pl.BlockSpec((1, fcols, d_model), lambda i: (layer, 0, 0)), wide, wide],
        out_specs=[pl.BlockSpec((blk, hcols), row), wide, wide, wide],
        out_shape=[jax.ShapeDtypeStruct((seq, hcols), BF16)] + [jax.ShapeDtypeStruct((seq, fcols), BF16)] * 3,
        compiler_params=pltpu.CompilerParams(dimension_semantics=("arbitrary",), vmem_limit_bytes=VMEM_MAX),
        cost_estimate=pl.CostEstimate(flops=flops, bytes_accessed=32 * 2 ** 20, transcendentals=seq * fcols),
        name="cotangents",
    )(*dy_parts, w_out, w_down, gate, up)


def tail_body(n_parts, each, *refs):
    attn_ref, hid_ref = refs[:2]
    parts = refs[2:2 + n_parts]
    q_ref, g_ref, u_ref = refs[2 + n_parts:5 + n_parts]
    q_out, out_out, g_out, u_out, down_out = refs[-5:]
    step = pl.program_id(0)
    for n, part in enumerate(parts):
        @pl.when(step // each == n)
        def _():
            right = part[...]
            out_out[0] = dot_tn(attn_ref[...], right).astype(BF16)
            down_out[0] = dot_tn(hid_ref[...], right).astype(BF16)
    q_out[0] = q_ref[...]
    g_out[0] = g_ref[...]
    u_out[0] = u_ref[...]


def tail_grads(attn, hidden, dy_parts, ready, grads, layer, n_layers, blk=512):
    seq = attn.shape[0]
    width = dy_parts[0].shape[1]
    d_model = width * len(dy_parts)
    each = width // blk
    whole = lambda j: (0, 0)
    hbm = pl.BlockSpec(memory_space=pl.ANY)
    rows = lambda width: pl.BlockSpec((blk, width), lambda j: (j, 0))
    rows_out = lambda width: pl.BlockSpec((1, blk, width), lambda j: (layer, j, 0))
    cols_out = lambda height: pl.BlockSpec((1, height, blk), lambda j: (layer, 0, j))
    part_spec = lambda n: pl.BlockSpec((seq, blk), lambda j: (0, jnp.clip(j - n * each, 0, each - 1)))
    hcols, fcols = attn.shape[1], hidden.shape[1]
    widths = [item.shape[1] for item in ready]
    old = [item for item in grads if item is not None]
    before = 5 + len(dy_parts)
    return pl.pallas_call(
        functools.partial(tail_body, len(dy_parts), each),
        grid=(d_model // blk,),
        in_specs=[pl.BlockSpec((seq, hcols), whole), pl.BlockSpec((seq, fcols), whole)] + [part_spec(n) for n in range(len(dy_parts))] + [rows(w) for w in widths] + [hbm] * len(old),
        out_specs=[rows_out(widths[0]), cols_out(hcols), rows_out(widths[1]), rows_out(widths[2]), cols_out(fcols)],
        out_shape=[jax.ShapeDtypeStruct((n_layers,) + dims, BF16) for dims in ((d_model, widths[0]), (hcols, d_model), (d_model, widths[1]), (d_model, widths[2]), (fcols, d_model))],
        input_output_aliases={before + n: n for n in range(len(old))},
        compiler_params=pltpu.CompilerParams(dimension_semantics=("arbitrary",), vmem_limit_bytes=VMEM_MAX),
        cost_estimate=pl.CostEstimate(flops=2 * seq * d_model * (hcols + fcols), bytes_accessed=60 * 2 ** 20, transcendentals=0),
        name="tail_grads",
    )(attn, hidden, *dy_parts, *ready, *old)


TILE = 256
WIDE = 512
NORM_ROWS = 16


def fill_weight_grads(u_hbm, grads, lhs, rhs, sems):
    load_sem, store_sem = sems
    seq, d_model = u_hbm.shape
    steps = d_model // TILE

    def cols_of(slot):
        return tile_ds(slot, TILE)

    def load(j, slot):
        return pltpu.make_async_copy(u_hbm.at[:, cols_of(j)], rhs[2].at[0:seq, cols_of(slot)], load_sem.at[slot])

    def rows_at(base, slot):
        return pl.ds(pl.multiple_of(base + slot * TILE, TILE), TILE)

    def spots(slot):
        return rhs[0].at[rows_at(seq, slot), :], rhs[1].at[rows_at(seq, slot), :], rhs[1].at[rows_at(seq + 2 * TILE, slot), :]

    def stores(j, slot):
        return [pltpu.make_async_copy(src, dst.at[cols_of(j), :], store_sem.at[slot, n]) for n, (src, dst) in enumerate(zip(spots(slot), grads))]

    load(0, 0).start()

    def step(j):
        slot = lax.rem(j, 2)
        load(j, slot).wait()

        @pl.when(j + 1 < steps)
        def _():
            load(j + 1, 1 - slot).start()

        @pl.when(j >= 2)
        def _():
            for copy in stores(j - 2, slot):
                copy.wait()
        left = rhs[2][0:seq, cols_of(slot)]
        for spot, right in zip(spots(slot), lhs):
            spot[...] = dot_tn(left, right[...]).astype(BF16)
        for copy in stores(j, slot):
            copy.start()

    loop(steps, step)
    for j in (steps - 2, steps - 1):
        for copy in stores(j, j % 2):
            copy.wait()


def rs_body(n_ops, layer, trans, back, tp_axis, *refs):
    refs = iter(refs)
    lhs_hbm = take(refs, n_ops)
    rhs_hbm = take(refs, n_ops)
    if back:
        u_hbm, x_ref, gain_ref, dy_ref, dy_out, gain_out = take(refs, 6)
        grad_hbm = take(refs, n_ops)
    out_ref = next(refs)
    lhs = take(refs, n_ops)
    rhs = take(refs, n_ops)
    (own, stage, pair_in, diag_in, near_in, far_in, last_out, last_in,
     lhs_sem, rhs_sem, pair_ssem, pair_rsem, diag_ssem, diag_rsem, near_ssem, near_rsem, far_ssem, far_rsem, last_ssem, last_rsem) = take(refs, 20)
    fill_sems = list(refs)
    tiles, rblk = own.shape[1:3]
    rows_out = rblk // 2
    core, chips, partner, dev_x, dev_y, near, far = ring_ids(tp_axis)
    other = 1 - core
    near_slot = XSIDE + core
    far_slot = YSIDE - core

    def row_ds(slot):
        return tile_ds(chips[slot], rblk)

    def own_ds(t):
        return tile_ds(core * tiles + t, TILE)

    def pair_ds(t):
        return tile_ds(other * tiles + t, TILE)

    def lhs_copy(i, slot):
        return pltpu.make_async_copy(lhs_hbm[i].at[row_ds(slot), :], lhs[i].at[row_ds(slot), :], lhs_sem.at[i, slot])

    def rhs_copy(i, cols, which, t):
        if trans:
            return pltpu.make_async_copy(rhs_hbm[i].at[layer, cols, :], rhs[i].at[cols, :], rhs_sem.at[i, which, t])
        return pltpu.make_async_copy(rhs_hbm[i].at[layer, :, cols], rhs[i].at[:, cols], rhs_sem.at[i, which, t])

    def pair_load(i, t):
        return rhs_copy(i, pair_ds(t), 0, t)

    def own_load(i, t):
        return rhs_copy(i, own_ds(t), 1, t)

    ops = range(n_ops)
    for i in ops:
        lhs_copy(i, DIAG).start()
    for t in range(tiles):
        for i in ops:
            pair_load(i, t).start()
        for i in ops:
            own_load(i, t).start()
    for slot in (XSIDE, YSIDE, SELF):
        for i in ops:
            lhs_copy(i, slot).start()

    greet(tp_axis, (partner, dev_x, dev_y))

    def product(slot, cols):
        acc = None
        for i in range(n_ops):
            left = lhs[i][row_ds(slot), :]
            part = dot_nt(left, rhs[i][cols, :]) if trans else dot_nn(left, rhs[i][:, cols])
            acc = part if acc is None else acc + part
        return acc

    remote = functools.partial(remote_copy, tp_axis)

    def spot(slot, t):
        return stage.at[t if slot in (DIAG, YSIDE) else tiles + t]

    def pair_copy(slot, t):
        return remote(spot(slot, t), pair_in.at[slot, t], pair_ssem.at[slot, t], pair_rsem.at[slot, t], partner)

    def pair_wait(slot, t):
        remote(stage.at[t], pair_in.at[slot, t], pair_ssem.at[slot, t], pair_rsem.at[slot, t], partner).wait_recv()

    def diag_copy(t):
        return remote(own.at[DIAG, t], diag_in.at[t], diag_ssem.at[t], diag_rsem.at[t], near)

    def near_copy(t):
        return remote(own.at[near_slot, t], near_in.at[t], near_ssem.at[t], near_rsem.at[t], near)

    def far_copy(t):
        return remote(own.at[far_slot, t], far_in.at[t], far_ssem.at[t], far_rsem.at[t], far)

    def last_copy(t):
        return remote(last_out.at[t], last_in.at[t], last_ssem.at[t], last_rsem.at[t], partner)

    def emit_pair(slot, t):
        spot(slot, t)[...] = product(slot, pair_ds(t))
        pair_copy(slot, t).start()

    for i in ops:
        lhs_copy(i, DIAG).wait()

    def finish_diag(t):
        pair_wait(DIAG, t)
        own[DIAG, t] += pair_in[DIAG, t]
        diag_copy(t).start()

    def lagged(finish, t):
        @pl.when(t == 0)
        def _():
            finish(t)

        @pl.when(t > 1)
        def _():
            finish(t - 1)

    def diag_step(t):
        for i in ops:
            pair_load(i, t).wait()
        emit_pair(DIAG, t)
        for i in ops:
            own_load(i, t).wait()
        own[DIAG, t] = product(DIAG, own_ds(t))
        lagged(finish_diag, t)

    loop(tiles, diag_step)
    finish_diag(tiles - 1)

    for slot in (XSIDE, YSIDE):
        for i in ops:
            lhs_copy(i, slot).wait()

    def finish_sides(t):
        pair_wait(near_slot, t)
        own[near_slot, t] += pair_in[near_slot, t]
        near_copy(t).start()
        pair_wait(far_slot, t)
        diag_copy(t).wait_recv()
        own[far_slot, t] += pair_in[far_slot, t] + diag_in[t]
        far_copy(t).start()

    def side_step(t):
        emit_pair(XSIDE, t)
        pair_copy(DIAG, t).wait_send()
        emit_pair(YSIDE, t)
        own[XSIDE, t] = product(XSIDE, own_ds(t))
        own[YSIDE, t] = product(YSIDE, own_ds(t))
        lagged(finish_sides, t)

    loop(tiles, side_step)
    finish_sides(tiles - 1)

    for i in ops:
        lhs_copy(i, SELF).wait()

    def self_step(t):
        pair_copy(XSIDE, t).wait_send()
        emit_pair(SELF, t)
        own[SELF, t] = product(SELF, own_ds(t))

    loop(tiles, self_step)

    if back:
        fill_weight_grads(u_hbm, grad_hbm, lhs, rhs, fill_sems)

    def final_step(t):
        pair_wait(SELF, t)
        near_copy(t).wait_recv()
        own[SELF, t] += pair_in[SELF, t] + near_in[t]
        far_copy(t).wait_recv()
        own[SELF, t] += far_in[t]
        last_out[t] = own[SELF, t, tile_ds(other, rows_out), :]
        last_copy(t).start()
        out_ref[:, own_ds(t)] = own[SELF, t, tile_ds(core, rows_out), :]

    loop(tiles, final_step)

    def close_step(t):
        last_copy(t).wait_recv()
        out_ref[:, pair_ds(t)] = last_in[t]
        for copy in (pair_copy(YSIDE, t), pair_copy(SELF, t), diag_copy(t), near_copy(t), far_copy(t), last_copy(t)):
            copy.wait_send()

    loop(tiles, close_step)

    if back:
        gain = gain_ref[...]
        gain_out[...] = jnp.zeros_like(gain)

        def norm_step(r):
            rows = tile_ds(r, NORM_ROWS)
            pull = jax.vjp(rms_scale, x_ref[rows, :].astype(F32), gain)[1]
            d_x, d_gain = pull(out_ref[rows, :].astype(BF16).astype(F32))
            dy_out[rows, :] = (dy_ref[rows, :].astype(F32) + d_x).astype(BF16)
            gain_out[...] += d_gain

        loop(rows_out // NORM_ROWS, norm_step)


def matmul_reduce_scatter(lhs_list, rhs_list, layer, trans, tp_axis, tp_size, cid, norm=None):
    n_ops = len(lhs_list)
    seq = lhs_list[0].shape[0]
    d_model = rhs_list[0].shape[1] if trans else rhs_list[0].shape[2]
    rblk = seq * 2 // tp_size
    tiles = d_model // 2 // TILE
    rows_out = seq // tp_size
    ks = [item.shape[1] for item in lhs_list]
    dma = pltpu.SemaphoreType.DMA
    scratch = [pltpu.VMEM((seq, k), BF16) for k in ks]
    scratch += [pltpu.VMEM((d_model, k) if trans else (k, d_model), BF16) for k in ks]
    scratch += [
        pltpu.VMEM((4, tiles, rblk, TILE), F32),
        pltpu.VMEM((2 * tiles, rblk, TILE), F32),
        pltpu.VMEM((4, tiles, rblk, TILE), F32),
        pltpu.VMEM((tiles, rblk, TILE), F32),
        pltpu.VMEM((tiles, rblk, TILE), F32),
        pltpu.VMEM((tiles, rblk, TILE), F32),
        pltpu.VMEM((tiles, rows_out, TILE), F32),
        pltpu.VMEM((tiles, rows_out, TILE), F32),
        dma((n_ops, 4)), dma((n_ops, 2, tiles)),
        dma((4, tiles)), dma((4, tiles)),
    ] + [dma((tiles,))] * 8
    flops = 2 * seq * d_model * sum(ks)
    hbm = pl.BlockSpec(memory_space=pl.ANY)
    vmem = pl.BlockSpec(memory_space=pltpu.VMEM)
    operands = list(lhs_list) + list(rhs_list)
    in_specs = [hbm] * len(operands)
    out_specs, out_shape = [vmem], [jax.ShapeDtypeStruct((rows_out, d_model), F32)]
    if norm is not None:
        operands += norm
        in_specs += [hbm] + [vmem] * (len(norm) - 1)
        scratch = [pltpu.VMEM((rows_out, d_model), F32)] + scratch + [dma((2,)), dma((2, 3))]
        out_specs = [vmem] * 2 + [hbm] * n_ops
        out_shape = [jax.ShapeDtypeStruct((rows_out, d_model), BF16), jax.ShapeDtypeStruct((1, d_model), F32)]
        out_shape += [jax.ShapeDtypeStruct((d_model, k), BF16) for k in ks]
    return pl.pallas_call(
        functools.partial(rs_body, n_ops, layer, trans, norm is not None, tp_axis),
        in_specs=in_specs,
        out_specs=out_specs,
        out_shape=out_shape,
        scratch_shapes=scratch,
        compiler_params=pltpu.CompilerParams(collective_id=cid, has_side_effects=True, vmem_limit_bytes=VMEM_MAX),
        cost_estimate=pl.CostEstimate(flops=flops * 3, bytes_accessed=40 * 2 ** 20, transcendentals=0),
        name="matmul_rs",
    )(*operands)


def ag_body(layer, with_total, with_hidden, with_u, tp_axis, *refs):
    refs = iter(refs)
    n_stage = 3 + with_hidden
    n_res = n_stage + with_u
    x_ref = next(refs)
    if with_total:
        total_ref = next(refs)
    gain_ref, wq_hbm, wg_hbm, wu_hbm = take(refs, 4)
    if with_total:
        x_out = next(refs)
    u_out = next(refs)
    res_hbm = take(refs, n_res)
    wq, wg, wu, ubuf = take(refs, 4)
    stage = take(refs, n_stage)
    w_sem, x_ssem, y_ssem, ici_rsem, fwd_ssem, pair_ssem, pair_rsem, out_sem = refs
    piece = ubuf.shape[1]

    core, chips, partner, dev_x, dev_y, near, far = ring_ids(tp_axis)
    qcols = wq.shape[1]
    fcols = wg.shape[1]
    qtiles = [(s, min(WIDE, qcols - s)) for s in range(0, qcols, WIDE)]
    ftiles = fcols // WIDE

    def w_copy(k):
        if k < len(qtiles):
            cols = slice(qtiles[k][0], qtiles[k][0] + qtiles[k][1])
            return pltpu.make_async_copy(wq_hbm.at[layer, :, cols], wq.at[:, cols], w_sem.at[k])
        t, which = divmod(k - len(qtiles), 2)
        cols = slice(t * WIDE, (t + 1) * WIDE)
        src, dst = ((wg_hbm, wg), (wu_hbm, wu))[which]
        return pltpu.make_async_copy(src.at[layer, :, cols], dst.at[:, cols], w_sem.at[k])

    n_w = len(qtiles) + 2 * ftiles
    for k in range(n_w):
        w_copy(k).start()

    def spot(group, cc):
        return group * 2 + cc

    gain = gain_ref[...]
    for half in HALVES:
        rows = tile_ds(half, piece)
        x_f32 = x_ref[rows, :].astype(F32)
        if with_total:
            x_new = (x_f32 + total_ref[rows, :]).astype(BF16)
            x_out[rows, :] = x_new
            x_f32 = x_new.astype(F32)
        u_new = rms_scale(x_f32, gain).astype(BF16)
        u_out[rows, :] = u_new
        ubuf[spot(half, core)] = u_new
    greet(tp_axis, (partner, dev_x, dev_y))

    remote = functools.partial(remote_copy, tp_axis)

    def x_group(half):
        return 2 + 2 * half

    def y_group(half):
        return 3 + 2 * half

    def d_group(half):
        return 6 + half

    def my_piece(group):
        return ubuf.at[spot(group, core)]

    def x_copy(half):
        return remote(my_piece(half), my_piece(x_group(half)), x_ssem.at[half], ici_rsem.at[x_group(half)], dev_x)

    def y_copy(half):
        return remote(my_piece(half), my_piece(y_group(half)), y_ssem.at[half], ici_rsem.at[y_group(half)], dev_y)

    def fwd_copy(half):
        return remote(my_piece(x_group(half) + core), my_piece(d_group(half)), fwd_ssem.at[half], ici_rsem.at[d_group(half)], far)

    def pair_copy(k):
        return remote(my_piece(k), my_piece(k), pair_ssem.at[k], pair_rsem.at[k], partner)

    def pair_arrived(k):
        remote(my_piece(k), ubuf.at[spot(k, 1 - core)], pair_ssem.at[k], pair_rsem.at[k], partner).wait_recv()

    def ici_arrived(k):
        remote(my_piece(0), my_piece(k), x_ssem.at[0], ici_rsem.at[k], dev_x).wait_recv()

    for half in HALVES:
        x_copy(half).start()
        y_copy(half).start()
        pair_copy(half).start()

    def group_rows(k, cc):
        side = lax.rem(k, 2)
        is_own = (k < 2).astype(jnp.int32)
        is_diag = (k >= 6).astype(jnp.int32)
        is_side = 1 - is_own - is_diag
        side_chip = chips[1] * (1 - side) + chips[2] * side
        chip = chips[3] * is_own + chips[0] * is_diag + side_chip * is_side
        half = side * (1 - is_side) + ((k - 2) // 2) * is_side
        return pl.ds(pl.multiple_of(chip * 4 * piece + cc * 2 * piece + half * piece, 32), piece)

    def out_copy(k, cc, n):
        src = ubuf if n == n_stage else stage[n]
        return pltpu.make_async_copy(src.at[spot(k, cc)], res_hbm[n].at[group_rows(k, cc), :], out_sem.at[n, spot(k, cc)])

    def compute(j, first, count):
        four = pl.ds(first, count)
        left = ubuf[four].reshape(count * piece, ubuf.shape[2])
        for n, (start, size) in enumerate(qtiles):
            @pl.when(j == 0)
            def _():
                w_copy(n).wait()
            cols = slice(start, start + size)
            part = dot_nn(left, wq[:, cols]).astype(BF16)
            stage[0][four, :, cols] = part.reshape(count, piece, size)
        for t in range(ftiles):
            @pl.when(j == 0)
            def _():
                w_copy(len(qtiles) + 2 * t).wait()
                w_copy(len(qtiles) + 2 * t + 1).wait()
            cols = slice(t * WIDE, (t + 1) * WIDE)
            gate = dot_nn(left, wg[:, cols]).astype(BF16)
            up = dot_nn(left, wu[:, cols]).astype(BF16)
            stage[1][four, :, cols] = gate.reshape(count, piece, WIDE)
            stage[2][four, :, cols] = up.reshape(count, piece, WIDE)
            if with_hidden:
                hid = gated(gate.astype(F32), up.astype(F32)).astype(BF16)
                stage[3][four, :, cols] = hid.reshape(count, piece, WIDE)
        for n in range(n_res):
            for i in range(count):
                out_copy(first // 2 + i // 2, i % 2, n).start()

    def pass_on(k):
        ici_arrived(k)
        pair_copy(k).start()

    def step(j):
        for half in HALVES:
            @pl.when(j == half + 1)
            def _():
                pass_on(x_group(half))

                @pl.when(core == 0)
                def _():
                    fwd_copy(half).start()
                pass_on(y_group(half))

                @pl.when(core == 1)
                def _():
                    fwd_copy(half).start()
        for half in HALVES:
            pair_arrived(2 * j + half)
        compute(j, 4 * j, 4)

    loop(3, step)

    def diag_step(half):
        k = d_group(half)
        pass_on(k)
        pair_arrived(k)
        compute(k, 2 * k, 2)

    loop(2, diag_step)

    for half in HALVES:
        x_copy(half).wait_send()
        y_copy(half).wait_send()
        fwd_copy(half).wait_send()

    def drain(k):
        pair_copy(k).wait_send()
        for cc in HALVES:
            for n in range(n_res):
                out_copy(k, cc, n).wait()

    loop(8, drain)


def gather_project(x_loc, total, gain_row, w_qkv, w_gate, w_up, layer, with_hidden, with_u, tp_axis, tp_size, cid):
    rows, d_model = x_loc.shape
    seq = rows * tp_size
    piece = rows // 2
    qcols, fcols = w_qkv.shape[2], w_gate.shape[2]
    with_total = total is not None
    vmem = pl.BlockSpec(memory_space=pltpu.VMEM)
    hbm = pl.BlockSpec(memory_space=pl.ANY)
    widths = [qcols, fcols, fcols] + [fcols] * with_hidden + [d_model] * with_u
    stage_widths = widths[:3 + with_hidden]
    n_w = -(-qcols // WIDE) + 2 * (fcols // WIDE)
    dma = pltpu.SemaphoreType.DMA
    local = jax.ShapeDtypeStruct((rows, d_model), BF16)
    return pl.pallas_call(
        functools.partial(ag_body, layer, with_total, with_hidden, with_u, tp_axis),
        in_specs=[vmem] * (2 + with_total) + [hbm] * 3,
        out_specs=[vmem] * (1 + with_total) + [hbm] * len(widths),
        out_shape=[local] * (1 + with_total) + [jax.ShapeDtypeStruct((seq, w), BF16) for w in widths],
        scratch_shapes=[pltpu.VMEM((d_model, qcols), BF16), pltpu.VMEM((d_model, fcols), BF16), pltpu.VMEM((d_model, fcols), BF16), pltpu.VMEM((2 * tp_size, piece, d_model), BF16)]
        + [pltpu.VMEM((2 * tp_size, piece, w), BF16) for w in stage_widths]
        + [dma((n_w,)), dma((2,)), dma((2,)), dma((8,)), dma((2,)), dma((8,)), dma((8,)), dma((len(widths), 16))],
        compiler_params=pltpu.CompilerParams(collective_id=cid, has_side_effects=True, vmem_limit_bytes=VMEM_MAX),
        cost_estimate=pl.CostEstimate(flops=4 * seq * d_model * (qcols + 2 * fcols), bytes_accessed=40 * 2 ** 20, transcendentals=0),
        name="ag_project",
    )(*([x_loc] + ([total] if with_total else []) + [gain_row, w_qkv, w_gate, w_up]))


def gain_body(tp_axis, tp_size, in_ref, out_ref, slots, ssem, rsem):
    me = lax.axis_index(tp_axis)
    barrier = pltpu.get_barrier_semaphore()
    for k in range(1, tp_size):
        pl.semaphore_signal(barrier, inc=1, device_id={tp_axis: lax.rem(me + k, tp_size)}, device_id_type=pl.DeviceIdType.MESH)
    pl.semaphore_wait(barrier, tp_size - 1)
    slots[me] = in_ref[...]
    copies = []
    for k in range(1, tp_size):
        copies.append(pltpu.make_async_remote_copy(src_ref=in_ref, dst_ref=slots.at[me], send_sem=ssem.at[k], recv_sem=rsem.at[k], device_id={tp_axis: lax.rem(me + k, tp_size)}, device_id_type=pl.DeviceIdType.MESH))
        copies[-1].start()
    for k in range(1, tp_size):
        source = lax.rem(me + tp_size - k, tp_size)
        pltpu.make_async_remote_copy(src_ref=in_ref, dst_ref=slots.at[source], send_sem=ssem.at[k], recv_sem=rsem.at[k], device_id={tp_axis: source}, device_id_type=pl.DeviceIdType.MESH).wait_recv()
    total = slots[0]
    for k in range(1, tp_size):
        total = total + slots[k]
    out_ref[...] = total
    for copy in copies:
        copy.wait_send()


def sum_gains(part, tp_axis, tp_size, cid):
    return pl.pallas_call(
        functools.partial(gain_body, tp_axis, tp_size),
        in_specs=[pl.BlockSpec(memory_space=pltpu.VMEM)],
        out_specs=pl.BlockSpec(memory_space=pltpu.VMEM),
        out_shape=jax.ShapeDtypeStruct(part.shape, F32),
        scratch_shapes=[pltpu.VMEM((tp_size,) + part.shape, F32), pltpu.SemaphoreType.DMA((tp_size,)), pltpu.SemaphoreType.DMA((tp_size,))],
        compiler_params=pltpu.CompilerParams(collective_id=cid, has_side_effects=True),
        name="gain_sum",
    )(part)


def solution(mesh):
    tp_size = mesh.shape['tp']
    row_spec = P(('dp', 'tp'), None)
    col_spec = P(None, None, 'tp')
    inner_spec = P(None, 'tp', None)

    def device_program(x_loc, dy_loc, norm_gain, w_qkv, w_out, w_gate, w_up, w_down):
        n_layers = w_qkv.shape[0]
        heads = w_out.shape[1] // HEAD_DIM
        hcols = heads * HEAD_DIM
        seq = x_loc.shape[0] * tp_size
        cos_tab, sin_tab = rope_tables(seq)
        gather = lambda value: lax.all_gather(value, 'tp', axis=0, tiled=True)
        saved = []
        x_cur, total = x_loc, None
        u_full = None
        dy_parts = []
        for layer in range(n_layers):
            last = layer == n_layers - 1
            results = list(gather_project(x_cur, total, norm_gain[layer:layer + 1], w_qkv, w_gate, w_up, layer, not last, last, 'tp', tp_size, 2 * n_layers + layer))
            if total is not None:
                x_cur = results.pop(0)
            u_loc, qkv, gate, up, extra = results
            if last:
                u_full = extra
            query, key, value, attn, lse, dy_part = attn_forward(qkv, cos_tab, sin_tab, dy_loc, heads, 'tp', 3 * n_layers + 1 + layer, layer, n_layers)
            dy_parts.append(dy_part)
            saved.append((x_cur, u_loc, query, key, value, attn, lse, gate, up))
            if not last:
                total, = matmul_reduce_scatter([attn, extra], [w_out, w_down], layer, False, 'tp', tp_size, layer)

        grads = [None] * 5
        gains = [None] * n_layers
        dy_cur = dy_loc
        for layer in reversed(range(n_layers)):
            x_sav, u_loc, query, key, value, attn, lse, gate, up = saved[layer]
            d_attn, d_gate, d_up, hidden = cotangents(dy_parts, w_out, w_down, gate, up, layer)
            d_qkv = attn_backward(query, d_attn, lse, key, value, cos_tab, sin_tab, heads)
            dy_cur, gains[layer], *ready = matmul_reduce_scatter([d_qkv, d_gate, d_up], [w_qkv, w_gate, w_up], layer, True, 'tp', tp_size, n_layers + layer, [u_full, x_sav, norm_gain[layer:layer + 1], dy_cur])
            dy_cur, attn, hidden, *rest = lax.optimization_barrier((dy_cur, attn, hidden, *ready, *dy_parts))
            ready, dy_parts = rest[:3], rest[3:]
            if layer > 0:
                dy_next = gather(dy_cur)
            grads = tail_grads(attn, hidden, dy_parts, ready, grads, layer, n_layers)
            if layer > 0:
                dy_next, u_next, *grads = lax.optimization_barrier((dy_next, saved[layer - 1][1], *grads))
                dy_parts = [dy_next]
                u_full = gather(u_next)
        grad_gain = sum_gains(jnp.concatenate(gains), 'tp', tp_size, 3 * n_layers)
        return (dy_cur, grad_gain, *grads)

    return jax.shard_map(device_program, mesh=mesh, in_specs=(row_spec, row_spec, P(None, None), col_spec, inner_spec, col_spec, col_spec, inner_spec), out_specs=(row_spec, P('dp', None), P('dp', None, 'tp'), P('dp', 'tp', None), P('dp', None, 'tp'), P('dp', None, 'tp'), P('dp', 'tp', None)), check_vma=False)
```

time: 1250 us -> 1050 us (0.84)
  matrix products: 203 us -> 0 us
  Pallas kernels: 772 us -> 951 us
  waiting for transfers between devices: 173 us -> 68.9 us
  other arithmetic: 39.5 us -> 5.98 us
  blocking collectives: 23.1 us -> 0 us
    dot_general x15 -> x0, matrix products: 203 us -> none  [the longest x9 126 us: dot_nn(): lax.dot_general(lhs, rhs, (((1,), (0,)), ((), ())), preferred_element_typ...]
    pallas_call x23 -> x18, Pallas kernels: 695 us -> 882 us  [the longest x5 483 us: matmul_reduce_scatter(): pl.pallas_call(functools.partial(rs_body, n_ops, layer, trans, norm is no...]
    all_gather x8 -> x4, waiting for transfers between devices: 173 us -> 68.8 us  [device_program(): gather = lambda value: lax.all_gather(value, 'tp', axis=0, tiled=True)]
    psum x1 -> x0, blocking collectives: 23.1 us -> none  [device_program(): grad_gain = lax.psum(jnp.stack(gains), 'tp')]
    reduce_sum x6 -> x0, other arithmetic: 17.5 us -> none  [the longest x3 11 us: rms_scale(): return x_f32 * inv_rms * gain_row]
    convert_element_type x6 -> x0, other arithmetic: 15.6 us -> none  [the longest x3 10.1 us: device_program(): dy_cur = (dy_cur.astype(F32) + d_x_norm).astype(BF16)]
  transfers between devices with their start and end apart: 8 -> 4, of which waited for: 4 -> 4; matrix products, arithmetic and copies ran while one was open for 7% -> 0% of each run, Pallas kernels for 30% -> 14%
where the time goes in v2:
time: 1050 us
  Pallas kernels  951 us (91%)
  waiting for transfers between devices  68.9 us (7%)
  between operations  14.1 us (1%)
    pallas_call x5, Pallas kernels, matmul_reduce_scatter(): pl.pallas_call(functools.partial(rs_body, n_ops, layer, trans, norm is no...  483 us
    pallas_call x3, Pallas kernels, gather_project(): pl.pallas_call(functools.partial(ag_body, layer, with_total, with_hidden,...  172 us
    pallas_call x3, Pallas kernels, cotangents(): pl.pallas_call(functools.partial(dgrad_body, len(dy_parts)), grid=(seq //...  75.9 us
    pallas_call x3, Pallas kernels, tail_grads(): pl.pallas_call(functools.partial(tail_body, len(dy_parts), each), grid=(d...  74.2 us
    pallas_call x3, Pallas kernels, attn_backward(): pl.pallas_call(functools.partial(attn_bwd_body, heads, blk), grid=(steps,...  69.8 us
    all_gather x4, waiting for transfers between devices, device_program(): gather = lambda value: lax.all_gather(value, 'tp', axis=0, tiled=True)  68.8 us
    pallas_call x3, Pallas kernels, attn_forward(): pl.pallas_call(functools.partial(attn_fwd_body, heads, blk, tp_axis, part...  68 us
  transfers between devices with their start and end apart: 4, of which 4 were waited for; matrix products, arithmetic and copies ran while one was open for 0% of the time, Pallas kernels for 14%

profile of v2, /device:TPU:0, one launch (start us, length us, event | category | flops | bytes accessed | tf_op | source)
XLA Modules:
  0.0 1045.7 jit_solution(14237040486782925620)
XLA Ops:
  7.2 0.0 all-gather.5.cloned.1.call-start
  7.2 1.6 fusion.3
  8.8 2.9 fusion.2
  11.7 1.6 pad_maximum_fusion
  13.3 58.3 %ag_project.3 = (bf16[192,3072]{1,0:T(8,128)(2,1)}, bf16[1536,640]{1,0:T(8,128)(2,1)}, bf16[1536,1024]{1,0:T(8,128)(2,1)}, bf16[1536,1024]{1,0:T(8,128)(2,1)}, bf16[1536,1024]{1,0:T(8,128)(2,1)}) custom-call(bf16[192,3072]{1,0:T(8,128)(2,1)} %refs_7_.1, f32[1,3072]{1,0:T(1,128)} %get-tuple-element.234.refs_1_.refs_8_, bf16[3,3072,640]{2,1,0:T(8,128)(2,1)} %refs_3_.17, ...), custom_call_target="tpu_custom_call" | custom-call | flops 50734301184 | bytes 41943040 | tf_op jit(solution)/shard_map/ag_project/pallas_call | solution.py:918
  71.6 22.7 %attn_fwd.3 = (bf16[1536,384]{1,0:T(8,128)(2,1)}, bf16[1536,128]{1,0:T(8,128)(2,1)}, bf16[1536,128]{1,0:T(8,128)(2,1)}, bf16[1536,384]{1,0:T(8,128)(2,1)}, f32[1...) custom-call(bf16[1536,640]{1,0:T(8,128)(2,1)} %get-tuple-element.120.qkv_ref.v_ref, f32[1536,128]{1,0:T(8,128)} %get-tuple-element.239.cos_ref, ...), custom_call_target="tpu_custom_call" | custom-call | flops 7247757312 | bytes 8388608 | tf_op jit(solution)/shard_map/attn_fwd/pallas_call | solution.py:261
  94.3 87.5 %matmul_rs.5.refs_1_ = f32[192,3072]{1,0:T(8,128)} custom-call(bf16[1536,384]{1,0:T(8,128)(2,1)} %get-tuple-element.217.refs_0_, bf16[1536,1024]{1,0:T(8,128)(2,1)} %get-tuple-element.123.refs_1_, bf16[3,384,3072]{2,1,0:T(8,128)(2,1)} %refs_1_.3, bf16[3,1024,3072]{2,1,0:T(8,128)(2,1)} %refs_2_.9), custom_call_target="tpu_custom_call" | custom-call | flops 39862665216 | bytes 41943040 | tf_op jit(solution)/shard_map/matmul_rs/pallas_call | solution.py:717
  181.9 56.6 %ag_project.4 = (bf16[192,3072]{1,0:T(8,128)(2,1)}, bf16[192,3072]{1,0:T(8,128)(2,1)}, bf16[1536,640]{1,0:T(8,128)(2,1)}, bf16[1536,1024]{1,0:T(8,128)(2,1)}, bf...) custom-call(bf16[192,3072]{1,0:T(8,128)(2,1)} %refs_7_.1, f32[192,3072]{1,0:T(8,128)} %matmul_rs.5.refs_1_, ...), custom_call_target="tpu_custom_call" | custom-call | flops 50734301184 | bytes 41943040 | tf_op jit(solution)/shard_map/ag_project/pallas_call | solution.py:918
  238.5 22.7 %attn_fwd.4 = (bf16[1536,384]{1,0:T(8,128)(2,1)}, bf16[1536,128]{1,0:T(8,128)(2,1)}, bf16[1536,128]{1,0:T(8,128)(2,1)}, bf16[1536,384]{1,0:T(8,128)(2,1)}, f32[1...) custom-call(bf16[1536,640]{1,0:T(8,128)(2,1)} %get-tuple-element.124.qkv_ref.v_ref, f32[1536,128]{1,0:T(8,128)} %get-tuple-element.239.cos_ref, ...), custom_call_target="tpu_custom_call" | custom-call | flops 7247757312 | bytes 8388608 | tf_op jit(solution)/shard_map/attn_fwd/pallas_call | solution.py:261
  261.2 88.2 %matmul_rs.6.refs_1_ = f32[192,3072]{1,0:T(8,128)} custom-call(bf16[1536,384]{1,0:T(8,128)(2,1)} %get-tuple-element.182.refs_0_, bf16[1536,1024]{1,0:T(8,128)(2,1)} %get-tuple-element.128.refs_1_, bf16[3,384,3072]{2,1,0:T(8,128)(2,1)} %refs_1_.3, bf16[3,1024,3072]{2,1,0:T(8,128)(2,1)} %refs_2_.9), custom_call_target="tpu_custom_call" | custom-call | flops 39862665216 | bytes 41943040 | tf_op jit(solution)/shard_map/matmul_rs/pallas_call | solution.py:717
  349.4 56.7 %ag_project.5 = (bf16[192,3072]{1,0:T(8,128)(2,1)}, bf16[192,3072]{1,0:T(8,128)(2,1)}, bf16[1536,640]{1,0:T(8,128)(2,1)}, bf16[1536,1024]{1,0:T(8,128)(2,1)}, bf...) custom-call(bf16[192,3072]{1,0:T(8,128)(2,1)} %get-tuple-element.126.refs_0_.refs_7_, f32[192,3072]{1,0:T(8,128)} %matmul_rs.6.refs_1_, ...), custom_call_target="tpu_custom_call" | custom-call | flops 50734301184 | bytes 41943040 | tf_op jit(solution)/shard_map/ag_project/pallas_call | solution.py:918
  406.1 22.6 %attn_fwd.5 = (bf16[1536,384]{1,0:T(8,128)(2,1)}, bf16[1536,128]{1,0:T(8,128)(2,1)}, bf16[1536,128]{1,0:T(8,128)(2,1)}, bf16[1536,384]{1,0:T(8,128)(2,1)}, f32[1...) custom-call(bf16[1536,640]{1,0:T(8,128)(2,1)} %get-tuple-element.129.qkv_ref.v_ref, f32[1536,128]{1,0:T(8,128)} %get-tuple-element.239.cos_ref, ...), custom_call_target="tpu_custom_call" | custom-call | flops 7247757312 | bytes 8388608 | tf_op jit(solution)/shard_map/attn_fwd/pallas_call | solution.py:261
  428.7 25.7 %cotangents.3 = (bf16[1536,384]{1,0:T(8,128)(2,1)}, bf16[1536,1024]{1,0:T(8,128)(2,1)}, bf16[1536,1024]{1,0:T(8,128)(2,1)}, bf16[1536,1024]{1,0:T(8,128)(2,1)}) custom-call(bf16[1536,1024]{1,0:T(8,128)(2,1)} %get-tuple-element.154.refs_0_.refs_2_, bf16[1536,1024]{1,0:T(8,128)(2,1)} %get-tuple-element.155.refs_1_.refs_3_, ...), custom_call_target="tpu_custom_call" | custom-call | flops 13287555072 | bytes 33554432 | tf_op jit(solution)/shard_map/cotangents/pallas_call | solution.py:381
  454.4 23.2 %attn_bwd.3.refs_0_ = bf16[1536,640]{1,0:T(8,128)(2,1)} custom-call(bf16[1536,384]{1,0:T(8,128)(2,1)} %get-tuple-element.130.q_ref, bf16[1536,384]{1,0:T(8,128)(2,1)} %get-tuple-element.136.do_ref, f32[1536,128]{1,0:T(8,128)} %get-tuple-element.137.lse_ref, bf16[1536,128]{1,0:T(8,128)(2,1)} %get-tuple-element.138.k_ref, ...), custom_call_target="tpu_custom_call" | custom-call | flops 18119393280 | bytes 10485760 | tf_op jit(solution)/shard_map/attn_bwd/pallas_call | solution.py:338
  477.6 102.0 %matmul_rs.7 = (bf16[192,3072]{1,0:T(8,128)(2,1)}, f32[1,3072]{1,0:T(1,128)}, bf16[3072,640]{1,0:T(8,128)(2,1)}, bf16[3072,1024]{1,0:T(8,128)(2,1)}, bf16[3072,1024]{1,0:T(8,128)(2,1)}) custom-call(bf16[1536,640]{1,0:T(8,128)(2,1)} %attn_bwd.3.refs_0_, bf16[1536,1024]{1,0:T(8,128)(2,1)} %get-tuple-element.140.refs_1_, ...), custom_call_target="tpu_custom_call" | custom-call | flops 76101451776 | bytes 41943040 | tf_op jit(solution)/shard_map/matmul_rs/pallas_call | solution.py:717
  579.7 0.0 all-gather.5.cloned.1.call-update
  579.7 0.0 all-gather.7.cloned.1.call-start
  579.7 25.0 %tail_grads.3 = (bf16[3,3072,640]{2,1,0:T(8,128)(2,1)}, bf16[3,384,3072]{2,1,0:T(8,128)(2,1)}, bf16[3,3072,1024]{2,1,0:T(8,128)(2,1)}, bf16[3,3072,1024]{2,1,0:T(8,128)(2,1)}, bf16[3,1024,3072]{2,1,0:T(8,128)(2,1)}) custom-call(bf16[1536,384]{1,0:T(8,128)(2,1)} %get-tuple-element.152.refs_0_, bf16[1536,1024]{1,0:T(8,128)(2,1)} %get-tuple-element.153.refs_1_, ...), custom_call_target="tpu_custom_call" | custom-call | flops 13287555072 | bytes 62914560 | tf_op jit(solution)/shard_map/tail_grads/pallas_call | solution.py:425
  604.7 28.2 %all-gather.5.cloned.1.call-done.refs_0_.refs_2_ = bf16[1536,3072]{1,0:T(8,128)(2,1)} async-done(((bf16[192,3072]{1,0:T(8,128)(2,1)}), bf16[1536,3072]{1,0:T(8,128)(2,1)}) %all-gather.5.cloned.1.call-update) | async-done | bytes 9437200 | tf_op jit(solution)/shard_map/all_gather | solution.py:978
  632.9 0.0 all-gather.7.cloned.1.call-update
  632.9 0.0 all-gather.9.cloned.1.call-start
  633.0 25.2 %cotangents.4 = (bf16[1536,384]{1,0:T(8,128)(2,1)}, bf16[1536,1024]{1,0:T(8,128)(2,1)}, bf16[1536,1024]{1,0:T(8,128)(2,1)}, bf16[1536,1024]{1,0:T(8,128)(2,1)}) custom-call(bf16[1536,3072]{1,0:T(8,128)(2,1)} %all-gather.5.cloned.1.call-done.refs_0_.refs_2_, bf16[3,384,3072]{2,1,0:T(8,128)(2,1)} %refs_1_.3, bf16[3,1024,3072]{2,1,0:T(8,128)(2,1)} %refs_2_.9, ...), custom_call_target="tpu_custom_call" | custom-call | flops 13287555072 | bytes 33554432 | tf_op jit(solution)/shard_map/cotangents/pallas_call | solution.py:381
  658.2 23.3 %attn_bwd.4.refs_0_ = bf16[1536,640]{1,0:T(8,128)(2,1)} custom-call(bf16[1536,384]{1,0:T(8,128)(2,1)} %get-tuple-element.125.q_ref, bf16[1536,384]{1,0:T(8,128)(2,1)} %get-tuple-element.168.do_ref, f32[1536,128]{1,0:T(8,128)} %get-tuple-element.169.lse_ref, bf16[1536,128]{1,0:T(8,128)(2,1)} %get-tuple-element.170.k_ref, ...), custom_call_target="tpu_custom_call" | custom-call | flops 18119393280 | bytes 10485760 | tf_op jit(solution)/shard_map/attn_bwd/pallas_call | solution.py:338
  681.4 6.2 all-gather.7.cloned.1.call-done.refs_6_
  687.7 103.1 %matmul_rs.8 = (bf16[192,3072]{1,0:T(8,128)(2,1)}, f32[1,3072]{1,0:T(1,128)}, bf16[3072,640]{1,0:T(8,128)(2,1)}, bf16[3072,1024]{1,0:T(8,128)(2,1)}, bf16[3072,1024]{1,0:T(8,128)(2,1)}) custom-call(bf16[1536,640]{1,0:T(8,128)(2,1)} %attn_bwd.4.refs_0_, bf16[1536,1024]{1,0:T(8,128)(2,1)} %get-tuple-element.172.refs_1_, ...), custom_call_target="tpu_custom_call" | custom-call | flops 76101451776 | bytes 41943040 | tf_op jit(solution)/shard_map/matmul_rs/pallas_call | solution.py:717
  790.7 0.0 all-gather.9.cloned.1.call-update
  790.8 0.0 all-gather.11.cloned.1.call-start
  790.8 24.6 %tail_grads.4 = (bf16[3,3072,640]{2,1,0:T(8,128)(2,1)}, bf16[3,384,3072]{2,1,0:T(8,128)(2,1)}, bf16[3,3072,1024]{2,1,0:T(8,128)(2,1)}, bf16[3,3072,1024]{2,1,0:T(8,128)(2,1)}, bf16[3,1024,3072]{2,1,0:T(8,128)(2,1)}) custom-call(bf16[1536,384]{1,0:T(8,128)(2,1)} %get-tuple-element.182.r, ...), custom_call_target="tpu_custom_call", output_to_operand_aliasing={{0}: (6, {}), {1}: (7, {}), {2}: (8, {}), {3}: (9, {}), {4}... | custom-call | flops 13287555072 | bytes 62914560 | tf_op jit(solution)/shard_map/tail_grads/pallas_call | solution.py:425
  815.4 28.1 %all-gather.9.cloned.1.call-done.refs_0_.refs_2_ = bf16[1536,3072]{1,0:T(8,128)(2,1)} async-done(((bf16[192,3072]{1,0:T(8,128)(2,1)}), bf16[1536,3072]{1,0:T(8,128)(2,1)}) %all-gather.9.cloned.1.call-update) | async-done | bytes 9437200 | tf_op jit(solution)/shard_map/all_gather | solution.py:978
  843.5 0.0 all-gather.11.cloned.1.call-update
  843.5 25.1 %cotangents.5 = (bf16[1536,384]{1,0:T(8,128)(2,1)}, bf16[1536,1024]{1,0:T(8,128)(2,1)}, bf16[1536,1024]{1,0:T(8,128)(2,1)}, bf16[1536,1024]{1,0:T(8,128)(2,1)}) custom-call(bf16[1536,3072]{1,0:T(8,128)(2,1)} %all-gather.9.cloned.1.call-done.refs_0_.refs_2_, bf16[3,384,3072]{2,1,0:T(8,128)(2,1)} %refs_1_.3, bf16[3,1024,3072]{2,1,0:T(8,128)(2,1)} %refs_2_.9, ...), custom_call_target="tpu_custom_call" | custom-call | flops 13287555072 | bytes 33554432 | tf_op jit(solution)/shard_map/cotangents/pallas_call | solution.py:381
  868.6 23.2 %attn_bwd.5.refs_0_ = bf16[1536,640]{1,0:T(8,128)(2,1)} custom-call(bf16[1536,384]{1,0:T(8,128)(2,1)} %get-tuple-element.121.q_ref, bf16[1536,384]{1,0:T(8,128)(2,1)} %get-tuple-element.201.do_ref, f32[1536,128]{1,0:T(8,128)} %get-tuple-element.202.lse_ref, bf16[1536,128]{1,0:T(8,128)(2,1)} %get-tuple-element.203.k_ref, ...), custom_call_target="tpu_custom_call" | custom-call | flops 18119393280 | bytes 10485760 | tf_op jit(solution)/shard_map/attn_bwd/pallas_call | solution.py:338
  891.8 6.3 all-gather.11.cloned.1.call-done.refs_6_
  898.1 102.7 %matmul_rs.9 = (bf16[192,3072]{1,0:T(8,128)(2,1)}, f32[1,3072]{1,0:T(1,128)}, bf16[3072,640]{1,0:T(8,128)(2,1)}, bf16[3072,1024]{1,0:T(8,128)(2,1)}, bf16[3072,1024]{1,0:T(8,128)(2,1)}) custom-call(bf16[1536,640]{1,0:T(8,128)(2,1)} %attn_bwd.5.refs_0_, bf16[1536,1024]{1,0:T(8,128)(2,1)} %get-tuple-element.205.refs_1_, ...), custom_call_target="tpu_custom_call" | custom-call | flops 76101451776 | bytes 41943040 | tf_op jit(solution)/shard_map/matmul_rs/pallas_call | solution.py:717
  1000.8 1.4 pad_maximum_fusion.2.in_ref
  1002.2 8.4 gain_sum.1
  1010.6 24.6 %tail_grads.5 = (bf16[3,3072,640]{2,1,0:T(8,128)(2,1)}, bf16[3,384,3072]{2,1,0:T(8,128)(2,1)}, bf16[3,3072,1024]{2,1,0:T(8,128)(2,1)}, bf16[3,3072,1024]{2,1,0:T(8,128)(2,1)}, bf16[3,1024,3072]{2,1,0:T(8,128)(2,1)}) custom-call(bf16[1536,384]{1,0:T(8,128)(2,1)} %get-tuple-element.217.r, ...), custom_call_target="tpu_custom_call", output_to_operand_aliasing={{0}: (6, {}), {1}: (7, {}), {2}: (8, {}), {3}: (9, {}), {4}... | custom-call | flops 13287555072 | bytes 62914560 | tf_op jit(solution)/shard_map/tail_grads/pallas_call | solution.py:425
  1035.2 2.4 copy.37
  1037.5 1.4 copy.38
  (1 shorter events, 0.0 us)
Async XLA Ops:
  7.2 625.7 %all-gather.5.cloned.1.call-start = ((), (), s32[]{:S(2)}) async-start(), calls=%async_computation | async-start | bytes 10616832 | tf_op jit(solution)/shard_map/all_gather | solution.py:978
  579.7 108.0 %all-gather.7.cloned.1.call-start = ((), (), s32[]{:S(2)}) async-start(), calls=%async_computation.1 | async-start | bytes 10616832 | tf_op jit(solution)/shard_map/all_gather | solution.py:978
  632.9 210.6 %all-gather.9.cloned.1.call-start = ((), (), s32[]{:S(2)}) async-start(), calls=%async_computation.2 | async-start | bytes 10616832 | tf_op jit(solution)/shard_map/all_gather | solution.py:978
  790.8 107.3 %all-gather.11.cloned.1.call-start = ((), (), s32[]{:S(2)}) async-start(), calls=%async_computation.3 | async-start | bytes 10616832 | tf_op jit(solution)/shard_map/all_gather | solution.py:978
Sparse Core Ops, SparseCore 0:
  579.8 53.0 all-gather.4
  634.7 52.9 all-gather.6
  790.9 52.5 all-gather.8
  845.1 52.9 all-gather.10

commit v3 on v2

--- a/solution.py
+++ b/solution.py
@@ -2,6 +2,7 @@
 
 import jax
 import jax.numpy as jnp
+import numpy as np
 from jax import lax
 from jax.experimental import pallas as pl
 from jax.experimental.pallas import tpu as pltpu
@@ -38,10 +39,11 @@
 
 def rope_tables(seq_len):
     half_dim = HEAD_DIM // 2
-    freqs = ROPE_BASE ** (-2.0 * jnp.arange(half_dim, dtype=F32) / HEAD_DIM)
-    angles = jnp.arange(seq_len, dtype=F32)[:, None] * freqs[None, :]
-    cos, sin = jnp.cos(angles), jnp.sin(angles)
-    return jnp.concatenate([cos, cos], axis=1), jnp.concatenate([-sin, sin], axis=1)
+    freqs = ROPE_BASE ** (-2.0 * np.arange(half_dim) / HEAD_DIM)
+    angles = np.arange(seq_len)[:, None] * freqs[None, :]
+    cos, sin = np.cos(angles), np.sin(angles)
+    tables = np.concatenate([cos, cos], axis=1), np.concatenate([-sin, sin], axis=1)
+    return [jnp.asarray(table.astype(np.float32)) for table in tables]
 
 
 def rms_scale(x_f32, gain_row):
@@ -95,6 +97,27 @@
     return pltpu.make_async_remote_copy(src_ref=src, dst_ref=dst, send_sem=ssem, recv_sem=rsem, device_id={tp_axis: target}, device_id_type=pl.DeviceIdType.MESH)
 
 
+def sum_over(tp_axis, tp_size, slots, ssem, rsem):
+    me = lax.axis_index(tp_axis)
+    mine = slots.at[me]
+    others = range(1, tp_size)
+
+    def pushed(k):
+        return remote_copy(tp_axis, mine, mine, ssem.at[k], rsem.at[k], lax.rem(me + k, tp_size))
+
+    for k in others:
+        pushed(k).start()
+    for k in others:
+        source = lax.rem(me + tp_size - k, tp_size)
+        remote_copy(tp_axis, mine, slots.at[source], ssem.at[k], rsem.at[k], source).wait_recv()
+    total = slots[0]
+    for k in others:
+        total = total + slots[k]
+    for k in others:
+        pushed(k).wait_send()
+    return total
+
+
 class PushGather:
     def __init__(self, tp_axis, src, dst, sems):
         self.tp_axis, self.src, self.dst = tp_axis, src, dst
@@ -165,9 +188,49 @@
             self.remote(self.src, block, self.pair_ssem.at[k], self.pair_rsem.at[k], self.partner).wait_recv()
 
 
-def push_sems():
-    dma = pltpu.SemaphoreType.DMA
-    return [dma(()), dma(()), dma(()), dma((4,)), dma((4,)), dma((4,)), dma(())]
+    def open(self, step):
+        @pl.when(step == 0)
+        def _():
+            self.start()
+
+        @pl.when(step == pl.num_programs(0) - 1)
+        def _():
+            self.pass_sides()
+
+    def close(self, step):
+        @pl.when(step == pl.num_programs(0) - 1)
+        def _():
+            self.finish()
+
+
+class NoPush:
+    n_refs, specs, shapes, sems, params, operands = 0, [], [], [], {}, []
+
+    def __call__(self, src, dst, sems):
+        return self
+
+    def open(self, step):
+        pass
+
+    close = open
+
+
+class PushOf:
+    n_refs = 1
+
+    def __init__(self, value, part, n_parts, tp_axis, tp_size, cid):
+        self.tp_axis = tp_axis
+        rows, self.width = value.shape[0], value.shape[1] // n_parts
+        self.cols = slice(part * self.width, (part + 1) * self.width)
+        dma = pltpu.SemaphoreType.DMA
+        self.operands = [value]
+        self.specs = [pl.BlockSpec(memory_space=pl.ANY)]
+        self.shapes = [jax.ShapeDtypeStruct((rows * tp_size, self.width), BF16)]
+        self.sems = [dma(())] * 3 + [dma((4,))] * 3 + [dma(())]
+        self.params = {'collective_id': cid, 'has_side_effects': True}
+
+    def __call__(self, src, dst, sems):
+        return PushGather(self.tp_axis, src[0].at[:, self.cols], dst[0], list(sems))
 
 
 def fold(values, op):
@@ -177,18 +240,10 @@
     return acc
 
 
-def attn_fwd_body(heads, blk, tp_axis, part, qkv_ref, cos_ref, sin_ref, v_ref, dy_hbm, q_out, k_out, v_out, o_out, lse_out, dy_full, score_buf, k_rot, *sems):
+def attn_fwd_body(heads, blk, push_of, qkv_ref, cos_ref, sin_ref, v_ref, dy_hbm, q_out, k_out, v_out, o_out, lse_out, dy_full, score_buf, k_rot, *sems):
     step = pl.program_id(0)
-    width = dy_full.shape[1]
-    push = PushGather(tp_axis, dy_hbm.at[:, pl.ds(part * width, width)], dy_full, sems)
-
-    @pl.when(step == 0)
-    def _():
-        push.start()
-
-    @pl.when(step == pl.num_programs(0) - 1)
-    def _():
-        push.pass_sides()
+    push = push_of([dy_hbm], [dy_full], sems)
+    push.open(step)
     scale = HEAD_DIM ** -0.5
     kcol = heads * HEAD_DIM
     vcol = kcol + HEAD_DIM
@@ -246,33 +301,37 @@
         o_out[:, head * HEAD_DIM:(head + 1) * HEAD_DIM] = acc[rws].astype(BF16)
         packed = jnp.where(lane == head, lse[rws], packed)
     lse_out[...] = packed
-
-    @pl.when(step == pl.num_programs(0) - 1)
-    def _():
-        push.finish()
-
-
-def attn_forward(qkv, cos_tab, sin_tab, dy_loc, heads, tp_axis, cid, part, n_parts, blk=384):
+    push.close(step)
+
+
+def attn_forward(qkv, cos_tab, sin_tab, heads, push_of, blk=384):
     seq, width = qkv.shape
     hcols = heads * HEAD_DIM
     steps = seq // blk
     row = lambda i: (i, 0)
     flops = 4 * heads * seq * seq * HEAD_DIM // 2
     return pl.pallas_call(
-        functools.partial(attn_fwd_body, heads, blk, tp_axis, part),
+        functools.partial(attn_fwd_body, heads, blk, push_of),
         grid=(steps,),
-        in_specs=[pl.BlockSpec((blk, width), row), pl.BlockSpec((blk, HEAD_DIM), row), pl.BlockSpec((blk, HEAD_DIM), row), pl.BlockSpec((seq, HEAD_DIM), lambda i: (0, heads + 1)), pl.BlockSpec(memory_space=pl.ANY)],
-        out_specs=[pl.BlockSpec((blk, hcols), row), pl.BlockSpec((blk, HEAD_DIM), row), pl.BlockSpec((blk, HEAD_DIM), row), pl.BlockSpec((blk, hcols), row), pl.BlockSpec((blk, HEAD_DIM), row), pl.BlockSpec(memory_space=pl.ANY)],
-        out_shape=[jax.ShapeDtypeStruct((seq, hcols), BF16), jax.ShapeDtypeStruct((seq, HEAD_DIM), BF16), jax.ShapeDtypeStruct((seq, HEAD_DIM), BF16), jax.ShapeDtypeStruct((seq, hcols), BF16), jax.ShapeDtypeStruct((seq, HEAD_DIM), F32), jax.ShapeDtypeStruct((seq, dy_loc.shape[1] // n_parts), BF16)],
-        scratch_shapes=[pltpu.VMEM((steps, heads * blk, blk), F32), pltpu.VMEM((seq, HEAD_DIM), BF16)] + push_sems(),
-        compiler_params=pltpu.CompilerParams(collective_id=cid, has_side_effects=True, dimension_semantics=("arbitrary",), vmem_limit_bytes=VMEM_MAX),
+        in_specs=[pl.BlockSpec((blk, width), row), pl.BlockSpec((blk, HEAD_DIM), row), pl.BlockSpec((blk, HEAD_DIM), row), pl.BlockSpec((seq, HEAD_DIM), lambda i: (0, heads + 1))] + push_of.specs,
+        out_specs=[pl.BlockSpec((blk, hcols), row), pl.BlockSpec((blk, HEAD_DIM), row), pl.BlockSpec((blk, HEAD_DIM), row), pl.BlockSpec((blk, hcols), row), pl.BlockSpec((blk, HEAD_DIM), row)] + push_of.specs,
+        out_shape=[jax.ShapeDtypeStruct((seq, hcols), BF16), jax.ShapeDtypeStruct((seq, HEAD_DIM), BF16), jax.ShapeDtypeStruct((seq, HEAD_DIM), BF16), jax.ShapeDtypeStruct((seq, hcols), BF16), jax.ShapeDtypeStruct((seq, HEAD_DIM), F32)] + push_of.shapes,
+        scratch_shapes=[pltpu.VMEM((steps, heads * blk, blk), F32), pltpu.VMEM((seq, HEAD_DIM), BF16)] + push_of.sems,
+        compiler_params=pltpu.CompilerParams(**push_of.params, dimension_semantics=("arbitrary",), vmem_limit_bytes=VMEM_MAX),
         cost_estimate=pl.CostEstimate(flops=flops * 4, bytes_accessed=8 * 2 ** 20, transcendentals=heads * seq * seq // 2),
         name="attn_fwd",
-    )(qkv, cos_tab, sin_tab, qkv, dy_loc)
-
-
-def attn_bwd_body(heads, blk, q_ref, do_ref, lse_ref, k_ref, v_ref, cos_ref, sin_ref, out_ref, prob_buf, dprob_buf, dk_acc, dv_acc):
+    )(qkv, cos_tab, sin_tab, qkv, *push_of.operands)
+
+
+def attn_bwd_body(heads, blk, push_of, q_ref, do_ref, lse_ref, k_ref, v_ref, cos_ref, sin_ref, *refs):
+    refs = iter(refs)
+    src = take(refs, push_of.n_refs)
+    out_ref = next(refs)
+    dst = take(refs, push_of.n_refs)
+    prob_buf, dprob_buf, dk_acc, dv_acc = take(refs, 4)
+    push = push_of(src, dst, refs)
     step = pl.program_id(0)
+    push.open(step)
     scale = HEAD_DIM ** -0.5
     rows = heads * blk
     hcols = heads * HEAD_DIM
@@ -326,8 +385,10 @@
         out_ref[:, hcols:hcols + HEAD_DIM] = turn(d_key, cos_ref[...], -sin_ref[...]).astype(BF16)
         out_ref[:, hcols + HEAD_DIM:] = dv_acc[...].astype(BF16)
 
-
-def attn_backward(query, d_attn, lse, key, value, cos_tab, sin_tab, heads, blk=384):
+    push.close(step)
+
+
+def attn_backward(query, d_attn, lse, key, value, cos_tab, sin_tab, heads, push_of, blk=384):
     seq = query.shape[0]
     hcols = heads * HEAD_DIM
     width = hcols + 2 * HEAD_DIM
@@ -336,21 +397,26 @@
     whole = lambda i: (0, 0)
     flops = 10 * heads * seq * seq * HEAD_DIM // 2
     return pl.pallas_call(
-        functools.partial(attn_bwd_body, heads, blk),
+        functools.partial(attn_bwd_body, heads, blk, push_of),
         grid=(steps,),
-        in_specs=[pl.BlockSpec((blk, hcols), row), pl.BlockSpec((blk, hcols), row), pl.BlockSpec((blk, HEAD_DIM), row)] + [pl.BlockSpec((seq, HEAD_DIM), whole)] * 4,
-        out_specs=pl.BlockSpec((seq, width), whole),
-        out_shape=jax.ShapeDtypeStruct((seq, width), BF16),
-        scratch_shapes=[pltpu.VMEM((steps, heads * blk, blk), F32), pltpu.VMEM((steps, heads * blk, blk), BF16), pltpu.VMEM((seq, HEAD_DIM), F32), pltpu.VMEM((seq, HEAD_DIM), F32)],
-        compiler_params=pltpu.CompilerParams(dimension_semantics=("arbitrary",), vmem_limit_bytes=VMEM_MAX),
+        in_specs=[pl.BlockSpec((blk, hcols), row), pl.BlockSpec((blk, hcols), row), pl.BlockSpec((blk, HEAD_DIM), row)] + [pl.BlockSpec((seq, HEAD_DIM), whole)] * 4 + push_of.specs,
+        out_specs=[pl.BlockSpec((seq, width), whole)] + push_of.specs,
+        out_shape=[jax.ShapeDtypeStruct((seq, width), BF16)] + push_of.shapes,
+        scratch_shapes=[pltpu.VMEM((steps, heads * blk, blk), F32), pltpu.VMEM((steps, heads * blk, blk), BF16), pltpu.VMEM((seq, HEAD_DIM), F32), pltpu.VMEM((seq, HEAD_DIM), F32)] + push_of.sems,
+        compiler_params=pltpu.CompilerParams(**push_of.params, dimension_semantics=("arbitrary",), vmem_limit_bytes=VMEM_MAX),
         cost_estimate=pl.CostEstimate(flops=flops * 4, bytes_accessed=10 * 2 ** 20, transcendentals=heads * seq * seq // 2),
         name="attn_bwd",
-    )(query, d_attn, lse, key, value, cos_tab, sin_tab)
-
-
-def dgrad_body(n_parts, *refs):
-    parts = refs[:n_parts]
-    wo_ref, wd_ref, gate_ref, up_ref, dattn_ref, dgate_ref, dup_ref, hid_ref = refs[n_parts:]
+    )(query, d_attn, lse, key, value, cos_tab, sin_tab, *push_of.operands)
+
+
+def dgrad_body(n_parts, push_of, *refs):
+    refs = iter(refs)
+    parts = take(refs, n_parts)
+    wo_ref, wd_ref, gate_ref, up_ref = take(refs, 4)
+    src = take(refs, push_of.n_refs)
+    dattn_ref, dgate_ref, dup_ref, hid_ref = take(refs, 4)
+    push = push_of(src, take(refs, push_of.n_refs), refs)
+    push.open(pl.program_id(0))
 
     def product(w_ref, rows):
         acc, at = None, 0
@@ -362,142 +428,183 @@
         return acc.astype(BF16)
 
     dattn_ref[...] = product(wo_ref, slice(None))
-    for t in range(gate_ref.shape[1] // WIDE):
-        cols = slice(t * WIDE, (t + 1) * WIDE)
+    for t in range(gate_ref.shape[1] // BROAD):
+        cols = slice(t * BROAD, (t + 1) * BROAD)
         d_hidden = product(wd_ref, cols)
         hidden, pull = jax.vjp(gated, gate_ref[:, cols].astype(F32), up_ref[:, cols].astype(F32))
         d_gate, d_up = pull(d_hidden.astype(F32))
         hid_ref[:, cols] = hidden.astype(BF16)
         dgate_ref[:, cols] = d_gate.astype(BF16)
         dup_ref[:, cols] = d_up.astype(BF16)
-
-
-def cotangents(dy_parts, w_out, w_down, gate, up, layer, blk=512):
+    push.close(pl.program_id(0))
+
+
+def cotangents(dy_parts, w_out, w_down, gate, up, layer, push_of, blk=512):
     seq, fcols = gate.shape
     hcols, d_model = w_out.shape[1:]
     row = lambda i: (i, 0)
     flops = 2 * seq * d_model * (hcols + fcols)
     wide = pl.BlockSpec((blk, fcols), row)
     return pl.pallas_call(
-        functools.partial(dgrad_body, len(dy_parts)),
+        functools.partial(dgrad_body, len(dy_parts), push_of),
         grid=(seq // blk,),
-        in_specs=[pl.BlockSpec((blk, part.shape[1]), row) for part in dy_parts] + [pl.BlockSpec((1, hcols, d_model), lambda i: (layer, 0, 0)), pl.BlockSpec((1, fcols, d_model), lambda i: (layer, 0, 0)), wide, wide],
-        out_specs=[pl.BlockSpec((blk, hcols), row), wide, wide, wide],
-        out_shape=[jax.ShapeDtypeStruct((seq, hcols), BF16)] + [jax.ShapeDtypeStruct((seq, fcols), BF16)] * 3,
-        compiler_params=pltpu.CompilerParams(dimension_semantics=("arbitrary",), vmem_limit_bytes=VMEM_MAX),
+        in_specs=[pl.BlockSpec((blk, part.shape[1]), row) for part in dy_parts] + [pl.BlockSpec((1, hcols, d_model), lambda i: (layer, 0, 0)), pl.BlockSpec((1, fcols, d_model), lambda i: (layer, 0, 0)), wide, wide] + push_of.specs,
+        out_specs=[pl.BlockSpec((blk, hcols), row), wide, wide, wide] + push_of.specs,
+        out_shape=[jax.ShapeDtypeStruct((seq, hcols), BF16)] + [jax.ShapeDtypeStruct((seq, fcols), BF16)] * 3 + push_of.shapes,
+        scratch_shapes=push_of.sems,
+        compiler_params=pltpu.CompilerParams(**push_of.params, dimension_semantics=("arbitrary",), vmem_limit_bytes=VMEM_MAX),
         cost_estimate=pl.CostEstimate(flops=flops, bytes_accessed=32 * 2 ** 20, transcendentals=seq * fcols),
         name="cotangents",
-    )(*dy_parts, w_out, w_down, gate, up)
-
-
-def tail_body(n_parts, each, *refs):
-    attn_ref, hid_ref = refs[:2]
-    parts = refs[2:2 + n_parts]
-    q_ref, g_ref, u_ref = refs[2 + n_parts:5 + n_parts]
-    q_out, out_out, g_out, u_out, down_out = refs[-5:]
+    )(*dy_parts, w_out, w_down, gate, up, *push_of.operands)
+
+
+def spans(parts, blk):
+    result, begin = [], 0
+    for part in parts:
+        end = begin + part.shape[1] // blk
+        result.append((begin, end - 1))
+        begin = end
+    return result
+
+
+def on_part(step, ranges, parts, body):
+    for (begin, last), part in zip(ranges, parts):
+        @pl.when(jnp.logical_and(step >= begin, step <= last))
+        def _():
+            body(part[...])
+
+
+def tail_body(dy_spans, u_spans, *refs):
+    refs = iter(refs)
+    attn_ref, hid_ref = take(refs, 2)
+    parts = take(refs, len(dy_spans))
+    u_parts = take(refs, len(u_spans))
+    q_ref, g_ref, u_ref = take(refs, 3)
+    q_out, out_out, g_out, u_out, down_out = list(refs)[-5:]
     step = pl.program_id(0)
-    for n, part in enumerate(parts):
-        @pl.when(step // each == n)
-        def _():
-            right = part[...]
-            out_out[0] = dot_tn(attn_ref[...], right).astype(BF16)
-            down_out[0] = dot_tn(hid_ref[...], right).astype(BF16)
-    q_out[0] = q_ref[...]
+
+    def from_dy(right):
+        out_out[0] = dot_tn(attn_ref[...], right).astype(BF16)
+        down_out[0] = dot_tn(hid_ref[...], right).astype(BF16)
+
+    def from_u(left):
+        q_out[0] = dot_tn(left, q_ref[...]).astype(BF16)
+
+    on_part(step, dy_spans, parts, from_dy)
+    if u_spans:
+        on_part(step, u_spans, u_parts, from_u)
+    else:
+        q_out[0] = q_ref[...]
     g_out[0] = g_ref[...]
     u_out[0] = u_ref[...]
 
 
-def tail_grads(attn, hidden, dy_parts, ready, grads, layer, n_layers, blk=512):
+def tail_grads(attn, hidden, dy_parts, u_parts, ready, grads, layer, n_layers, blk=512):
     seq = attn.shape[0]
-    width = dy_parts[0].shape[1]
-    d_model = width * len(dy_parts)
-    each = width // blk
+    d_model = sum(part.shape[1] for part in dy_parts)
     whole = lambda j: (0, 0)
     hbm = pl.BlockSpec(memory_space=pl.ANY)
     rows = lambda width: pl.BlockSpec((blk, width), lambda j: (j, 0))
     rows_out = lambda width: pl.BlockSpec((1, blk, width), lambda j: (layer, j, 0))
     cols_out = lambda height: pl.BlockSpec((1, height, blk), lambda j: (layer, 0, j))
-    part_spec = lambda n: pl.BlockSpec((seq, blk), lambda j: (0, jnp.clip(j - n * each, 0, each - 1)))
+
+    dy_spans, u_spans = spans(dy_parts, blk), spans(u_parts, blk)
+
+    def part_specs(ranges):
+        return [pl.BlockSpec((seq, blk), lambda j, begin=begin, last=last: (0, jnp.clip(j, begin, last) - begin)) for begin, last in ranges]
+
     hcols, fcols = attn.shape[1], hidden.shape[1]
     widths = [item.shape[1] for item in ready]
     old = [item for item in grads if item is not None]
-    before = 5 + len(dy_parts)
+    before = 5 + len(dy_parts) + len(u_parts)
+    q_spec = pl.BlockSpec((seq, widths[0]), whole) if u_parts else rows(widths[0])
     return pl.pallas_call(
-        functools.partial(tail_body, len(dy_parts), each),
+        functools.partial(tail_body, dy_spans, u_spans),
         grid=(d_model // blk,),
-        in_specs=[pl.BlockSpec((seq, hcols), whole), pl.BlockSpec((seq, fcols), whole)] + [part_spec(n) for n in range(len(dy_parts))] + [rows(w) for w in widths] + [hbm] * len(old),
+        in_specs=[pl.BlockSpec((seq, hcols), whole), pl.BlockSpec((seq, fcols), whole)] + part_specs(dy_spans + u_spans) + [q_spec] + [rows(w) for w in widths[1:]] + [hbm] * len(old),
         out_specs=[rows_out(widths[0]), cols_out(hcols), rows_out(widths[1]), rows_out(widths[2]), cols_out(fcols)],
         out_shape=[jax.ShapeDtypeStruct((n_layers,) + dims, BF16) for dims in ((d_model, widths[0]), (hcols, d_model), (d_model, widths[1]), (d_model, widths[2]), (fcols, d_model))],
         input_output_aliases={before + n: n for n in range(len(old))},
         compiler_params=pltpu.CompilerParams(dimension_semantics=("arbitrary",), vmem_limit_bytes=VMEM_MAX),
         cost_estimate=pl.CostEstimate(flops=2 * seq * d_model * (hcols + fcols), bytes_accessed=60 * 2 ** 20, transcendentals=0),
         name="tail_grads",
-    )(attn, hidden, *dy_parts, *ready, *old)
+    )(attn, hidden, *dy_parts, *u_parts, *ready, *old)
 
 
 TILE = 256
 WIDE = 512
-NORM_ROWS = 16
-
-
-def fill_weight_grads(u_hbm, grads, lhs, rhs, sems):
+BROAD = 1024
+NORM_ROWS = 32
+
+
+def fill_weight_grads(fill_ops, u_parts, grads, lhs, rhs, sems):
     load_sem, store_sem = sems
-    seq, d_model = u_hbm.shape
-    steps = d_model // TILE
-
-    def cols_of(slot):
-        return tile_ds(slot, TILE)
-
-    def load(j, slot):
-        return pltpu.make_async_copy(u_hbm.at[:, cols_of(j)], rhs[2].at[0:seq, cols_of(slot)], load_sem.at[slot])
+    seq = u_parts[0].shape[0]
 
     def rows_at(base, slot):
         return pl.ds(pl.multiple_of(base + slot * TILE, TILE), TILE)
 
     def spots(slot):
-        return rhs[0].at[rows_at(seq, slot), :], rhs[1].at[rows_at(seq, slot), :], rhs[1].at[rows_at(seq + 2 * TILE, slot), :]
-
-    def stores(j, slot):
-        return [pltpu.make_async_copy(src, dst.at[cols_of(j), :], store_sem.at[slot, n]) for n, (src, dst) in enumerate(zip(spots(slot), grads))]
-
-    load(0, 0).start()
-
-    def step(j):
-        slot = lax.rem(j, 2)
-        load(j, slot).wait()
-
-        @pl.when(j + 1 < steps)
-        def _():
-            load(j + 1, 1 - slot).start()
-
-        @pl.when(j >= 2)
-        def _():
-            for copy in stores(j - 2, slot):
+        places = (rhs[0].at[rows_at(seq, slot), :], rhs[1].at[rows_at(seq, slot), :], rhs[1].at[rows_at(seq + WIDE, slot), :])
+        return [places[i] for i in fill_ops]
+
+    def one_part(begin, steps, u_hbm):
+        def load(j, slot):
+            return pltpu.make_async_copy(u_hbm.at[:, tile_ds(j, TILE)], rhs[2].at[0:seq, tile_ds(slot, TILE)], load_sem.at[slot])
+
+        def stores(j, slot):
+            return [pltpu.make_async_copy(src, dst.at[tile_ds(begin + j, TILE), :], store_sem.at[slot, k]) for k, (src, dst) in enumerate(zip(spots(slot), grads))]
+
+        load(0, 0).start()
+
+        def step(j):
+            slot = lax.rem(j, 2)
+            load(j, slot).wait()
+
+            @pl.when(j + 1 < steps)
+            def _():
+                load(j + 1, 1 - slot).start()
+
+            @pl.when(j >= 2)
+            def _():
+                for copy in stores(j - 2, slot):
+                    copy.wait()
+            left = rhs[2][0:seq, tile_ds(slot, TILE)]
+            for spot, i in zip(spots(slot), fill_ops):
+                spot[...] = dot_tn(left, lhs[i][...]).astype(BF16)
+            for copy in stores(j, slot):
+                copy.start()
+
+        loop(steps, step)
+        for j in (steps - 2, steps - 1):
+            for copy in stores(j, j % 2):
                 copy.wait()
-        left = rhs[2][0:seq, cols_of(slot)]
-        for spot, right in zip(spots(slot), lhs):
-            spot[...] = dot_tn(left, right[...]).astype(BF16)
-        for copy in stores(j, slot):
-            copy.start()
-
-    loop(steps, step)
-    for j in (steps - 2, steps - 1):
-        for copy in stores(j, j % 2):
-            copy.wait()
-
-
-def rs_body(n_ops, layer, trans, back, tp_axis, *refs):
+
+    begin = 0
+    for u_hbm in u_parts:
+        steps = u_hbm.shape[1] // TILE
+        one_part(begin, steps, u_hbm)
+        begin += steps
+
+
+def rs_body(n_ops, layer, trans, back, fill_ops, tp_size, tp_axis, *refs):
     refs = iter(refs)
     lhs_hbm = take(refs, n_ops)
     rhs_hbm = take(refs, n_ops)
     if back:
-        u_hbm, x_ref, gain_ref, dy_ref, dy_out, gain_out = take(refs, 6)
-        grad_hbm = take(refs, n_ops)
+        u_hbm = take(refs, back)
+        x_ref, gain_ref, dy_ref = take(refs, 3)
+        if tp_size:
+            above_ref = next(refs)
+        dy_out, gain_out = take(refs, 2)
+        grad_hbm = take(refs, len(fill_ops))
     out_ref = next(refs)
     lhs = take(refs, n_ops)
     rhs = take(refs, n_ops)
     (own, stage, pair_in, diag_in, near_in, far_in, last_out, last_in,
      lhs_sem, rhs_sem, pair_ssem, pair_rsem, diag_ssem, diag_rsem, near_ssem, near_rsem, far_ssem, far_rsem, last_ssem, last_rsem) = take(refs, 20)
+    if tp_size:
+        slots, slot_ssem, slot_rsem = take(refs, 3)
     fill_sems = list(refs)
     tiles, rblk = own.shape[1:3]
     rows_out = rblk // 2
@@ -541,7 +648,11 @@
         for i in ops:
             lhs_copy(i, slot).start()
 
-    greet(tp_axis, (partner, dev_x, dev_y))
+    if tp_size:
+        me = lax.axis_index(tp_axis)
+        greet(tp_axis, [lax.rem(me + k, tp_size) for k in range(1, tp_size)])
+    else:
+        greet(tp_axis, (partner, dev_x, dev_y))
 
     def product(slot, cols):
         acc = None
@@ -642,7 +753,7 @@
     loop(tiles, self_step)
 
     if back:
-        fill_weight_grads(u_hbm, grad_hbm, lhs, rhs, fill_sems)
+        fill_weight_grads(fill_ops, u_hbm, grad_hbm, lhs, rhs, fill_sems)
 
     def final_step(t):
         pair_wait(SELF, t)
@@ -666,19 +777,23 @@
 
     if back:
         gain = gain_ref[...]
-        gain_out[...] = jnp.zeros_like(gain)
+        gain_sum = slots.at[me, 0:1, :] if tp_size else gain_out
+        gain_sum[...] = jnp.zeros_like(gain)
 
         def norm_step(r):
             rows = tile_ds(r, NORM_ROWS)
             pull = jax.vjp(rms_scale, x_ref[rows, :].astype(F32), gain)[1]
             d_x, d_gain = pull(out_ref[rows, :].astype(BF16).astype(F32))
             dy_out[rows, :] = (dy_ref[rows, :].astype(F32) + d_x).astype(BF16)
-            gain_out[...] += d_gain
+            gain_sum[...] += d_gain
 
         loop(rows_out // NORM_ROWS, norm_step)
-
-
-def matmul_reduce_scatter(lhs_list, rhs_list, layer, trans, tp_axis, tp_size, cid, norm=None):
+        if tp_size:
+            slots[me, 1:, :] = above_ref[...]
+            gain_out[...] = sum_over(tp_axis, tp_size, slots, slot_ssem, slot_rsem)
+
+
+def matmul_reduce_scatter(lhs_list, rhs_list, layer, trans, tp_axis, tp_size, cid, u_parts=(), norm=(), fill_ops=(), n_gains=1):
     n_ops = len(lhs_list)
     seq = lhs_list[0].shape[0]
     d_model = rhs_list[0].shape[1] if trans else rhs_list[0].shape[2]
@@ -707,15 +822,18 @@
     operands = list(lhs_list) + list(rhs_list)
     in_specs = [hbm] * len(operands)
     out_specs, out_shape = [vmem], [jax.ShapeDtypeStruct((rows_out, d_model), F32)]
-    if norm is not None:
-        operands += norm
-        in_specs += [hbm] + [vmem] * (len(norm) - 1)
-        scratch = [pltpu.VMEM((rows_out, d_model), F32)] + scratch + [dma((2,)), dma((2, 3))]
-        out_specs = [vmem] * 2 + [hbm] * n_ops
-        out_shape = [jax.ShapeDtypeStruct((rows_out, d_model), BF16), jax.ShapeDtypeStruct((1, d_model), F32)]
-        out_shape += [jax.ShapeDtypeStruct((d_model, k), BF16) for k in ks]
+    if u_parts:
+        operands += u_parts + norm
+        in_specs += [hbm] * len(u_parts) + [vmem] * len(norm)
+        scratch = [pltpu.VMEM((rows_out, d_model), F32)] + scratch
+        if n_gains > 1:
+            scratch += [pltpu.VMEM((tp_size, n_gains, d_model), F32), dma((tp_size,)), dma((tp_size,))]
+        scratch += [dma((2,)), dma((2, 3))]
+        out_specs = [vmem] * 2 + [hbm] * len(fill_ops)
+        out_shape = [jax.ShapeDtypeStruct((rows_out, d_model), BF16), jax.ShapeDtypeStruct((n_gains, d_model), F32)]
+        out_shape += [jax.ShapeDtypeStruct((d_model, ks[i]), BF16) for i in fill_ops]
     return pl.pallas_call(
-        functools.partial(rs_body, n_ops, layer, trans, norm is not None, tp_axis),
+        functools.partial(rs_body, n_ops, layer, trans, len(u_parts), fill_ops, tp_size if n_gains > 1 else 0, tp_axis),
         in_specs=in_specs,
         out_specs=out_specs,
         out_shape=out_shape,
@@ -746,15 +864,15 @@
     core, chips, partner, dev_x, dev_y, near, far = ring_ids(tp_axis)
     qcols = wq.shape[1]
     fcols = wg.shape[1]
-    qtiles = [(s, min(WIDE, qcols - s)) for s in range(0, qcols, WIDE)]
-    ftiles = fcols // WIDE
+    qtiles = [(s, min(BROAD, qcols - s)) for s in range(0, qcols, BROAD)]
+    ftiles = fcols // BROAD
 
     def w_copy(k):
         if k < len(qtiles):
             cols = slice(qtiles[k][0], qtiles[k][0] + qtiles[k][1])
             return pltpu.make_async_copy(wq_hbm.at[layer, :, cols], wq.at[:, cols], w_sem.at[k])
         t, which = divmod(k - len(qtiles), 2)
-        cols = slice(t * WIDE, (t + 1) * WIDE)
+        cols = slice(t * BROAD, (t + 1) * BROAD)
         src, dst = ((wg_hbm, wg), (wu_hbm, wu))[which]
         return pltpu.make_async_copy(src.at[layer, :, cols], dst.at[:, cols], w_sem.at[k])
 
@@ -844,14 +962,14 @@
             def _():
                 w_copy(len(qtiles) + 2 * t).wait()
                 w_copy(len(qtiles) + 2 * t + 1).wait()
-            cols = slice(t * WIDE, (t + 1) * WIDE)
+            cols = slice(t * BROAD, (t + 1) * BROAD)
             gate = dot_nn(left, wg[:, cols]).astype(BF16)
             up = dot_nn(left, wu[:, cols]).astype(BF16)
-            stage[1][four, :, cols] = gate.reshape(count, piece, WIDE)
-            stage[2][four, :, cols] = up.reshape(count, piece, WIDE)
+            stage[1][four, :, cols] = gate.reshape(count, piece, BROAD)
+            stage[2][four, :, cols] = up.reshape(count, piece, BROAD)
             if with_hidden:
                 hid = gated(gate.astype(F32), up.astype(F32)).astype(BF16)
-                stage[3][four, :, cols] = hid.reshape(count, piece, WIDE)
+                stage[3][four, :, cols] = hid.reshape(count, piece, BROAD)
         for n in range(n_res):
             for i in range(count):
                 out_copy(first // 2 + i // 2, i % 2, n).start()
@@ -912,7 +1030,7 @@
     hbm = pl.BlockSpec(memory_space=pl.ANY)
     widths = [qcols, fcols, fcols] + [fcols] * with_hidden + [d_model] * with_u
     stage_widths = widths[:3 + with_hidden]
-    n_w = -(-qcols // WIDE) + 2 * (fcols // WIDE)
+    n_w = -(-qcols // BROAD) + 2 * (fcols // BROAD)
     dma = pltpu.SemaphoreType.DMA
     local = jax.ShapeDtypeStruct((rows, d_model), BF16)
     return pl.pallas_call(
@@ -929,40 +1047,6 @@
     )(*([x_loc] + ([total] if with_total else []) + [gain_row, w_qkv, w_gate, w_up]))
 
 
-def gain_body(tp_axis, tp_size, in_ref, out_ref, slots, ssem, rsem):
-    me = lax.axis_index(tp_axis)
-    barrier = pltpu.get_barrier_semaphore()
-    for k in range(1, tp_size):
-        pl.semaphore_signal(barrier, inc=1, device_id={tp_axis: lax.rem(me + k, tp_size)}, device_id_type=pl.DeviceIdType.MESH)
-    pl.semaphore_wait(barrier, tp_size - 1)
-    slots[me] = in_ref[...]
-    copies = []
-    for k in range(1, tp_size):
-        copies.append(pltpu.make_async_remote_copy(src_ref=in_ref, dst_ref=slots.at[me], send_sem=ssem.at[k], recv_sem=rsem.at[k], device_id={tp_axis: lax.rem(me + k, tp_size)}, device_id_type=pl.DeviceIdType.MESH))
-        copies[-1].start()
-    for k in range(1, tp_size):
-        source = lax.rem(me + tp_size - k, tp_size)
-        pltpu.make_async_remote_copy(src_ref=in_ref, dst_ref=slots.at[source], send_sem=ssem.at[k], recv_sem=rsem.at[k], device_id={tp_axis: source}, device_id_type=pl.DeviceIdType.MESH).wait_recv()
-    total = slots[0]
-    for k in range(1, tp_size):
-        total = total + slots[k]
-    out_ref[...] = total
-    for copy in copies:
-        copy.wait_send()
-
-
-def sum_gains(part, tp_axis, tp_size, cid):
-    return pl.pallas_call(
-        functools.partial(gain_body, tp_axis, tp_size),
-        in_specs=[pl.BlockSpec(memory_space=pltpu.VMEM)],
-        out_specs=pl.BlockSpec(memory_space=pltpu.VMEM),
-        out_shape=jax.ShapeDtypeStruct(part.shape, F32),
-        scratch_shapes=[pltpu.VMEM((tp_size,) + part.shape, F32), pltpu.SemaphoreType.DMA((tp_size,)), pltpu.SemaphoreType.DMA((tp_size,))],
-        compiler_params=pltpu.CompilerParams(collective_id=cid, has_side_effects=True),
-        name="gain_sum",
-    )(part)
-
-
 def solution(mesh):
     tp_size = mesh.shape['tp']
     row_spec = P(('dp', 'tp'), None)
@@ -978,7 +1062,6 @@
         gather = lambda value: lax.all_gather(value, 'tp', axis=0, tiled=True)
         saved = []
         x_cur, total = x_loc, None
-        u_full = None
         dy_parts = []
         for layer in range(n_layers):
             last = layer == n_layers - 1
@@ -987,8 +1070,8 @@
                 x_cur = results.pop(0)
             u_loc, qkv, gate, up, extra = results
             if last:
-                u_full = extra
-            query, key, value, attn, lse, dy_part = attn_forward(qkv, cos_tab, sin_tab, dy_loc, heads, 'tp', 3 * n_layers + 1 + layer, layer, n_layers)
+                u_parts = [extra]
+            query, key, value, attn, lse, dy_part = attn_forward(qkv, cos_tab, sin_tab, heads, PushOf(dy_loc, layer, n_layers, 'tp', tp_size, 3 * n_layers + 1 + layer))
             dy_parts.append(dy_part)
             saved.append((x_cur, u_loc, query, key, value, attn, lse, gate, up))
             if not last:
@@ -999,19 +1082,24 @@
         dy_cur = dy_loc
         for layer in reversed(range(n_layers)):
             x_sav, u_loc, query, key, value, attn, lse, gate, up = saved[layer]
-            d_attn, d_gate, d_up, hidden = cotangents(dy_parts, w_out, w_down, gate, up, layer)
-            d_qkv = attn_backward(query, d_attn, lse, key, value, cos_tab, sin_tab, heads)
-            dy_cur, gains[layer], *ready = matmul_reduce_scatter([d_qkv, d_gate, d_up], [w_qkv, w_gate, w_up], layer, True, 'tp', tp_size, n_layers + layer, [u_full, x_sav, norm_gain[layer:layer + 1], dy_cur])
-            dy_cur, attn, hidden, *rest = lax.optimization_barrier((dy_cur, attn, hidden, *ready, *dy_parts))
-            ready, dy_parts = rest[:3], rest[3:]
-            if layer > 0:
-                dy_next = gather(dy_cur)
-            grads = tail_grads(attn, hidden, dy_parts, ready, grads, layer, n_layers)
-            if layer > 0:
-                dy_next, u_next, *grads = lax.optimization_barrier((dy_next, saved[layer - 1][1], *grads))
-                dy_parts = [dy_next]
-                u_full = gather(u_next)
-        grad_gain = sum_gains(jnp.concatenate(gains), 'tp', tp_size, 3 * n_layers)
-        return (dy_cur, grad_gain, *grads)
+            d_attn, d_gate, d_up, hidden = cotangents(dy_parts, w_out, w_down, gate, up, layer, NoPush())
+            d_qkv, = attn_backward(query, d_attn, lse, key, value, cos_tab, sin_tab, heads, NoPush())
+            fill_ops = (1, 2) if layer else (0, 1, 2)
+            norm = [x_sav, norm_gain[layer:layer + 1], dy_cur]
+            if layer == 0:
+                norm.append(jnp.concatenate(gains[1:]))
+            dy_cur, gains[layer], *ready = matmul_reduce_scatter([d_qkv, d_gate, d_up], [w_qkv, w_gate, w_up], layer, True, 'tp', tp_size, n_layers + layer, u_parts, norm, fill_ops, 1 if layer else n_layers)
+            if layer == 0:
+                grads = tail_grads(attn, hidden, dy_parts, [], ready, grads, layer, n_layers)
+                continue
+            dy_cur, attn = lax.optimization_barrier((dy_cur, attn))
+            dy_next = gather(dy_cur)
+            grads = tail_grads(attn, hidden, dy_parts, u_parts, [d_qkv] + ready, grads, layer, n_layers)
+            below = list(saved[layer - 1])
+            dy_next, below[1], *grads = lax.optimization_barrier((dy_next, below[1], *grads))
+            saved[layer - 1] = below
+            u_parts = [gather(below[1])]
+            dy_parts = [dy_next]
+        return (dy_cur, gains[0], *grads)
 
     return jax.shard_map(device_program, mesh=mesh, in_specs=(row_spec, row_spec, P(None, None), col_spec, inner_spec, col_spec, col_spec, inner_spec), out_specs=(row_spec, P('dp', None), P('dp', None, 'tp'), P('dp', 'tp', None), P('dp', None, 'tp'), P('dp', None, 'tp'), P('dp', 'tp', None)), check_vma=False)

time: 1050 us -> 1020 us (0.971)
  waiting for transfers between devices: 68.9 us -> 54.5 us
  Pallas kernels: 951 us -> 939 us
    all_gather x4, waiting for transfers between devices: 68.8 us -> 54.4 us  [device_program(): gather = lambda value: lax.all_gather(value, 'tp', axis=0, tiled=True)]
    pallas_call x18 -> x17, Pallas kernels: 780 us -> 774 us  [the longest x5 473 us: matmul_reduce_scatter(): pl.pallas_call(functools.partial(rs_body, n_ops, layer, trans, len(u_part...]
  transfers between devices with their start and end apart: 4 -> 4, of which waited for: 4 -> 4; matrix products, arithmetic and copies ran while one was open for 0% -> 0% of each run, Pallas kernels for 14% -> 16%
where the time goes in v3:
time: 1020 us; the launch traced here: 1010 us
  Pallas kernels  939 us (92%)
  waiting for transfers between devices  54.5 us (5%)
  between operations  14.2 us (1%)
    pallas_call x5, Pallas kernels, matmul_reduce_scatter(): pl.pallas_call(functools.partial(rs_body, n_ops, layer, trans, len(u_part...  473 us
    pallas_call x3, Pallas kernels, gather_project(): pl.pallas_call(functools.partial(ag_body, layer, with_total, with_hidden,...  164 us
    pallas_call x3, Pallas kernels, tail_grads(): pl.pallas_call(functools.partial(tail_body, dy_spans, u_spans), grid=(d_m...  87.2 us
    pallas_call x3, Pallas kernels, cotangents(): pl.pallas_call(functools.partial(dgrad_body, len(dy_parts), push_of), gri...  75.8 us
    pallas_call x3, Pallas kernels, attn_backward(): pl.pallas_call(functools.partial(attn_bwd_body, heads, blk, push_of), gri...  69.9 us
    pallas_call x3, Pallas kernels, attn_forward(): pl.pallas_call(functools.partial(attn_fwd_body, heads, blk, push_of), gri...  68.4 us
    all_gather x4, waiting for transfers between devices, device_program(): gather = lambda value: lax.all_gather(value, 'tp', axis=0, tiled=True)  54.4 us
  transfers between devices with their start and end apart: 4, of which 4 were waited for; matrix products, arithmetic and copies ran while one was open for 0% of the time, Pallas kernels for 16%

profile of v3, /device:TPU:0, one launch (start us, length us, event | category | flops | bytes accessed | tf_op | source)
XLA Modules:
  0.0 1014.5 jit_solution(207709735037900203)
XLA Ops:
  7.2 0.0 all-gather.5.cloned.1.call-start
  7.2 1.5 fusion
  8.8 55.6 %ag_project.3 = (bf16[192,3072]{1,0:T(8,128)(2,1)}, bf16[1536,640]{1,0:T(8,128)(2,1)}, bf16[1536,1024]{1,0:T(8,128)(2,1)}, bf16[1536,1024]{1,0:T(8,128)(2,1)}, bf16[1536,1024]{1,0:T(8,128)(2,1)}) custom-call(bf16[192,3072]{1,0:T(8,128)(2,1)} %refs_7_.1, f32[1,3072]{1,0:T(1,128)} %get-tuple-element.192.refs_1_.refs_8_, bf16[3,3072,640]{2,1,0:T(8,128)(2,1)} %refs_3_.17, ...), custom_call_target="tpu_custom_call" | custom-call | flops 50734301184 | bytes 41943040 | tf_op jit(solution)/shard_map/ag_project/pallas_call | solution.py:1036
  64.4 23.1 %attn_fwd.3 = (bf16[1536,384]{1,0:T(8,128)(2,1)}, bf16[1536,128]{1,0:T(8,128)(2,1)}, bf16[1536,128]{1,0:T(8,128)(2,1)}, bf16[1536,384]{1,0:T(8,128)(2,1)}, f32[1...) custom-call(bf16[1536,640]{1,0:T(8,128)(2,1)} %get-tuple-element.99.qkv_ref.v_ref, f32[1536,128]{1,0:T(8,128)} %constant.4.clone.cos_ref, ...), custom_call_target="tpu_custom_call" | custom-call | flops 7247757312 | bytes 8388608 | tf_op jit(solution)/shard_map/attn_fwd/pallas_call | solution.py:313
  87.5 87.5 %matmul_rs.5.refs_1_ = f32[192,3072]{1,0:T(8,128)} custom-call(bf16[1536,384]{1,0:T(8,128)(2,1)} %get-tuple-element.101.refs_0_, bf16[1536,1024]{1,0:T(8,128)(2,1)} %get-tuple-element.102.refs_1_, bf16[3,384,3072]{2,1,0:T(8,128)(2,1)} %refs_1_.3, bf16[3,1024,3072]{2,1,0:T(8,128)(2,1)} %refs_2_.9), custom_call_target="tpu_custom_call" | custom-call | flops 39862665216 | bytes 41943040 | tf_op jit(solution)/shard_map/matmul_rs/pallas_call | solution.py:835
  175.1 54.5 %ag_project.4 = (bf16[192,3072]{1,0:T(8,128)(2,1)}, bf16[192,3072]{1,0:T(8,128)(2,1)}, bf16[1536,640]{1,0:T(8,128)(2,1)}, bf16[1536,1024]{1,0:T(8,128)(2,1)}, bf...) custom-call(bf16[192,3072]{1,0:T(8,128)(2,1)} %refs_7_.1, f32[192,3072]{1,0:T(8,128)} %matmul_rs.5.refs_1_, ...), custom_call_target="tpu_custom_call" | custom-call | flops 50734301184 | bytes 41943040 | tf_op jit(solution)/shard_map/ag_project/pallas_call | solution.py:1036
  229.5 22.6 %attn_fwd.4 = (bf16[1536,384]{1,0:T(8,128)(2,1)}, bf16[1536,128]{1,0:T(8,128)(2,1)}, bf16[1536,128]{1,0:T(8,128)(2,1)}, bf16[1536,384]{1,0:T(8,128)(2,1)}, f32[1...) custom-call(bf16[1536,640]{1,0:T(8,128)(2,1)} %get-tuple-element.103.qkv_ref.v_ref, f32[1536,128]{1,0:T(8,128)} %constant.4.clone.cos_ref, ...), custom_call_target="tpu_custom_call" | custom-call | flops 7247757312 | bytes 8388608 | tf_op jit(solution)/shard_map/attn_fwd/pallas_call | solution.py:313
  252.2 88.2 %matmul_rs.6.refs_1_ = f32[192,3072]{1,0:T(8,128)} custom-call(bf16[1536,384]{1,0:T(8,128)(2,1)} %get-tuple-element.149.refs_0_, bf16[1536,1024]{1,0:T(8,128)(2,1)} %get-tuple-element.107.refs_1_, bf16[3,384,3072]{2,1,0:T(8,128)(2,1)} %refs_1_.3, bf16[3,1024,3072]{2,1,0:T(8,128)(2,1)} %refs_2_.9), custom_call_target="tpu_custom_call" | custom-call | flops 39862665216 | bytes 41943040 | tf_op jit(solution)/shard_map/matmul_rs/pallas_call | solution.py:835
  340.4 54.4 %ag_project.5 = (bf16[192,3072]{1,0:T(8,128)(2,1)}, bf16[192,3072]{1,0:T(8,128)(2,1)}, bf16[1536,640]{1,0:T(8,128)(2,1)}, bf16[1536,1024]{1,0:T(8,128)(2,1)}, bf...) custom-call(bf16[192,3072]{1,0:T(8,128)(2,1)} %get-tuple-element.105.refs_0_.refs_7_, f32[192,3072]{1,0:T(8,128)} %matmul_rs.6.refs_1_, ...), custom_call_target="tpu_custom_call" | custom-call | flops 50734301184 | bytes 41943040 | tf_op jit(solution)/shard_map/ag_project/pallas_call | solution.py:1036
  394.8 22.6 %attn_fwd.5 = (bf16[1536,384]{1,0:T(8,128)(2,1)}, bf16[1536,128]{1,0:T(8,128)(2,1)}, bf16[1536,128]{1,0:T(8,128)(2,1)}, bf16[1536,384]{1,0:T(8,128)(2,1)}, f32[1...) custom-call(bf16[1536,640]{1,0:T(8,128)(2,1)} %get-tuple-element.108.qkv_ref.v_ref, f32[1536,128]{1,0:T(8,128)} %constant.4.clone.cos_ref, ...), custom_call_target="tpu_custom_call" | custom-call | flops 7247757312 | bytes 8388608 | tf_op jit(solution)/shard_map/attn_fwd/pallas_call | solution.py:313
  417.4 25.6 %cotangents.3 = (bf16[1536,384]{1,0:T(8,128)(2,1)}, bf16[1536,1024]{1,0:T(8,128)(2,1)}, bf16[1536,1024]{1,0:T(8,128)(2,1)}, bf16[1536,1024]{1,0:T(8,128)(2,1)}) custom-call(bf16[1536,1024]{1,0:T(8,128)(2,1)} %get-tuple-element.110.refs_0_.refs_2_, bf16[1536,1024]{1,0:T(8,128)(2,1)} %get-tuple-element.111.refs_1_.refs_3_, ...), custom_call_target="tpu_custom_call" | custom-call | flops 13287555072 | bytes 33554432 | tf_op jit(solution)/shard_map/cotangents/pallas_call | solution.py:448
  443.0 23.3 %attn_bwd.3.refs_0_.refs_6_ = bf16[1536,640]{1,0:T(8,128)(2,1)} custom-call(bf16[1536,384]{1,0:T(8,128)(2,1)} %get-tuple-element.109.q_ref, bf16[1536,384]{1,0:T(8,128)(2,1)} %get-tuple-element.115.do_ref, f32[1536,128]{1,0:T(8,128)} %get-tuple-element.116.lse_ref, bf16[1536,128]{1,0:T(8,128)(2,1)} %get-tuple-element.117.k_ref, ...), custom_call_target="tpu_custom_call" | custom-call | flops 18119393280 | bytes 10485760 | tf_op jit(solution)/shard_map/attn_bwd/pallas_call | solution.py:399
  466.3 94.4 %matmul_rs.7 = (bf16[192,3072]{1,0:T(8,128)(2,1)}, f32[1,3072]{1,0:T(1,128)}, bf16[3072,1024]{1,0:T(8,128)(2,1)}, bf16[3072,1024]{1,0:T(8,128)(2,1)}) custom-call(bf16[1536,640]{1,0:T(8,128)(2,1)} %attn_bwd.3.refs_0_.refs_6_, bf16[1536,1024]{1,0:T(8,128)(2,1)} %get-tuple-element.119.refs_1_, bf16[1536,1024]{1,0:T(8,128)(2,1)} %get-tuple-element.120.refs_2_, ...), custom_call_target="tpu_custom_call" | custom-call | flops 76101451776 | bytes 41943040 | tf_op jit(solution)/shard_map/matmul_rs/pallas_call | solution.py:835
  560.7 0.0 all-gather.5.cloned.1.call-update
  560.7 0.0 all-gather.7.cloned.1.call-start
  560.8 32.3 %tail_grads.3 = (bf16[3,3072,640]{2,1,0:T(8,128)(2,1)}, bf16[3,384,3072]{2,1,0:T(8,128)(2,1)}, bf16[3,3072,1024]{2,1,0:T(8,128)(2,1)}, bf16[3,3072,1024]{2,1,0:T(8,128)(2,1)}, bf16[3,1024,3072]{2,1,0:T(8,128)(2,1)}) custom-call(bf16[1536,384]{1,0:T(8,128)(2,1)} %get-tuple-element.127.refs_0_, bf16[1536,1024]{1,0:T(8,128)(2,1)} %get-tuple-element.128.refs_1_, ...), custom_call_target="tpu_custom_call" | custom-call | flops 13287555072 | bytes 62914560 | tf_op jit(solution)/shard_map/tail_grads/pallas_call | solution.py:521
  593.0 20.9 %all-gather.5.cloned.1.call-done.refs_0_.refs_2_ = bf16[1536,3072]{1,0:T(8,128)(2,1)} async-done(((bf16[192,3072]{1,0:T(8,128)(2,1)}), bf16[1536,3072]{1,0:T(8,128)(2,1)}) %all-gather.5.cloned.1.call-update) | async-done | bytes 9437200 | tf_op jit(solution)/shard_map/all_gather | solution.py:1062
  613.9 0.0 all-gather.7.cloned.1.call-update
  614.0 0.0 all-gather.9.cloned.1.call-start
  614.0 25.3 %cotangents.4 = (bf16[1536,384]{1,0:T(8,128)(2,1)}, bf16[1536,1024]{1,0:T(8,128)(2,1)}, bf16[1536,1024]{1,0:T(8,128)(2,1)}, bf16[1536,1024]{1,0:T(8,128)(2,1)}) custom-call(bf16[1536,3072]{1,0:T(8,128)(2,1)} %all-gather.5.cloned.1.call-done.refs_0_.refs_2_, bf16[3,384,3072]{2,1,0:T(8,128)(2,1)} %refs_1_.3, bf16[3,1024,3072]{2,1,0:T(8,128)(2,1)} %refs_2_.9, ...), custom_call_target="tpu_custom_call" | custom-call | flops 13287555072 | bytes 33554432 | tf_op jit(solution)/shard_map/cotangents/pallas_call | solution.py:448
  639.3 23.2 %attn_bwd.4.refs_0_.refs_4_ = bf16[1536,640]{1,0:T(8,128)(2,1)} custom-call(bf16[1536,384]{1,0:T(8,128)(2,1)} %get-tuple-element.104.q_ref, bf16[1536,384]{1,0:T(8,128)(2,1)} %get-tuple-element.139.do_ref, f32[1536,128]{1,0:T(8,128)} %get-tuple-element.140.lse_ref, bf16[1536,128]{1,0:T(8,128)(2,1)} %get-tuple-element.141.k_ref, ...), custom_call_target="tpu_custom_call" | custom-call | flops 18119393280 | bytes 10485760 | tf_op jit(solution)/shard_map/attn_bwd/pallas_call | solution.py:399
  662.6 6.2 all-gather.7.cloned.1.call-done.refs_6_.refs_3_
  668.7 95.1 %matmul_rs.8 = (bf16[192,3072]{1,0:T(8,128)(2,1)}, f32[1,3072]{1,0:T(1,128)}, bf16[3072,1024]{1,0:T(8,128)(2,1)}, bf16[3072,1024]{1,0:T(8,128)(2,1)}) custom-call(bf16[1536,640]{1,0:T(8,128)(2,1)} %attn_bwd.4.refs_0_.refs_4_, bf16[1536,1024]{1,0:T(8,128)(2,1)} %get-tuple-element.143.refs_1_, bf16[1536,1024]{1,0:T(8,128)(2,1)} %get-tuple-element.144.refs_2_, ...), custom_call_target="tpu_custom_call" | custom-call | flops 76101451776 | bytes 41943040 | tf_op jit(solution)/shard_map/matmul_rs/pallas_call | solution.py:835
  763.8 0.0 all-gather.9.cloned.1.call-update
  763.8 0.0 all-gather.11.cloned.1.call-start
  763.9 30.3 %tail_grads.4 = (bf16[3,3072,640]{2,1,0:T(8,128)(2,1)}, bf16[3,384,3072]{2,1,0:T(8,128)(2,1)}, bf16[3,3072,1024]{2,1,0:T(8,128)(2,1)}, bf16[3,3072,1024]{2,1,0:T(8,128)(2,1)}, bf16[3,1024,3072]{2,1,0:T(8,128)(2,1)}) custom-call(bf16[1536,384]{1,0:T(8,128)(2,1)} %get-tuple-element.149.r, ...), custom_call_target="tpu_custom_call", output_to_operand_aliasing={{0}: (7, {}), {1}: (8, {}), {2}: (9, {}), {3}: (10, {}), {4... | custom-call | flops 13287555072 | bytes 62914560 | tf_op jit(solution)/shard_map/tail_grads/pallas_call | solution.py:521
  794.2 22.4 %all-gather.9.cloned.1.call-done.refs_0_.refs_2_ = bf16[1536,3072]{1,0:T(8,128)(2,1)} async-done(((bf16[192,3072]{1,0:T(8,128)(2,1)}), bf16[1536,3072]{1,0:T(8,128)(2,1)}) %all-gather.9.cloned.1.call-update) | async-done | bytes 9437200 | tf_op jit(solution)/shard_map/all_gather | solution.py:1062
  816.6 0.0 all-gather.11.cloned.1.call-update
  816.6 1.4 pad_maximum_fusion.refs_10_
  818.0 24.9 %cotangents.5 = (bf16[1536,384]{1,0:T(8,128)(2,1)}, bf16[1536,1024]{1,0:T(8,128)(2,1)}, bf16[1536,1024]{1,0:T(8,128)(2,1)}, bf16[1536,1024]{1,0:T(8,128)(2,1)}) custom-call(bf16[1536,3072]{1,0:T(8,128)(2,1)} %all-gather.9.cloned.1.call-done.refs_0_.refs_2_, bf16[3,384,3072]{2,1,0:T(8,128)(2,1)} %refs_1_.3, bf16[3,1024,3072]{2,1,0:T(8,128)(2,1)} %refs_2_.9, ...), custom_call_target="tpu_custom_call" | custom-call | flops 13287555072 | bytes 33554432 | tf_op jit(solution)/shard_map/cotangents/pallas_call | solution.py:448
  842.8 23.4 %attn_bwd.5.refs_0_ = bf16[1536,640]{1,0:T(8,128)(2,1)} custom-call(bf16[1536,384]{1,0:T(8,128)(2,1)} %get-tuple-element.100.q_ref, bf16[1536,384]{1,0:T(8,128)(2,1)} %get-tuple-element.166.do_ref, f32[1536,128]{1,0:T(8,128)} %get-tuple-element.167.lse_ref, bf16[1536,128]{1,0:T(8,128)(2,1)} %get-tuple-element.168.k_ref, ...), custom_call_target="tpu_custom_call" | custom-call | flops 18119393280 | bytes 10485760 | tf_op jit(solution)/shard_map/attn_bwd/pallas_call | solution.py:399
  866.2 5.0 all-gather.11.cloned.1.call-done.refs_6_
  871.2 107.9 %matmul_rs.9 = (bf16[192,3072]{1,0:T(8,128)(2,1)}, f32[3,3072]{1,0:T(4,128)}, bf16[3072,640]{1,0:T(8,128)(2,1)}, bf16[3072,1024]{1,0:T(8,128)(2,1)}, bf16[3072,1024]{1,0:T(8,128)(2,1)}) custom-call(bf16[1536,640]{1,0:T(8,128)(2,1)} %attn_bwd.5.refs_0_, bf16[1536,1024]{1,0:T(8,128)(2,1)} %get-tuple-element.170.refs_1_, ...), custom_call_target="tpu_custom_call" | custom-call | flops 76101451776 | bytes 41943040 | tf_op jit(solution)/shard_map/matmul_rs/pallas_call | solution.py:835
  979.1 24.6 %tail_grads.5 = (bf16[3,3072,640]{2,1,0:T(8,128)(2,1)}, bf16[3,384,3072]{2,1,0:T(8,128)(2,1)}, bf16[3,3072,1024]{2,1,0:T(8,128)(2,1)}, bf16[3,3072,1024]{2,1,0:T(8,128)(2,1)}, bf16[3,1024,3072]{2,1,0:T(8,128)(2,1)}) custom-call(bf16[1536,384]{1,0:T(8,128)(2,1)} %get-tuple-element.101.r, ...), custom_call_target="tpu_custom_call", output_to_operand_aliasing={{0}: (6, {}), {1}: (7, {}), {2}: (8, {}), {3}: (9, {}), {4}... | custom-call | flops 13287555072 | bytes 62914560 | tf_op jit(solution)/shard_map/tail_grads/pallas_call | solution.py:521
  1003.8 2.4 copy.39
  1006.1 1.4 copy.40
Async XLA Ops:
  7.2 606.8 %all-gather.5.cloned.1.call-start = ((), (), s32[]{:S(2)}) async-start(), calls=%async_computation | async-start | bytes 10616832 | tf_op jit(solution)/shard_map/all_gather | solution.py:1062
  560.7 108.0 %all-gather.7.cloned.1.call-start = ((), (), s32[]{:S(2)}) async-start(), calls=%async_computation.1 | async-start | bytes 10616832 | tf_op jit(solution)/shard_map/all_gather | solution.py:1062
  614.0 202.6 %all-gather.9.cloned.1.call-start = ((), (), s32[]{:S(2)}) async-start(), calls=%async_computation.2 | async-start | bytes 10616832 | tf_op jit(solution)/shard_map/all_gather | solution.py:1062
  763.8 107.4 %all-gather.11.cloned.1.call-start = ((), (), s32[]{:S(2)}) async-start(), calls=%async_computation.3 | async-start | bytes 10616832 | tf_op jit(solution)/shard_map/all_gather | solution.py:1062
Sparse Core Ops, SparseCore 0:
  560.8 53.0 all-gather.4
  615.7 52.9 all-gather.6
  764.0 52.5 all-gather.8
  818.2 52.9 all-gather.10

commit v4 on v3

--- a/solution.py
+++ b/solution.py
@@ -37,13 +37,22 @@
     return pl.ds(pl.multiple_of(index * size, size), size)
 
 
-def rope_tables(seq_len):
+def rope_tables(seq_len, fine=64):
     half_dim = HEAD_DIM // 2
     freqs = ROPE_BASE ** (-2.0 * np.arange(half_dim) / HEAD_DIM)
-    angles = np.arange(seq_len)[:, None] * freqs[None, :]
-    cos, sin = np.cos(angles), np.sin(angles)
-    tables = np.concatenate([cos, cos], axis=1), np.concatenate([-sin, sin], axis=1)
-    return [jnp.asarray(table.astype(np.float32)) for table in tables]
+
+    def small(positions):
+        angles = positions[:, None] * freqs[None, :]
+        cos, sin = np.cos(angles), np.sin(angles)
+        tables = np.concatenate([cos, cos], axis=1), np.concatenate([-sin, sin], axis=1)
+        return [jnp.asarray(table.astype(np.float32)) for table in tables]
+
+    parts = lax.optimization_barrier(small(np.arange(seq_len // fine) * fine) + small(np.arange(fine)))
+    cos_far, sin_far = [part[:, None, :] for part in parts[:2]]
+    cos_near, sin_near = [part[None, :, :] for part in parts[2:]]
+    cos_tab = cos_far * cos_near - sin_far * sin_near
+    sin_tab = sin_far * cos_near + cos_far * sin_near
+    return cos_tab.reshape(seq_len, HEAD_DIM), sin_tab.reshape(seq_len, HEAD_DIM)
 
 
 def rms_scale(x_f32, gain_row):
@@ -480,8 +489,11 @@
     parts = take(refs, len(dy_spans))
     u_parts = take(refs, len(u_spans))
     q_ref, g_ref, u_ref = take(refs, 3)
-    q_out, out_out, g_out, u_out, down_out = list(refs)[-5:]
+    q_out, out_out, g_out, u_out, down_out, right_buf = list(refs)[-6:]
     step = pl.program_id(0)
+
+    def pick(right):
+        right_buf[...] = right
 
     def from_dy(right):
         out_out[0] = dot_tn(attn_ref[...], right).astype(BF16)
@@ -490,7 +502,11 @@
     def from_u(left):
         q_out[0] = dot_tn(left, q_ref[...]).astype(BF16)
 
-    on_part(step, dy_spans, parts, from_dy)
+    if len(dy_spans) > 1:
+        on_part(step, dy_spans, parts, pick)
+        from_dy(right_buf[...])
+    else:
+        from_dy(parts[0][...])
     if u_spans:
         on_part(step, u_spans, u_parts, from_u)
     else:
@@ -525,6 +541,7 @@
         out_specs=[rows_out(widths[0]), cols_out(hcols), rows_out(widths[1]), rows_out(widths[2]), cols_out(fcols)],
         out_shape=[jax.ShapeDtypeStruct((n_layers,) + dims, BF16) for dims in ((d_model, widths[0]), (hcols, d_model), (d_model, widths[1]), (d_model, widths[2]), (fcols, d_model))],
         input_output_aliases={before + n: n for n in range(len(old))},
+        scratch_shapes=[pltpu.VMEM((seq, blk), BF16)],
         compiler_params=pltpu.CompilerParams(dimension_semantics=("arbitrary",), vmem_limit_bytes=VMEM_MAX),
         cost_estimate=pl.CostEstimate(flops=2 * seq * d_model * (hcols + fcols), bytes_accessed=60 * 2 ** 20, transcendentals=0),
         name="tail_grads",

time: 1020 us -> 1030 us (level)
  no operation moved by 1% of the time
where the time goes in v4:
time: 1030 us; the launch traced here: 1020 us
  Pallas kernels  940 us (91%)
  waiting for transfers between devices  53.2 us (5%)
  between operations  14 us (1%)
    pallas_call x5, Pallas kernels, matmul_reduce_scatter(): pl.pallas_call(functools.partial(rs_body, n_ops, layer, trans, len(u_part...  474 us
    pallas_call x3, Pallas kernels, gather_project(): pl.pallas_call(functools.partial(ag_body, layer, with_total, with_hidden,...  165 us
    pallas_call x3, Pallas kernels, tail_grads(): pl.pallas_call(functools.partial(tail_body, dy_spans, u_spans), grid=(d_m...  88.2 us
    pallas_call x3, Pallas kernels, cotangents(): pl.pallas_call(functools.partial(dgrad_body, len(dy_parts), push_of), gri...  75.4 us
    pallas_call x3, Pallas kernels, attn_backward(): pl.pallas_call(functools.partial(attn_bwd_body, heads, blk, push_of), gri...  69.9 us
    pallas_call x3, Pallas kernels, attn_forward(): pl.pallas_call(functools.partial(attn_fwd_body, heads, blk, push_of), gri...  68.6 us
    all_gather x4, waiting for transfers between devices, device_program(): gather = lambda value: lax.all_gather(value, 'tp', axis=0, tiled=True)  53.1 us
  transfers between devices with their start and end apart: 4, of which 4 were waited for; matrix products, arithmetic and copies ran while one was open for 0% of the time, Pallas kernels for 16%

profile of v4, /device:TPU:0, one launch (start us, length us, event | category | flops | bytes accessed | tf_op | source)
XLA Modules:
  0.0 1016.6 jit_solution(12475347398074073120)
XLA Ops:
  7.2 0.0 all-gather.5.cloned.1.call-start
  7.2 1.5 fusion
  8.8 2.2 multiply_add_fusion
  10.9 55.5 %ag_project.3 = (bf16[192,3072]{1,0:T(8,128)(2,1)}, bf16[1536,640]{1,0:T(8,128)(2,1)}, bf16[1536,1024]{1,0:T(8,128)(2,1)}, bf16[1536,1024]{1,0:T(8,128)(2,1)}, bf16[1536,1024]{1,0:T(8,128)(2,1)}) custom-call(bf16[192,3072]{1,0:T(8,128)(2,1)} %refs_7_.1, f32[1,3072]{1,0:T(1,128)} %get-tuple-element.202.refs_1_.refs_8_, bf16[3,3072,640]{2,1,0:T(8,128)(2,1)} %refs_3_.17, ...), custom_call_target="tpu_custom_call" | custom-call | flops 50734301184 | bytes 41943040 | tf_op jit(solution)/shard_map/ag_project/pallas_call | solution.py:1053
  66.5 23.2 %attn_fwd.3 = (bf16[1536,384]{1,0:T(8,128)(2,1)}, bf16[1536,128]{1,0:T(8,128)(2,1)}, bf16[1536,128]{1,0:T(8,128)(2,1)}, bf16[1536,384]{1,0:T(8,128)(2,1)}, f32[1...) custom-call(bf16[1536,640]{1,0:T(8,128)(2,1)} %get-tuple-element.103.qkv_ref.v_ref, f32[1536,128]{1,0:T(8,128)} %bitcast.8, ...), custom_call_target="tpu_custom_call" | custom-call | flops 7247757312 | bytes 8388608 | tf_op jit(solution)/shard_map/attn_fwd/pallas_call | solution.py:322
  89.7 87.3 %matmul_rs.5.refs_1_ = f32[192,3072]{1,0:T(8,128)} custom-call(bf16[1536,384]{1,0:T(8,128)(2,1)} %get-tuple-element.109.refs_0_, bf16[1536,1024]{1,0:T(8,128)(2,1)} %get-tuple-element.110.refs_1_, bf16[3,384,3072]{2,1,0:T(8,128)(2,1)} %refs_1_.3, bf16[3,1024,3072]{2,1,0:T(8,128)(2,1)} %refs_2_.9), custom_call_target="tpu_custom_call" | custom-call | flops 39862665216 | bytes 41943040 | tf_op jit(solution)/shard_map/matmul_rs/pallas_call | solution.py:852
  177.0 54.7 %ag_project.4 = (bf16[192,3072]{1,0:T(8,128)(2,1)}, bf16[192,3072]{1,0:T(8,128)(2,1)}, bf16[1536,640]{1,0:T(8,128)(2,1)}, bf16[1536,1024]{1,0:T(8,128)(2,1)}, bf...) custom-call(bf16[192,3072]{1,0:T(8,128)(2,1)} %refs_7_.1, f32[192,3072]{1,0:T(8,128)} %matmul_rs.5.refs_1_, ...), custom_call_target="tpu_custom_call" | custom-call | flops 50734301184 | bytes 41943040 | tf_op jit(solution)/shard_map/ag_project/pallas_call | solution.py:1053
  231.7 22.7 %attn_fwd.4 = (bf16[1536,384]{1,0:T(8,128)(2,1)}, bf16[1536,128]{1,0:T(8,128)(2,1)}, bf16[1536,128]{1,0:T(8,128)(2,1)}, bf16[1536,384]{1,0:T(8,128)(2,1)}, f32[1...) custom-call(bf16[1536,640]{1,0:T(8,128)(2,1)} %get-tuple-element.111.qkv_ref.v_ref, f32[1536,128]{1,0:T(8,128)} %bitcast.9, ...), custom_call_target="tpu_custom_call" | custom-call | flops 7247757312 | bytes 8388608 | tf_op jit(solution)/shard_map/attn_fwd/pallas_call | solution.py:322
  254.4 88.2 %matmul_rs.6.refs_1_ = f32[192,3072]{1,0:T(8,128)} custom-call(bf16[1536,384]{1,0:T(8,128)(2,1)} %get-tuple-element.157.refs_0_, bf16[1536,1024]{1,0:T(8,128)(2,1)} %get-tuple-element.115.refs_1_, bf16[3,384,3072]{2,1,0:T(8,128)(2,1)} %refs_1_.3, bf16[3,1024,3072]{2,1,0:T(8,128)(2,1)} %refs_2_.9), custom_call_target="tpu_custom_call" | custom-call | flops 39862665216 | bytes 41943040 | tf_op jit(solution)/shard_map/matmul_rs/pallas_call | solution.py:852
  342.7 54.4 %ag_project.5 = (bf16[192,3072]{1,0:T(8,128)(2,1)}, bf16[192,3072]{1,0:T(8,128)(2,1)}, bf16[1536,640]{1,0:T(8,128)(2,1)}, bf16[1536,1024]{1,0:T(8,128)(2,1)}, bf...) custom-call(bf16[192,3072]{1,0:T(8,128)(2,1)} %get-tuple-element.113.refs_0_.refs_7_, f32[192,3072]{1,0:T(8,128)} %matmul_rs.6.refs_1_, ...), custom_call_target="tpu_custom_call" | custom-call | flops 50734301184 | bytes 41943040 | tf_op jit(solution)/shard_map/ag_project/pallas_call | solution.py:1053
  397.0 22.7 %attn_fwd.5 = (bf16[1536,384]{1,0:T(8,128)(2,1)}, bf16[1536,128]{1,0:T(8,128)(2,1)}, bf16[1536,128]{1,0:T(8,128)(2,1)}, bf16[1536,384]{1,0:T(8,128)(2,1)}, f32[1...) custom-call(bf16[1536,640]{1,0:T(8,128)(2,1)} %get-tuple-element.116.qkv_ref.v_ref, f32[1536,128]{1,0:T(8,128)} %bitcast.10, ...), custom_call_target="tpu_custom_call" | custom-call | flops 7247757312 | bytes 8388608 | tf_op jit(solution)/shard_map/attn_fwd/pallas_call | solution.py:322
  419.7 25.4 %cotangents.3 = (bf16[1536,384]{1,0:T(8,128)(2,1)}, bf16[1536,1024]{1,0:T(8,128)(2,1)}, bf16[1536,1024]{1,0:T(8,128)(2,1)}, bf16[1536,1024]{1,0:T(8,128)(2,1)}) custom-call(bf16[1536,1024]{1,0:T(8,128)(2,1)} %get-tuple-element.118.refs_0_.refs_2_, bf16[1536,1024]{1,0:T(8,128)(2,1)} %get-tuple-element.119.refs_1_.refs_3_, ...), custom_call_target="tpu_custom_call" | custom-call | flops 13287555072 | bytes 33554432 | tf_op jit(solution)/shard_map/cotangents/pallas_call | solution.py:457
  445.1 23.3 %attn_bwd.3.refs_0_.refs_6_ = bf16[1536,640]{1,0:T(8,128)(2,1)} custom-call(bf16[1536,384]{1,0:T(8,128)(2,1)} %get-tuple-element.117.q_ref, bf16[1536,384]{1,0:T(8,128)(2,1)} %get-tuple-element.123.do_ref, f32[1536,128]{1,0:T(8,128)} %get-tuple-element.124.lse_ref, bf16[1536,128]{1,0:T(8,128)(2,1)} %get-tuple-element.125.k_ref, ...), custom_call_target="tpu_custom_call" | custom-call | flops 18119393280 | bytes 10485760 | tf_op jit(solution)/shard_map/attn_bwd/pallas_call | solution.py:408
  468.4 94.7 %matmul_rs.7 = (bf16[192,3072]{1,0:T(8,128)(2,1)}, f32[1,3072]{1,0:T(1,128)}, bf16[3072,1024]{1,0:T(8,128)(2,1)}, bf16[3072,1024]{1,0:T(8,128)(2,1)}) custom-call(bf16[1536,640]{1,0:T(8,128)(2,1)} %attn_bwd.3.refs_0_.refs_6_, bf16[1536,1024]{1,0:T(8,128)(2,1)} %get-tuple-element.127.refs_1_, bf16[1536,1024]{1,0:T(8,128)(2,1)} %get-tuple-element.128.refs_2_, ...), custom_call_target="tpu_custom_call" | custom-call | flops 76101451776 | bytes 41943040 | tf_op jit(solution)/shard_map/matmul_rs/pallas_call | solution.py:852
  563.1 0.0 all-gather.5.cloned.1.call-update
  563.1 0.0 all-gather.7.cloned.1.call-start
  563.2 32.9 %tail_grads.3 = (bf16[3,3072,640]{2,1,0:T(8,128)(2,1)}, bf16[3,384,3072]{2,1,0:T(8,128)(2,1)}, bf16[3,3072,1024]{2,1,0:T(8,128)(2,1)}, bf16[3,3072,1024]{2,1,0:T(8,128)(2,1)}, bf16[3,1024,3072]{2,1,0:T(8,128)(2,1)}) custom-call(bf16[1536,384]{1,0:T(8,128)(2,1)} %get-tuple-element.135.refs_0_, bf16[1536,1024]{1,0:T(8,128)(2,1)} %get-tuple-element.136.refs_1_, ...), custom_call_target="tpu_custom_call" | custom-call | flops 13287555072 | bytes 62914560 | tf_op jit(solution)/shard_map/tail_grads/pallas_call | solution.py:537
  596.1 20.3 %all-gather.5.cloned.1.call-done.refs_0_.refs_2_ = bf16[1536,3072]{1,0:T(8,128)(2,1)} async-done(((bf16[192,3072]{1,0:T(8,128)(2,1)}), bf16[1536,3072]{1,0:T(8,128)(2,1)}) %all-gather.5.cloned.1.call-update) | async-done | bytes 9437200 | tf_op jit(solution)/shard_map/all_gather | solution.py:1079
  616.3 0.0 all-gather.7.cloned.1.call-update
  616.4 0.0 all-gather.9.cloned.1.call-start
  616.4 25.1 %cotangents.4 = (bf16[1536,384]{1,0:T(8,128)(2,1)}, bf16[1536,1024]{1,0:T(8,128)(2,1)}, bf16[1536,1024]{1,0:T(8,128)(2,1)}, bf16[1536,1024]{1,0:T(8,128)(2,1)}) custom-call(bf16[1536,3072]{1,0:T(8,128)(2,1)} %all-gather.5.cloned.1.call-done.refs_0_.refs_2_, bf16[3,384,3072]{2,1,0:T(8,128)(2,1)} %refs_1_.3, bf16[3,1024,3072]{2,1,0:T(8,128)(2,1)} %refs_2_.9, ...), custom_call_target="tpu_custom_call" | custom-call | flops 13287555072 | bytes 33554432 | tf_op jit(solution)/shard_map/cotangents/pallas_call | solution.py:457
  641.5 23.3 %attn_bwd.4.refs_0_.refs_4_ = bf16[1536,640]{1,0:T(8,128)(2,1)} custom-call(bf16[1536,384]{1,0:T(8,128)(2,1)} %get-tuple-element.112.q_ref, bf16[1536,384]{1,0:T(8,128)(2,1)} %get-tuple-element.147.do_ref, f32[1536,128]{1,0:T(8,128)} %get-tuple-element.148.lse_ref, bf16[1536,128]{1,0:T(8,128)(2,1)} %get-tuple-element.149.k_ref, ...), custom_call_target="tpu_custom_call" | custom-call | flops 18119393280 | bytes 10485760 | tf_op jit(solution)/shard_map/attn_bwd/pallas_call | solution.py:408
  664.7 6.4 all-gather.7.cloned.1.call-done.refs_6_.refs_3_
  671.1 95.4 %matmul_rs.8 = (bf16[192,3072]{1,0:T(8,128)(2,1)}, f32[1,3072]{1,0:T(1,128)}, bf16[3072,1024]{1,0:T(8,128)(2,1)}, bf16[3072,1024]{1,0:T(8,128)(2,1)}) custom-call(bf16[1536,640]{1,0:T(8,128)(2,1)} %attn_bwd.4.refs_0_.refs_4_, bf16[1536,1024]{1,0:T(8,128)(2,1)} %get-tuple-element.151.refs_1_, bf16[1536,1024]{1,0:T(8,128)(2,1)} %get-tuple-element.152.refs_2_, ...), custom_call_target="tpu_custom_call" | custom-call | flops 76101451776 | bytes 41943040 | tf_op jit(solution)/shard_map/matmul_rs/pallas_call | solution.py:852
  766.5 0.0 all-gather.9.cloned.1.call-update
  766.6 0.0 all-gather.11.cloned.1.call-start
  766.6 31.2 %tail_grads.4 = (bf16[3,3072,640]{2,1,0:T(8,128)(2,1)}, bf16[3,384,3072]{2,1,0:T(8,128)(2,1)}, bf16[3,3072,1024]{2,1,0:T(8,128)(2,1)}, bf16[3,3072,1024]{2,1,0:T(8,128)(2,1)}, bf16[3,1024,3072]{2,1,0:T(8,128)(2,1)}) custom-call(bf16[1536,384]{1,0:T(8,128)(2,1)} %get-tuple-element.157.r, ...), custom_call_target="tpu_custom_call", output_to_operand_aliasing={{0}: (7, {}), {1}: (8, {}), {2}: (9, {}), {3}: (10, {}), {4... | custom-call | flops 13287555072 | bytes 62914560 | tf_op jit(solution)/shard_map/tail_grads/pallas_call | solution.py:537
  797.8 21.4 %all-gather.9.cloned.1.call-done.refs_0_.refs_2_ = bf16[1536,3072]{1,0:T(8,128)(2,1)} async-done(((bf16[192,3072]{1,0:T(8,128)(2,1)}), bf16[1536,3072]{1,0:T(8,128)(2,1)}) %all-gather.9.cloned.1.call-update) | async-done | bytes 9437200 | tf_op jit(solution)/shard_map/all_gather | solution.py:1079
  819.2 0.0 all-gather.11.cloned.1.call-update
  819.2 1.4 pad_maximum_fusion.refs_10_
  820.6 24.9 %cotangents.5 = (bf16[1536,384]{1,0:T(8,128)(2,1)}, bf16[1536,1024]{1,0:T(8,128)(2,1)}, bf16[1536,1024]{1,0:T(8,128)(2,1)}, bf16[1536,1024]{1,0:T(8,128)(2,1)}) custom-call(bf16[1536,3072]{1,0:T(8,128)(2,1)} %all-gather.9.cloned.1.call-done.refs_0_.refs_2_, bf16[3,384,3072]{2,1,0:T(8,128)(2,1)} %refs_1_.3, bf16[3,1024,3072]{2,1,0:T(8,128)(2,1)} %refs_2_.9, ...), custom_call_target="tpu_custom_call" | custom-call | flops 13287555072 | bytes 33554432 | tf_op jit(solution)/shard_map/cotangents/pallas_call | solution.py:457
  845.5 23.3 %attn_bwd.5.refs_0_ = bf16[1536,640]{1,0:T(8,128)(2,1)} custom-call(bf16[1536,384]{1,0:T(8,128)(2,1)} %get-tuple-element.108.q_ref, bf16[1536,384]{1,0:T(8,128)(2,1)} %get-tuple-element.174.do_ref, f32[1536,128]{1,0:T(8,128)} %get-tuple-element.175.lse_ref, bf16[1536,128]{1,0:T(8,128)(2,1)} %get-tuple-element.176.k_ref, ...), custom_call_target="tpu_custom_call" | custom-call | flops 18119393280 | bytes 10485760 | tf_op jit(solution)/shard_map/attn_bwd/pallas_call | solution.py:408
  868.8 5.0 all-gather.11.cloned.1.call-done.refs_6_
  873.8 108.1 %matmul_rs.9 = (bf16[192,3072]{1,0:T(8,128)(2,1)}, f32[3,3072]{1,0:T(4,128)}, bf16[3072,640]{1,0:T(8,128)(2,1)}, bf16[3072,1024]{1,0:T(8,128)(2,1)}, bf16[3072,1024]{1,0:T(8,128)(2,1)}) custom-call(bf16[1536,640]{1,0:T(8,128)(2,1)} %attn_bwd.5.refs_0_, bf16[1536,1024]{1,0:T(8,128)(2,1)} %get-tuple-element.178.refs_1_, ...), custom_call_target="tpu_custom_call" | custom-call | flops 76101451776 | bytes 41943040 | tf_op jit(solution)/shard_map/matmul_rs/pallas_call | solution.py:852
  982.0 24.1 %tail_grads.5 = (bf16[3,3072,640]{2,1,0:T(8,128)(2,1)}, bf16[3,384,3072]{2,1,0:T(8,128)(2,1)}, bf16[3,3072,1024]{2,1,0:T(8,128)(2,1)}, bf16[3,3072,1024]{2,1,0:T(8,128)(2,1)}, bf16[3,1024,3072]{2,1,0:T(8,128)(2,1)}) custom-call(bf16[1536,384]{1,0:T(8,128)(2,1)} %get-tuple-element.109.r, ...), custom_call_target="tpu_custom_call", output_to_operand_aliasing={{0}: (6, {}), {1}: (7, {}), {2}: (8, {}), {3}: (9, {}), {4}... | custom-call | flops 13287555072 | bytes 62914560 | tf_op jit(solution)/shard_map/tail_grads/pallas_call | solution.py:537
  1006.1 2.4 copy.41
  1008.5 1.4 copy.42
Async XLA Ops:
  7.2 609.2 %all-gather.5.cloned.1.call-start = ((), (), s32[]{:S(2)}) async-start(), calls=%async_computation | async-start | bytes 10616832 | tf_op jit(solution)/shard_map/all_gather | solution.py:1079
  563.1 108.0 %all-gather.7.cloned.1.call-start = ((), (), s32[]{:S(2)}) async-start(), calls=%async_computation.1 | async-start | bytes 10616832 | tf_op jit(solution)/shard_map/all_gather | solution.py:1079
  616.4 202.8 %all-gather.9.cloned.1.call-start = ((), (), s32[]{:S(2)}) async-start(), calls=%async_computation.2 | async-start | bytes 10616832 | tf_op jit(solution)/shard_map/all_gather | solution.py:1079
  766.6 107.3 %all-gather.11.cloned.1.call-start = ((), (), s32[]{:S(2)}) async-start(), calls=%async_computation.3 | async-start | bytes 10616832 | tf_op jit(solution)/shard_map/all_gather | solution.py:1079
Sparse Core Ops, SparseCore 0:
  563.2 53.0 all-gather.4
  618.1 52.9 all-gather.6
  766.7 52.4 all-gather.8
  820.9 52.9 all-gather.10
